TPU v7x, 128 devices: a whole 4x4x4 slice. The times are simulated.
128 devices in a mesh: gy: 2 (over core), gx: 64 (over z, y, x).
Axes of the slice: x: 4, y: 4, z: 4, core: 2. Of those that a mesh axis runs over, the one named last changes fastest.
Arguments:
- basis_vectors: float32 [36, 256, 128, 256], P(None, 'gx', 'gy'), may hold values from -30 to 30, as said below
- reaction: float32 [256, 128, 256], P('gx', 'gy'), may hold values from 0.5 to 3
Outputs:
- new_vectors: float32 [4, 256, 128, 256], P(None, 'gx', 'gy')
- hessenberg: float32 [40, 4], replicated
Inputs may be any that keep to these rules, and one draw needn't show every extreme that they name: `basis_vectors`: under the inner product the basis vectors are nearly orthonormal.
All inputs are finite; a program needn't handle non-finite values.
Results may differ from a plain program's by a relative error of at most 0.0003.
Values sent between devices are 32-bit elements; how exact they have to be, the bound alone decides.
No kernel may reach another device: no remote copies, remote signals or barrier semaphores. Data moves between devices by JAX's collectives and lax.ppermute only.
A program may use at most 128 MiB of HBM per device.

v0:
```python
import jax
import jax.numpy as jnp
from jax import lax
from jax.sharding import Mesh
from jax.sharding import PartitionSpec as P

STEPS = 4
GX = ("gx_0", "gx_1", "gx_2")


WIND_SPEEDS = (0.9, 0.6, 0.4)
EPSILON = 1e-06


def shifted(block, axis, distance):
    devices = range(lax.axis_size(axis))
    route = [(i - distance, i) for i in devices if i - distance in devices]
    return lax.ppermute(block, axis, route)


def copy_for_each(array, axis):
    copies = jnp.broadcast_to(array, (lax.axis_size(axis), *array.shape))
    return lax.all_to_all(copies, axis, split_axis=0, concat_axis=0, tiled=True)


def over_copies(array, axis):
    everything = copy_for_each(array, axis)
    return jnp.sum(everything, axis=0)


def by_axis(array, axes):
    far, near = axes
    nearer = over_copies(array, near)
    return over_copies(nearer, far)


def in_one(arrays, axis):
    ends = [0]
    for a in arrays:
        ends.append(ends[-1] + a.size)
    running = by_axis(jnp.concatenate([a.ravel() for a in arrays]), axis)
    return tuple((running[b:e].reshape(a.shape) for a, b, e in zip(arrays, ends, ends[1:])))


def stencil(values, x_ext, y_ext, z_ext, reaction):
    summed = -reaction * values
    for position, extended in enumerate((x_ext, y_ext, z_ext)):
        count = values.shape[position]
        higher = lax.slice_in_dim(extended, 3, count + 3, axis=position)
        lower_one = lax.slice_in_dim(extended, 1, count + 1, axis=position)
        lower_two = lax.slice_in_dim(extended, 0, count, axis=position)
        wind_speed = WIND_SPEEDS[position]
        summed = (
            summed
            + higher
            + lower_one
            - 2.0 * values
            - wind_speed * (3.0 * values - 4.0 * lower_one + lower_two) * 0.5
        )
    return summed


def apply_operator(values, reaction):
    rows_x = values.shape[0]
    rows_y = values.shape[1]
    lower_x = shifted(values[rows_x - 2 :], GX, 1)
    upper_x = shifted(values[:1], GX, -1)
    lower_y = shifted(values[:, rows_y - 2 :], "gy", 1)
    upper_y = shifted(values[:, :1], "gy", -1)
    x_ext = jnp.concatenate([lower_x, values, upper_x], axis=0)
    y_ext = jnp.concatenate([lower_y, values, upper_y], axis=1)
    z_ext = jnp.pad(values, ((0, 0), (0, 0), (2, 1)))
    return stencil(values, x_ext, y_ext, z_ext, reaction)


def project(basis_vectors, created, image):
    local = jnp.einsum("kxyz,xyz->k", basis_vectors, image, precision=lax.Precision.HIGHEST)
    extra = [jnp.sum(vector * image)[None] for vector in created]
    return jnp.concatenate([local] + extra)


def combine(basis_vectors, created, weights):
    keep_count = basis_vectors.shape[0]
    summed = jnp.einsum(
        "k,kxyz->xyz", weights[:keep_count], basis_vectors, precision=lax.Precision.HIGHEST
    )
    for index, vector in enumerate(created):
        summed = summed + weights[keep_count + index] * vector
    return summed


def body(basis_vectors, reaction):
    keep_count = basis_vectors.shape[0]
    basis_size = keep_count + STEPS
    cell_count = float(
        basis_vectors.shape[1]
        * basis_vectors.shape[2]
        * basis_vectors.shape[3]
        * lax.axis_size(GX)
        * lax.axis_size("gy")
    )
    created = []
    columns = []
    local_gram = jnp.einsum(
        "axyz,bxyz->ab", basis_vectors, basis_vectors, precision=lax.Precision.HIGHEST
    )
    kept_gram = by_axis(local_gram, ("gy", ("gx_0", "gx_1", "gx_2"))) / cell_count
    gram_matrix = (
        jnp.zeros((basis_size, basis_size), jnp.float32).at[:keep_count, :keep_count].set(kept_gram)
    )
    for section in range(STEPS):
        current = keep_count + section
        vector_now = basis_vectors[keep_count - 1] if section == 0 else created[-1]
        image = apply_operator(vector_now, reaction)
        first_terms = (
            by_axis(project(basis_vectors, created, image), ("gy", ("gx_0", "gx_1", "gx_2")))
            / cell_count
        )
        first_rest = image - combine(basis_vectors, created, first_terms)
        second_terms, rest_square = in_one(
            (project(basis_vectors, created, first_rest), jnp.sum(first_rest * first_rest)),
            ("gy", ("gx_0", "gx_1", "gx_2")),
        )
        second_terms = second_terms / cell_count
        rest_square = rest_square / cell_count
        gram_now = gram_matrix[:current, :current]
        folded = jnp.dot(gram_now, second_terms, precision=lax.Precision.HIGHEST)
        second_rest = first_rest - combine(basis_vectors, created, second_terms)
        squared = (
            rest_square
            - 2.0 * jnp.sum(second_terms * second_terms)
            + jnp.sum(second_terms * folded)
        )
        length_now = jnp.sqrt(squared + EPSILON)
        cross_terms = (second_terms - folded) / length_now
        gram_matrix = gram_matrix.at[:current, current].set(cross_terms)
        gram_matrix = gram_matrix.at[current, :current].set(cross_terms)
        gram_matrix = gram_matrix.at[current, current].set(squared / (length_now * length_now))
        weights = first_terms + second_terms
        columns.append(
            jnp.concatenate(
                [weights, length_now[None], jnp.zeros((basis_size - current - 1,), jnp.float32)]
            )
        )
        created.append(second_rest / length_now)
    return (jnp.stack(created), jnp.stack(columns, axis=1))


def solution(mesh):
    split = Mesh(mesh.devices.reshape(mesh.shape["gy"], 4, 4, 4), ("gy", "gx_0", "gx_1", "gx_2"))
    placed = (P(None, GX, "gy", None), P(GX, "gy", None))
    return jax.shard_map(
        body, mesh=split, in_specs=placed, out_specs=(P(None, GX, "gy", None), P()), check_vma=False
    )
```

profile of v0, /device:TPU:1, one launch (start us, length us, event | category | flops | bytes accessed | tf_op | source)
XLA Modules:
  0.0 552.3 jit_solution(16492750439540442998)
XLA Ops:
  13.6 25.8 %fusion.34 = f32[36,36]{1,0:T(8,128)S(1)} fusion(f32[36,4,64,256]{3,2,1,0:T(8,128)} %param.22), kind=kOutput, calls=%fused_computation.34 | convolution fusion | flops 1019215872 | bytes 9442368 | tf_op jit(solution)/shard_map/axyz,bxyz->ab/dot_general | solution.py:104
  41.9 13.0 %fusion.38 = f32[36]{0:T(128)S(1)} fusion(f32[36,4,64,256]{3,2,1,0:T(8,128)S(1)} %copy-done, f32[4,64,256,1]{2,1,0,3:T(8,128)S(1)} %bitcast.255), kind=kOutput, calls=%fused_computation.40 | convolution fusion | flops 28311552 | bytes 9699472 | tf_op jit(solution)/shard_map/kxyz,xyz->k/dot_general | solution.py:77
  55.5 12.0 %all-to-all-start = ((f32[64,1,36]{2,1,0:T(1,128)}), f32[64,1,36]{2,1,0:T(1,128)S(1)}, u32[]{:S(2)}, u32[]{:S(2)}) async-start(f32[64,1,36]{2,1,0:T(1,128)} %broadcast_in_dim.103), calls=%async_computation | async-start | bytes 65536 | tf_op jit(solution)/shard_map/all_to_all | solution.py:23
  68.1 7.8 %all-to-all-done = f32[64,1,36]{2,1,0:T(1,128)S(1)} async-done(((f32[64,1,36]{2,1,0:T(1,128)}), f32[64,1,36]{2,1,0:T(1,128)S(1)}, u32[]{:S(2)}, u32[]{:S(2)}) %all-to-all-start) | async-done | bytes 9248 | tf_op jit(solution)/shard_map/all_to_all | solution.py:23
  80.7 14.5 %fusion.26 = f32[1,4,64,256]{3,0,2,1:T(1,128)S(1)} fusion(f32[36,4,64,256]{3,2,1,0:T(8,128)} %param.22, f32[36]{0:T(128)S(1)} %reduce_sum.379), kind=kOutput, calls=%fused_computation.26 | convolution fusion | flops 28311588 | bytes 9699472 | tf_op jit(solution)/shard_map/k,kxyz->xyz/dot_general | solution.py:84
  95.9 16.0 %fusion.41 = f32[36]{0:T(128)S(1)} fusion(f32[36,4,64,256]{3,2,1,0:T(8,128)} %param.22, f32[4,64,256,1]{2,1,0,3:T(8,128)S(1)} %get-tuple-element.149), kind=kOutput, calls=%fused_computation.41 | convolution fusion | flops 28311552 | bytes 9699472 | tf_op jit(solution)/shard_map/kxyz,xyz->k/dot_general | solution.py:77
  137.8 14.5 %fusion.22 = f32[1,4,64,256]{3,0,2,1:T(1,128)S(1)} fusion(f32[36,4,64,256]{3,2,1,0:T(8,128)} %param.22, f32[37]{0:T(128)S(1)} %reduce_sum.382), kind=kOutput, calls=%fused_computation.22 | convolution fusion | flops 28311588 | bytes 9699476 | tf_op jit(solution)/shard_map/k,kxyz->xyz/dot_general | solution.py:84
  172.9 16.3 %fusion.44 = f32[36]{0:T(128)S(1)} fusion(f32[36,4,64,256]{3,2,1,0:T(8,128)} %param.22, f32[4,64,256,1]{2,1,0,3:T(8,128)S(1)} %bitcast.258), kind=kOutput, calls=%fused_computation.42 | convolution fusion | flops 28311552 | bytes 9699472 | tf_op jit(solution)/shard_map/kxyz,xyz->k/dot_general | solution.py:77
  190.6 11.9 %all-to-all-start.6 = ((f32[64,1,37]{2,1,0:T(1,128)}), f32[64,1,37]{2,1,0:T(1,128)S(1)}, u32[]{:S(2)}, u32[]{:S(2)}) async-start(f32[64,1,37]{2,1,0:T(1,128)} %broadcast_in_dim.110), calls=%async_computation.6 | async-start | bytes 65536 | tf_op jit(solution)/shard_map/all_to_all | solution.py:23
  202.6 8.2 %all-to-all-done.6 = f32[64,1,37]{2,1,0:T(1,128)S(1)} async-done(((f32[64,1,37]{2,1,0:T(1,128)}), f32[64,1,37]{2,1,0:T(1,128)S(1)}, u32[]{:S(2)}, u32[]{:S(2)}) %all-to-all-start.6) | async-done | bytes 9504 | tf_op jit(solution)/shard_map/all_to_all | solution.py:23
  217.5 14.6 %fusion.18 = f32[1,4,64,256]{3,0,2,1:T(1,128)S(1)} fusion(f32[36,4,64,256]{3,2,1,0:T(8,128)} %param.22, f32[37]{0:T(128)S(1)} %broadcast_multiply_fusion.3), kind=kOutput, calls=%fused_computation.18 | convolution fusion | flops 28311552 | bytes 9699476 | tf_op jit(solution)/shard_map/k,kxyz->xyz/dot_general | solution.py:84
  234.1 16.0 %fusion.47 = f32[36]{0:T(128)S(1)} fusion(f32[36,4,64,256]{3,2,1,0:T(8,128)} %param.22, f32[4,64,256,1]{2,1,0,3:T(8,128)S(1)} %bitcast.256), kind=kOutput, calls=%fused_computation.43 | convolution fusion | flops 28311552 | bytes 9699472 | tf_op jit(solution)/shard_map/kxyz,xyz->k/dot_general | solution.py:77
  273.8 14.7 %fusion.14 = f32[1,4,64,256]{3,0,2,1:T(1,128)S(1)} fusion(f32[36,4,64,256]{3,2,1,0:T(8,128)} %param.22, f32[37]{0:T(128)S(1)} %get-tuple-element.172), kind=kOutput, calls=%fused_computation.14 | convolution fusion | flops 28311552 | bytes 9699476 | tf_op jit(solution)/shard_map/k,kxyz->xyz/dot_general | solution.py:84
  300.2 16.3 %fusion.50 = f32[36]{0:T(128)S(1)} fusion(f32[36,4,64,256]{3,2,1,0:T(8,128)} %param.22, f32[4,64,256,1]{2,1,0,3:T(8,128)S(1)} %bitcast.261), kind=kOutput, calls=%fused_computation.44 | convolution fusion | flops 28311552 | bytes 9699472 | tf_op jit(solution)/shard_map/kxyz,xyz->k/dot_general | solution.py:77
  318.5 10.9 %all-to-all-start.10 = ((f32[64,1,38]{2,1,0:T(1,128)}), f32[64,1,38]{2,1,0:T(1,128)S(1)}, u32[]{:S(2)}, u32[]{:S(2)}) async-start(f32[64,1,38]{2,1,0:T(1,128)} %broadcast_in_dim.117), calls=%async_computation.10 | async-start | bytes 65536 | tf_op jit(solution)/shard_map/all_to_all | solution.py:23
  330.1 7.6 %all-to-all-done.10 = f32[64,1,38]{2,1,0:T(1,128)S(1)} async-done(((f32[64,1,38]{2,1,0:T(1,128)}), f32[64,1,38]{2,1,0:T(1,128)S(1)}, u32[]{:S(2)}, u32[]{:S(2)}) %all-to-all-start.10) | async-done | bytes 9760 | tf_op jit(solution)/shard_map/all_to_all | solution.py:23
  344.4 14.6 %fusion.10 = f32[1,4,64,256]{3,0,2,1:T(1,128)S(1)} fusion(f32[36,4,64,256]{3,2,1,0:T(8,128)} %param.22, f32[38]{0:T(128)S(1)} %broadcast_multiply_fusion.2), kind=kOutput, calls=%fused_computation.10 | convolution fusion | flops 28311552 | bytes 9699480 | tf_op jit(solution)/shard_map/k,kxyz->xyz/dot_general | solution.py:84
  361.8 16.0 %fusion.53 = f32[36]{0:T(128)S(1)} fusion(f32[36,4,64,256]{3,2,1,0:T(8,128)} %param.22, f32[4,64,256,1]{2,1,0,3:T(8,128)S(1)} %bitcast.260), kind=kOutput, calls=%fused_computation.45 | convolution fusion | flops 28311552 | bytes 9699472 | tf_op jit(solution)/shard_map/kxyz,xyz->k/dot_general | solution.py:77
  402.1 14.7 %fusion.6 = f32[1,4,64,256]{3,0,2,1:T(1,128)S(1)} fusion(f32[36,4,64,256]{3,2,1,0:T(8,128)} %param.22, f32[38]{0:T(128)S(1)} %get-tuple-element.163), kind=kOutput, calls=%fused_computation.6 | convolution fusion | flops 28311552 | bytes 9699480 | tf_op jit(solution)/shard_map/k,kxyz->xyz/dot_general | solution.py:84
  428.6 16.3 %fusion.56 = f32[36]{0:T(128)S(1)} fusion(f32[36,4,64,256]{3,2,1,0:T(8,128)} %param.22, f32[4,64,256,1]{2,1,0,3:T(8,128)S(1)} %bitcast.257), kind=kOutput, calls=%fused_computation.46 | convolution fusion | flops 28311552 | bytes 9699472 | tf_op jit(solution)/shard_map/kxyz,xyz->k/dot_general | solution.py:77
  447.5 10.8 %all-to-all-start.14 = ((f32[64,1,39]{2,1,0:T(1,128)}), f32[64,1,39]{2,1,0:T(1,128)S(1)}, u32[]{:S(2)}, u32[]{:S(2)}) async-start(f32[64,1,39]{2,1,0:T(1,128)} %broadcast_in_dim.126), calls=%async_computation.14 | async-start | bytes 65536 | tf_op jit(solution)/shard_map/all_to_all | solution.py:23
  473.4 14.6 %fusion.2 = f32[1,4,64,256]{3,0,2,1:T(1,128)S(1)} fusion(f32[36,4,64,256]{3,2,1,0:T(8,128)} %param.22, f32[39]{0:T(128)S(1)} %broadcast_multiply_fusion.1), kind=kOutput, calls=%fused_computation.2 | convolution fusion | flops 28311552 | bytes 9699484 | tf_op jit(solution)/shard_map/k,kxyz->xyz/dot_general | solution.py:84
  491.5 16.0 %fusion.59 = f32[36]{0:T(128)S(1)} fusion(f32[36,4,64,256]{3,2,1,0:T(8,128)} %param.22, f32[4,64,256,1]{2,1,0,3:T(8,128)S(1)} %bitcast.259), kind=kOutput, calls=%fused_computation.47 | convolution fusion | flops 28311552 | bytes 9699472 | tf_op jit(solution)/shard_map/kxyz,xyz->k/dot_general | solution.py:77
  530.1 14.7 %fusion.28 = f32[1,4,64,256]{3,0,2,1:T(1,128)S(1)} fusion(f32[36,4,64,256]{3,2,1,0:T(8,128)} %param.22, f32[39]{0:T(128)S(1)} %get-tuple-element.156), kind=kOutput, calls=%fused_computation.28 | convolution fusion | flops 28311552 | bytes 9699484 | tf_op jit(solution)/shard_map/k,kxyz->xyz/dot_general | solution.py:84
  (196 shorter events, 204.7 us)
Async XLA Ops:
  1.8 39.6 %collective-permute-start.3 = (f32[4,2,256]{2,1,0:T(2,128)S(1)}, f32[4,2,256]{2,1,0:T(2,128)S(1)}, u32[]{:S(2)}, u32[]{:S(2)}) collective-permute-start(f32[4,2,256]{2,1,0:T(2,128)S(1)} %slice.566), channel_id=1, source_target_pairs={{0,64},{1,65},{2,66},{3,67},{4,68},{5,69},{6,70},{7,71},{8,72},{9,... | collective-permute-start | bytes 24584 | tf_op jit(solution)/shard_map/ppermute | solution.py:18
  3.4 38.0 %collective-permute-start.2 = (f32[4,1,256]{2,1,0:T(1,128)S(1)}, f32[4,1,256]{2,1,0:T(1,128)S(1)}, u32[]{:S(2)}, u32[]{:S(2)}) collective-permute-start(f32[4,1,256]{2,1,0:T(1,128)S(1)} %slice.565), channel_id=1, source_target_pairs={{64,0},{65,1},{66,2},{67,3},{68,4},{69,5},{70,6},{71,7},{72,8},{73... | collective-permute-start | bytes 12296 | tf_op jit(solution)/shard_map/ppermute | solution.py:18
  7.8 33.7 %collective-permute-start.1 = (f32[2,64,256]{2,1,0:T(8,128)S(1)}, f32[2,64,256]{2,1,0:T(8,128)S(1)}, u32[]{:S(2)}, u32[]{:S(2)}) collective-permute-start(f32[2,64,256]{2,1,0:T(8,128)S(1)} %slice_bitcast_fusion.1), channel_id=1, source_target_pairs={{0,1},{1,2},{2,3},{3,4},{4,5},{5,6},{6,7},{7,8},{8,9},{9,10},{10,1... | collective-permute-start | bytes 393224 | tf_op jit(solution)/shard_map/ppermute | solution.py:18
  12.3 29.2 %collective-permute-start = (f32[1,64,256]{2,1,0:T(8,128)S(1)}, f32[1,64,256]{2,1,0:T(8,128)S(1)}, u32[]{:S(2)}, u32[]{:S(2)}) collective-permute-start(f32[1,64,256]{2,1,0:T(8,128)S(1)} %slice_bitcast_fusion.2), channel_id=1, source_target_pairs={{1,0},{2,1},{3,2},{4,3},{5,4},{6,5},{7,6},{8,7},{9,8},{10,9},{11,1... | collective-permute-start | bytes 196616 | tf_op jit(solution)/shard_map/ppermute | solution.py:18
  55.5 20.4 %all-to-all-start = ((f32[64,1,36]{2,1,0:T(1,128)}), f32[64,1,36]{2,1,0:T(1,128)S(1)}, u32[]{:S(2)}, u32[]{:S(2)}) async-start(f32[64,1,36]{2,1,0:T(1,128)} %broadcast_in_dim.103), calls=%async_computation | async-start | bytes 65536 | tf_op jit(solution)/shard_map/all_to_all | solution.py:23
  113.3 13.1 %all-to-all-start.2 = ((f32[64,1,37]{2,1,0:T(1,128)}), f32[64,1,37]{2,1,0:T(1,128)S(1)}, u32[]{:S(2)}, u32[]{:S(2)}) async-start(f32[64,1,37]{2,1,0:T(1,128)} %broadcast_in_dim.105), calls=%async_computation.2 | async-start | bytes 65536 | tf_op jit(solution)/shard_map/all_to_all | solution.py:23
  131.5 20.7 %all-to-all-start.4 = ((f32[64,1,1296]{2,1,0:T(1,128)}), f32[64,1,1296]{2,1,0:T(1,128)S(1)}, u32[]{:S(2)}, u32[]{:S(2)}) async-start(f32[64,1,1296]{2,1,0:T(1,128)} %reshape.447), calls=%async_computation.4 | async-start | bytes 720896 | tf_op jit(solution)/shard_map/all_to_all | solution.py:23
  162.2 9.8 %collective-permute-start.5 = (f32[2,64,256]{2,1,0:T(8,128)S(1)}, f32[2,64,256]{2,1,0:T(8,128)S(1)}, u32[]{:S(2)}, u32[]{:S(2)}) collective-permute-start(f32[2,64,256]{2,1,0:T(8,128)S(1)} %slice.570), channel_id=1, source_target_pairs={{0,1},{1,2},{2,3},{3,4},{4,5},{5,6},{6,7},{7,8},{8,9},{9,10},{10,1... | collective-permute-start | bytes 393224 | tf_op jit(solution)/shard_map/ppermute | solution.py:18
  165.5 6.4 %collective-permute-start.4 = (f32[1,64,256]{2,1,0:T(8,128)S(1)}, f32[1,64,256]{2,1,0:T(8,128)S(1)}, u32[]{:S(2)}, u32[]{:S(2)}) collective-permute-start(f32[1,64,256]{2,1,0:T(8,128)S(1)} %slice.569), channel_id=1, source_target_pairs={{1,0},{2,1},{3,2},{4,3},{5,4},{6,5},{7,6},{8,7},{9,8},{10,9},{11,1... | collective-permute-start | bytes 196616 | tf_op jit(solution)/shard_map/ppermute | solution.py:18
  166.8 5.1 collective-permute-start.7
  168.1 3.8 collective-permute-start.6
  190.6 20.2 %all-to-all-start.6 = ((f32[64,1,37]{2,1,0:T(1,128)}), f32[64,1,37]{2,1,0:T(1,128)S(1)}, u32[]{:S(2)}, u32[]{:S(2)}) async-start(f32[64,1,37]{2,1,0:T(1,128)} %broadcast_in_dim.110), calls=%async_computation.6 | async-start | bytes 65536 | tf_op jit(solution)/shard_map/all_to_all | solution.py:23
  252.1 13.0 %all-to-all-start.8 = ((f32[64,1,38]{2,1,0:T(1,128)}), f32[64,1,38]{2,1,0:T(1,128)S(1)}, u32[]{:S(2)}, u32[]{:S(2)}) async-start(f32[64,1,38]{2,1,0:T(1,128)} %broadcast_in_dim.113), calls=%async_computation.8 | async-start | bytes 65536 | tf_op jit(solution)/shard_map/all_to_all | solution.py:23
  289.8 9.3 %collective-permute-start.9 = (f32[2,64,256]{2,1,0:T(8,128)S(1)}, f32[2,64,256]{2,1,0:T(8,128)S(1)}, u32[]{:S(2)}, u32[]{:S(2)}) collective-permute-start(f32[2,64,256]{2,1,0:T(8,128)S(1)} %slice.579), channel_id=1, source_target_pairs={{0,1},{1,2},{2,3},{3,4},{4,5},{5,6},{6,7},{7,8},{8,9},{9,10},{10,1... | collective-permute-start | bytes 393224 | tf_op jit(solution)/shard_map/ppermute | solution.py:18
  292.6 6.4 %collective-permute-start.8 = (f32[1,64,256]{2,1,0:T(8,128)S(1)}, f32[1,64,256]{2,1,0:T(8,128)S(1)}, u32[]{:S(2)}, u32[]{:S(2)}) collective-permute-start(f32[1,64,256]{2,1,0:T(8,128)S(1)} %slice.578), channel_id=1, source_target_pairs={{1,0},{2,1},{3,2},{4,3},{5,4},{6,5},{7,6},{8,7},{9,8},{10,9},{11,1... | collective-permute-start | bytes 196616 | tf_op jit(solution)/shard_map/ppermute | solution.py:18
  293.9 5.1 collective-permute-start.11
  295.2 3.8 collective-permute-start.10
  318.5 19.2 %all-to-all-start.10 = ((f32[64,1,38]{2,1,0:T(1,128)}), f32[64,1,38]{2,1,0:T(1,128)S(1)}, u32[]{:S(2)}, u32[]{:S(2)}) async-start(f32[64,1,38]{2,1,0:T(1,128)} %broadcast_in_dim.117), calls=%async_computation.10 | async-start | bytes 65536 | tf_op jit(solution)/shard_map/all_to_all | solution.py:23
  380.4 13.0 %all-to-all-start.12 = ((f32[64,1,39]{2,1,0:T(1,128)}), f32[64,1,39]{2,1,0:T(1,128)S(1)}, u32[]{:S(2)}, u32[]{:S(2)}) async-start(f32[64,1,39]{2,1,0:T(1,128)} %broadcast_in_dim.121), calls=%async_computation.12 | async-start | bytes 65536 | tf_op jit(solution)/shard_map/all_to_all | solution.py:23
  418.8 8.8 %collective-permute-start.13 = (f32[2,64,256]{2,1,0:T(8,128)S(1)}, f32[2,64,256]{2,1,0:T(8,128)S(1)}, u32[]{:S(2)}, u32[]{:S(2)}) collective-permute-start(f32[2,64,256]{2,1,0:T(8,128)S(1)} %slice.588), channel_id=1, source_target_pairs={{0,1},{1,2},{2,3},{3,4},{4,5},{5,6},{6,7},{7,8},{8,9},{9,10},{10,1... | collective-permute-start | bytes 393224 | tf_op jit(solution)/shard_map/ppermute | solution.py:18
  421.1 6.4 %collective-permute-start.12 = (f32[1,64,256]{2,1,0:T(8,128)S(1)}, f32[1,64,256]{2,1,0:T(8,128)S(1)}, u32[]{:S(2)}, u32[]{:S(2)}) collective-permute-start(f32[1,64,256]{2,1,0:T(8,128)S(1)} %slice.587), channel_id=1, source_target_pairs={{1,0},{2,1},{3,2},{4,3},{5,4},{6,5},{7,6},{8,7},{9,8},{10,9},{11,1... | collective-permute-start | bytes 196616 | tf_op jit(solution)/shard_map/ppermute | solution.py:18
  422.4 5.1 collective-permute-start.15
  447.5 19.2 %all-to-all-start.14 = ((f32[64,1,39]{2,1,0:T(1,128)}), f32[64,1,39]{2,1,0:T(1,128)S(1)}, u32[]{:S(2)}, u32[]{:S(2)}) async-start(f32[64,1,39]{2,1,0:T(1,128)} %broadcast_in_dim.126), calls=%async_computation.14 | async-start | bytes 65536 | tf_op jit(solution)/shard_map/all_to_all | solution.py:23
  510.7 13.0 %all-to-all-start.16 = ((f32[64,1,40]{2,1,0:T(1,128)}), f32[64,1,40]{2,1,0:T(1,128)S(1)}, u32[]{:S(2)}, u32[]{:S(2)}) async-start(f32[64,1,40]{2,1,0:T(1,128)} %broadcast_in_dim.131), calls=%async_computation.16 | async-start | bytes 65536 | tf_op jit(solution)/shard_map/all_to_all | solution.py:23
  (6 other events, 204.2 us)
where the time goes:
time: 562 us; the launch traced here: 552 us
  matrix products  272 us (48%)
  starting transfers between devices  104 us (19%)
  waiting for transfers between devices  53.9 us (10%)
  blocking collectives  48.8 us (9%)
  other arithmetic  36.2 us (6%)
  local copies, waits for them, and re-layouts  28 us (5%)
  between operations  9.69 us (2%)
    dot_general x8, matrix products, project(): jnp.einsum('kxyz,xyz->k', basis_vectors, image, precision=lax.Precision.H...  126 us
    dot_general x8, matrix products, combine(): jnp.einsum('k,kxyz->xyz', weights[:keep_count], basis_vectors, precision=...  117 us
    all_to_all x9, starting transfers between devices, copy_for_each(): return lax.all_to_all(copies, axis, split_axis=0, concat_axis=0, tiled=True)  69.3 us
    all_to_all x9, waiting for transfers between devices, copy_for_each(): return lax.all_to_all(copies, axis, split_axis=0, concat_axis=0, tiled=True)  51.6 us
    all_to_all x9, blocking collectives, copy_for_each(): return lax.all_to_all(copies, axis, split_axis=0, concat_axis=0, tiled=True)  48.8 us
    ppermute x16, starting transfers between devices, shifted(): return lax.ppermute(block, axis, route)  34.5 us
    dot_general x1, matrix products, body(): jnp.einsum('axyz,bxyz->ab', basis_vectors, basis_vectors, precision=lax.P...  25.8 us
  transfers between devices with their start and end apart: 25, of which 11 were waited for; matrix products, arithmetic and copies ran while one was open for 11% of the time, Pallas kernels for 0%

commit v1 on v0

v1 whole, which is shorter than its diff:
```python
import functools

import jax
import jax.numpy as jnp
from jax import lax
from jax.experimental import pallas as pl
from jax.experimental.pallas import tpu as pltpu
from jax.sharding import PartitionSpec as P

KEEP = 36
STEPS = 4
BASIS = KEEP + STEPS
WIND_SPEEDS = (0.9, 0.6, 0.4)
EPSILON = 1e-06
F32 = jnp.float32

XS, YS, ZS = 4, 64, 256
ROWS = XS * YS
GROUP = 6
PACK = 12
PACK_LANES = 40
CHUNK = 32

PARAMS = pltpu.CompilerParams(vmem_limit_bytes=16 * 2**20)
VMEM_SPEC = pl.BlockSpec(memory_space=pltpu.VMEM)


def iota(shape, axis):
    return lax.broadcasted_iota(jnp.int32, shape, axis)


def to_column(row):
    pick = iota((BASIS, 128), 0) == iota((BASIS, 128), 1)
    return jnp.sum(jnp.where(pick, row, 0.0), axis=1, keepdims=True)


def to_row(column):
    pick = iota((BASIS, 128), 0) == iota((BASIS, 128), 1)
    return jnp.sum(jnp.where(pick, column, 0.0), axis=0, keepdims=True)


def fold_tiles(block):
    return jnp.sum(block.reshape(-1, 8, ZS), axis=0)


def fold_row(acc):
    return jnp.sum(acc[:, :128] + acc[:, 128:], axis=0, keepdims=True)


def gram_kernel(v_hbm, v_ref, out_ref, sums_ref, matrix_ref, sems):
    groups = KEEP // GROUP
    copies = [
        pltpu.make_async_copy(
            v_hbm.at[pl.ds(g * GROUP, GROUP)], v_ref.at[pl.ds(g * GROUP, GROUP)], sems.at[g]
        )
        for g in range(groups)
    ]
    for c in copies:
        c.start()

    def block(ga, gb):
        pairs = [
            (a, b)
            for a in range(GROUP)
            for b in range(GROUP)
            if ga != gb or a <= b
        ]

        def step(t, accs):
            rows = pl.ds(pl.multiple_of(t * 8, 8), 8)
            accs = list(accs)
            for half in range(2):
                lanes = pl.ds(half * 128, 128)
                left = [v_ref[ga * GROUP + a, rows, lanes] for a in range(GROUP)]
                right = left if ga == gb else [v_ref[gb * GROUP + b, rows, lanes] for b in range(GROUP)]
                for n, (a, b) in enumerate(pairs):
                    accs[n] = accs[n] + left[a] * right[b]
            return tuple(accs)

        zero = jnp.zeros((8, 128), F32)
        accs = lax.fori_loop(0, ROWS // 8, step, tuple(zero for _ in pairs))
        for (a, b), acc in zip(pairs, accs):
            row = jnp.sum(acc, axis=0, keepdims=True)
            i, j = ga * GROUP + a, gb * GROUP + b
            sums_ref[i, pl.ds(j, 1), :] = row
            if i != j:
                sums_ref[j, pl.ds(i, 1), :] = row

    for gb in range(groups):
        copies[gb].wait()
        for ga in range(gb + 1):
            block(ga, gb)
    lane = iota((KEEP, 128), 1)
    matrix = jnp.zeros((KEEP, 128), F32)
    for i in range(KEEP):
        column = jnp.sum(sums_ref[i], axis=1, keepdims=True)
        matrix = jnp.where(lane == i, column, matrix)
    matrix_ref[...] = matrix
    packed = matrix_ref[pl.ds(0, PACK), :]
    for p in range(1, KEEP // PACK):
        packed = packed + pltpu.roll(matrix_ref[pl.ds(p * PACK, PACK), :], p * PACK_LANES, 1)
    out_ref[pl.ds(0, PACK), :] = packed
    out_ref[pl.ds(PACK, 16 - PACK), :] = jnp.zeros((16 - PACK, 128), F32)


def gram_call(basis):
    return pl.pallas_call(
        gram_kernel,
        in_specs=[pl.BlockSpec(memory_space=pl.ANY)],
        out_specs=(VMEM_SPEC, VMEM_SPEC),
        out_shape=(
            pltpu.VMEM((KEEP, ROWS, ZS), F32),
            jax.ShapeDtypeStruct((16, 128), F32),
        ),
        scratch_shapes=[
            pltpu.VMEM((KEEP, KEEP, 128), F32),
            pltpu.VMEM((KEEP, 128), F32),
            pltpu.SemaphoreType.DMA((KEEP // GROUP,)),
        ],
        compiler_params=PARAMS,
        name="gram",
    )(basis)


def dot_all(v_ref, others, x_ref, dots_ref):
    dots_ref[...] = jnp.zeros((BASIS, 128), F32)
    batch = 12

    def run(reads, base):
        def step(c, accs):
            rows = pl.ds(pl.multiple_of(c * CHUNK, CHUNK), CHUNK)
            x = x_ref[rows, :]
            return tuple(acc + fold_tiles(read(rows) * x) for acc, read in zip(accs, reads))

        zero = jnp.zeros((8, ZS), F32)
        accs = lax.fori_loop(0, ROWS // CHUNK, step, tuple(zero for _ in reads))
        for n, acc in enumerate(accs):
            dots_ref[pl.ds(base + n, 1), :] = fold_row(acc)

    for first in range(0, KEEP, batch):
        run([lambda rows, i=i: v_ref[i, rows, :] for i in range(first, first + batch)], first)
    if others:
        run([lambda rows, r=r: r[rows, :] for r in others], KEEP)
    return to_row(jnp.sum(dots_ref[...], axis=1, keepdims=True))


def self_dots_kernel(count, *refs):
    v_ref, *others = refs[: 1 + count]
    out_ref, dots_ref = refs[1 + count :]
    out_ref[...] = dot_all(v_ref, others, others[-1], dots_ref)


def self_dots_call(v, created):
    count = len(created)
    return pl.pallas_call(
        functools.partial(self_dots_kernel, count),
        in_specs=[VMEM_SPEC] * (1 + count),
        out_specs=VMEM_SPEC,
        out_shape=jax.ShapeDtypeStruct((1, 128), F32),
        scratch_shapes=[pltpu.VMEM((BASIS, 128), F32)],
        compiler_params=PARAMS,
        name="self_dots_%d" % count,
    )(v, *created)


def image_kernel(count, *refs):
    core_ref, v_ref, *others = refs[: 2 + count]
    up_ref, down_ref, swap_ref, reaction_ref, extra_ref = refs[2 + count : 7 + count]
    w_ref, out_ref, dots_ref, pad_ref = refs[7 + count :]
    core = core_ref[0]
    upper = core.astype(F32)
    lower = 1.0 - upper
    source = others[-1] if others else v_ref.at[KEEP - 1]
    lane = iota((YS, ZS), 1)
    center = -6.0 - 1.5 * sum(WIND_SPEEDS)
    near = [1.0 + 2.0 * s for s in WIND_SPEEDS]
    far = [-0.5 * s for s in WIND_SPEEDS]

    def plane(x):
        if x < 0:
            return up_ref[pl.ds((x + 2) * YS, YS), :]
        if x >= XS:
            return down_ref[...]
        return source[pl.ds(x * YS, YS), :]

    for x in range(XS):
        mine = plane(x)
        pad_ref[x, pl.ds(8, YS), :] = mine
        edge = swap_ref[pl.ds(2 * x, 2), :]
        pad_ref[x, pl.ds(6, 2), :] = edge * upper
        pad_ref[x, pl.ds(72, 1), :] = edge[0:1] * lower
        image = (center - reaction_ref[pl.ds(x * YS, YS), :]) * mine
        image = image + plane(x + 1) + near[0] * plane(x - 1) + far[0] * plane(x - 2)
        image = (
            image
            + pad_ref[x, pl.ds(9, YS), :]
            + near[1] * pad_ref[x, pl.ds(7, YS), :]
            + far[1] * pad_ref[x, pl.ds(6, YS), :]
        )
        image = (
            image
            + jnp.where(lane < ZS - 1, pltpu.roll(mine, ZS - 1, 1), 0.0)
            + near[2] * jnp.where(lane >= 1, pltpu.roll(mine, 1, 1), 0.0)
            + far[2] * jnp.where(lane >= 2, pltpu.roll(mine, 2, 1), 0.0)
        )
        w_ref[pl.ds(x * YS, YS), :] = image
    row = dot_all(v_ref, others, w_ref, dots_ref)
    if others:
        out_ref[pl.ds(0, 1), :] = row
        out_ref[pl.ds(1, 1), :] = extra_ref[...]
    else:
        out_ref[...] = extra_ref[...]
        out_ref[pl.ds(PACK, 1), :] = row


def image_call(core, v, created, halo, reaction, extra):
    count = len(created)
    payload = 2 if created else 16
    return pl.pallas_call(
        functools.partial(image_kernel, count),
        in_specs=[pl.BlockSpec(memory_space=pltpu.SMEM)] + [VMEM_SPEC] * (6 + count),
        out_specs=(VMEM_SPEC, VMEM_SPEC),
        out_shape=(
            pltpu.VMEM((ROWS, ZS), F32),
            jax.ShapeDtypeStruct((payload, 128), F32),
        ),
        scratch_shapes=[
            pltpu.VMEM((BASIS, 128), F32),
            pltpu.VMEM((XS, YS + 16, ZS), F32),
        ],
        compiler_params=PARAMS,
        name="image_%d" % count,
    )(core, v, *created, *halo, reaction, extra)


STATE_G, STATE_H, STATE_D, STATE_ROWS = 0, BASIS, 2 * BASIS, 2 * BASIS + 8


def summed_rows(recv_ref, count):
    if count >= 8:
        return jnp.sum(recv_ref[...].reshape(-1, count, 128), axis=0)
    total = jnp.sum(recv_ref[...].reshape(-1, 8, 128), axis=0)
    shift = count
    while shift < 8:
        total = total + pltpu.roll(total, 8 - shift, 0)
        shift *= 2
    return total


def combine_kernel(count, cells, *refs):
    core_ref, recv_ref, w_ref, v_ref, *others = refs[: 4 + count]
    pos = 4 + count
    if count:
        state_in = refs[pos]
        pos += 1
    u_ref, up_ref, down_ref, swap_ref, state_ref, square_ref, weight_ref = refs[pos:]
    lane = iota((1, 128), 1)
    lanes = iota((BASIS, 128), 1)
    subs = iota((BASIS, 128), 0)
    scale = 1.0 / cells
    if count == 0:
        total = summed_rows(recv_ref, 16) * scale
        state_ref[...] = jnp.zeros((STATE_ROWS, 128), F32)
        for p in range(KEEP // PACK):
            part = total[:PACK]
            if p:
                part = pltpu.roll(part, 128 - p * PACK_LANES, 1)
            part = jnp.where(iota((PACK, 128), 1) < KEEP, part, 0.0)
            state_ref[pl.ds(STATE_G + p * PACK, PACK), :] = part
        gram = state_ref[pl.ds(STATE_G, BASIS), :]
        hess = jnp.zeros((BASIS, 128), F32)
        inverse_row = jnp.where(lane < KEEP, 1.0, 0.0)
        first_row = total[PACK : PACK + 1]
        inverse = jnp.ones((1, 1), F32)
    else:
        total = summed_rows(recv_ref, 2) * scale
        newest = KEEP + count - 1
        raw_first, raw_gram = total[0:1], total[1:2]
        square = jnp.sum(jnp.where(lane == newest, raw_gram, 0.0), axis=1, keepdims=True)
        norm = jnp.sqrt(square + EPSILON)
        inverse = 1.0 / norm
        inverse_row = jnp.where(lane == newest, inverse, state_in[pl.ds(STATE_D, 1), :])
        gram_row = raw_gram * inverse_row * inverse
        first_row = raw_first * inverse_row * inverse
        gram = state_in[pl.ds(STATE_G, BASIS), :]
        gram = jnp.where(lanes == newest, to_column(gram_row), gram)
        gram = jnp.where(subs == newest, gram_row, gram)
        hess = state_in[pl.ds(STATE_H, BASIS), :]
        hess = jnp.where((subs == newest) & (lanes == count - 1), norm, hess)
    first = to_column(first_row)
    folded = jnp.sum(gram * first_row, axis=1, keepdims=True)
    weights = first + (first - folded)
    hess = jnp.where((lanes == count) & (subs < KEEP + count), weights, hess)
    state_ref[pl.ds(STATE_G, BASIS), :] = gram
    state_ref[pl.ds(STATE_H, BASIS), :] = hess
    state_ref[pl.ds(STATE_D, 8), :] = jnp.broadcast_to(inverse_row, (8, 128))
    weight_ref[...] = jnp.broadcast_to(weights * to_column(inverse_row), (BASIS, ZS))

    def step(c, acc):
        rows = pl.ds(pl.multiple_of(c * CHUNK, CHUNK), CHUNK)
        value = w_ref[rows, :] * inverse
        for i in range(KEEP):
            value = value - weight_ref[pl.ds(i, 1), :] * v_ref[i, rows, :]
        for i, other in enumerate(others):
            value = value - weight_ref[pl.ds(KEEP + i, 1), :] * other[rows, :]
        u_ref[rows, :] = value
        return acc + fold_tiles(value * value)

    acc = lax.fori_loop(0, ROWS // CHUNK, step, jnp.zeros((8, ZS), F32))
    square_ref[...] = fold_row(acc)
    up_ref[...] = u_ref[pl.ds((XS - 2) * YS, 2 * YS), :]
    down_ref[...] = u_ref[pl.ds(0, YS), :]
    upper = core_ref[0] == 1
    for x in range(XS):
        low = u_ref[pl.ds(x * YS, 2), :]
        high = u_ref[pl.ds(x * YS + YS - 2, 2), :]
        swap_ref[pl.ds(2 * x, 2), :] = jnp.where(upper, low, high)


def combine_call(core, recv, w, v, created, state, cells):
    count = len(created)
    states = [state] if created else []
    return pl.pallas_call(
        functools.partial(combine_kernel, count, cells),
        in_specs=[pl.BlockSpec(memory_space=pltpu.SMEM)] + [VMEM_SPEC] * (3 + count + len(states)),
        out_specs=(VMEM_SPEC,) * 6,
        out_shape=(
            pltpu.VMEM((ROWS, ZS), F32),
            jax.ShapeDtypeStruct((2 * YS, ZS), F32),
            jax.ShapeDtypeStruct((YS, ZS), F32),
            jax.ShapeDtypeStruct((2 * XS, ZS), F32),
            jax.ShapeDtypeStruct((STATE_ROWS, 128), F32),
            jax.ShapeDtypeStruct((1, 128), F32),
        ),
        scratch_shapes=[pltpu.VMEM((BASIS, ZS), F32)],
        compiler_params=PARAMS,
        name="combine_%d" % count,
    )(core, recv, w, v, *created, *states)


def finish_kernel(cells, *refs):
    recv_ref, state_ref, *created = refs[: 2 + STEPS]
    new_ref, hess_ref = refs[2 + STEPS :]
    lane = iota((1, 128), 1)
    total = summed_rows(recv_ref, 1)[0:1] * (1.0 / cells)
    norm = jnp.sqrt(jnp.sum(total, axis=1, keepdims=True) + EPSILON)
    lanes = iota((BASIS, 128), 1)
    subs = iota((BASIS, 128), 0)
    hess = state_ref[pl.ds(STATE_H, BASIS), :]
    hess = jnp.where((subs == BASIS - 1) & (lanes == STEPS - 1), norm, hess)
    hess_ref[...] = hess[:, :STEPS]
    inverse_row = state_ref[pl.ds(STATE_D, 1), :]
    for j, u_ref in enumerate(created):
        if j == STEPS - 1:
            inverse = 1.0 / norm
        else:
            inverse = jnp.sum(jnp.where(lane == KEEP + j, inverse_row, 0.0), axis=1, keepdims=True)
        for c in range(ROWS // CHUNK):
            rows = pl.ds(c * CHUNK, CHUNK)
            new_ref[j, rows, :] = u_ref[rows, :] * inverse


def finish_call(recv, state, created, cells):
    return pl.pallas_call(
        functools.partial(finish_kernel, cells),
        in_specs=[VMEM_SPEC] * (2 + STEPS),
        out_specs=(VMEM_SPEC, VMEM_SPEC),
        out_shape=(
            jax.ShapeDtypeStruct((STEPS, ROWS, ZS), F32),
            jax.ShapeDtypeStruct((BASIS, STEPS), F32),
        ),
        compiler_params=PARAMS,
        name="finish",
    )(recv, state, *created)


def exchange(up, down, swap):
    count = lax.axis_size("gx")
    up = lax.ppermute(up, "gx", [(i, i + 1) for i in range(count - 1)])
    down = lax.ppermute(down, "gx", [(i + 1, i) for i in range(count - 1)])
    swap = lax.ppermute(swap, "gy", [(0, 1), (1, 0)])
    return up, down, swap


def from_all(payload):
    axes = ("gy", "gx")
    devices = lax.axis_size(axes)
    copies = jnp.broadcast_to(payload, (devices, *payload.shape))
    got = lax.all_to_all(copies, axes, split_axis=0, concat_axis=0, tiled=True)
    return got.reshape(-1, 128)


def body(basis_vectors, reaction):
    cells = float(ROWS * ZS * lax.axis_size("gx") * lax.axis_size("gy"))
    core_index = lax.axis_index("gy")
    core = core_index.astype(jnp.int32).reshape(1)
    last = basis_vectors[KEEP - 1]
    edge = jnp.where(core_index == 1, last[:, :2], last[:, YS - 2 :])
    halo = exchange(
        last[XS - 2 :].reshape(2 * YS, ZS), last[:1].reshape(YS, ZS), edge.reshape(2 * XS, ZS)
    )
    reaction = reaction.reshape(ROWS, ZS)
    v, extra = gram_call(basis_vectors.reshape(KEEP, ROWS, ZS))
    created = []
    state = None
    for j in range(STEPS):
        if j:
            extra = self_dots_call(v, created)
        w, payload = image_call(core, v, created, halo, reaction, extra)
        recv = from_all(payload)
        u, up, down, swap, state, square = combine_call(core, recv, w, v, created, state, cells)
        created.append(u)
        if j + 1 < STEPS:
            halo = exchange(up, down, swap)
    new, hessenberg = finish_call(from_all(square), state, created, cells)
    return new.reshape(STEPS, XS, YS, ZS), hessenberg


def solution(mesh):
    return jax.shard_map(
        body,
        mesh=mesh,
        in_specs=(P(None, "gx", "gy", None), P("gx", "gy", None)),
        out_specs=(P(None, "gx", "gy", None), P()),
        check_vma=False,
    )
```

time: 562 us -> 188 us (0.33); the launches traced: 552 us -> 187 us
  matrix products: 272 us -> 0 us
  starting transfers between devices: 104 us -> 21.2 us
  blocking collectives: 48.8 us -> 115 us
  waiting for transfers between devices: 53.9 us -> 4.39 us
  Pallas kernels: 0 us -> 38.7 us
  other arithmetic: 36.2 us -> 0.01 us
  local copies, waits for them, and re-layouts: 28 us -> 7.34 us
  between operations: 9.69 us -> 0.8 us
    dot_general x21 -> x0, matrix products: 272 us -> none  [the longest x8 126 us: project(): jnp.einsum('kxyz,xyz->k', basis_vectors, image, precision=lax.Precision.H...]
    all_to_all x9 -> x0, starting transfers between devices: 69.3 us -> none  [copy_for_each(): return lax.all_to_all(copies, axis, split_axis=0, concat_axis=0, tiled=True)]
    all_to_all x9 -> x5, blocking collectives: 48.8 us -> 115 us  [from_all(): got = lax.all_to_all(copies, axes, split_axis=0, concat_axis=0, tiled=True)]
    all_to_all x9 -> x0, waiting for transfers between devices: 51.6 us -> none  [copy_for_each(): return lax.all_to_all(copies, axis, split_axis=0, concat_axis=0, tiled=True)]
    pallas_call x0 -> x13, Pallas kernels: none -> 38.7 us  [the longest x1 20.3 us: gram_call(): pl.pallas_call(gram_kernel, in_specs=[pl.BlockSpec(memory_space=pl.ANY)],...]
    ppermute x16 -> x12, starting transfers between devices: 34.5 us -> 21.2 us  [the longest x4 11.1 us: exchange(): up = lax.ppermute(up, 'gx', [(i, i + 1) for i in range(count - 1)])]
    another operation x16 -> x0, other arithmetic: 11.7 us -> none
    reduce_sum x24 -> x0, other arithmetic: 10.4 us -> none  [the longest x5 6.66 us: project(): extra = [jnp.sum(vector * image)[None] for vector in created]]
  transfers between devices with their start and end apart: 25 -> 12, of which waited for: 11 -> 3; matrix products, arithmetic and copies ran while one was open for 11% -> 1% of each run, Pallas kernels for 0% -> 13%
where the time goes in v1:
time: 188 us; the launch traced here: 187 us
  blocking collectives  115 us (61%)
  Pallas kernels  38.7 us (21%)
  starting transfers between devices  21.2 us (11%)
  local copies, waits for them, and re-layouts  7.34 us (4%)
  waiting for transfers between devices  4.39 us (2%)
    all_to_all x5, blocking collectives, from_all(): got = lax.all_to_all(copies, axes, split_axis=0, concat_axis=0, tiled=True)  115 us
    pallas_call x1, Pallas kernels, gram_call(): pl.pallas_call(gram_kernel, in_specs=[pl.BlockSpec(memory_space=pl.ANY)],...  20.3 us
    ppermute x4, starting transfers between devices, exchange(): up = lax.ppermute(up, 'gx', [(i, i + 1) for i in range(count - 1)])  11.1 us
    pallas_call x4, Pallas kernels, combine_call(): pl.pallas_call(functools.partial(combine_kernel, count, cells), in_specs=...  8.34 us
    pallas_call x4, Pallas kernels, image_call(): pl.pallas_call(functools.partial(image_kernel, count), in_specs=[pl.Block...  5.59 us
    ppermute x4, starting transfers between devices, exchange(): down = lax.ppermute(down, 'gx', [(i + 1, i) for i in range(count - 1)])  5.16 us
    ppermute x4, starting transfers between devices, exchange(): swap = lax.ppermute(swap, 'gy', [(0, 1), (1, 0)])  4.89 us
    ppermute x4, waiting for transfers between devices, exchange(): down = lax.ppermute(down, 'gx', [(i + 1, i) for i in range(count - 1)])  4.37 us
  transfers between devices with their start and end apart: 12, of which 3 were waited for; matrix products, arithmetic and copies ran while one was open for 1% of the time, Pallas kernels for 13%

profile of v1, /device:TPU:1, one launch (start us, length us, event | category | flops | bytes accessed | tf_op | source)
XLA Modules:
  0.0 187.4 jit_solution(1660349521896841621)
XLA Ops:
  3.7 4.6 %collective-permute-start = (f32[128,256]{1,0:T(8,128)S(1)}, f32[128,256]{1,0:T(8,128)S(1)}, u32[]{:S(2)}, u32[]{:S(2)}) collective-permute-start(f32[128,256]{1,0:T(8,128)S(1)} %bitcast.26), channel_id=1, source_target_pairs={{0,1},{1,2},{2,3},{3,4},{4,5},{5,6},{6,7},{7,8},{8,9},{9,10},{10,1... | collective-permute-start | bytes 393224 | tf_op jit(solution)/shard_map/ppermute | solution.py:379
  9.3 1.4 collective-permute-start.2
  10.8 3.7 %copy-done = f32[36,4,64,256]{3,2,1,0:T(8,128)S(1)} copy-done((f32[36,4,64,256]{3,2,1,0:T(8,128)S(1)}, f32[36,4,64,256]{3,2,1,0:T(8,128)}, u32[]{:S(2)}) %copy-start) | copy-done | bytes 9437208
  14.5 20.3 %gram.1 = (f32[36,256,256]{2,1,0:T(8,128)S(1)}, f32[16,128]{1,0:T(8,128)S(1)}) custom-call(f32[36,256,256]{2,1,0:T(8,128)S(1)} %bitcast.15), custom_call_target="tpu_custom_call" | custom-call | tf_op jit(solution)/shard_map/gram/pallas_call | solution.py:107
  34.8 1.3 image_0.1
  36.2 32.1 %all_to_all.25 = f32[128,16,128]{2,1,0:T(8,128)S(1)} all-to-all(f32[128,16,128]{2,1,0:T(8,128)S(1)} %broadcast_in_dim.15), channel_id=1, replica_groups=mesh['gy'=2,'gx'=64] {'gy','gx'}, dimensions={0} | all-to-all | bytes 2097152 | tf_op jit(solution)/shard_map/all_to_all | solution.py:389
  68.4 2.0 %combine_0.1 = (f32[256,256]{1,0:T(8,128)S(1)}, f32[128,256]{1,0:T(8,128)S(1)}, f32[64,256]{1,0:T(8,128)S(1)}, f32[8,256]{1,0:T(8,128)S(1)}, f32[88,128]{1,0:T(8,128)S(1)}, /*index=5*/f32[1,128]{1,0:T(1,128)}) custom-call(s32[1]{0:T(128)} %bitcast.refs_0_, f32[2048,128]{1,0:T(8,128)S(1)} %bitcast.20, f32[256,256]{1,0:T(8,128)S(1)} %get-tuple-element.35.refs_2_, ...), custom_call_target="tpu_custom_call" | custom-call | tf_op jit(solution)/shard_map/combine_0/pallas_call | solution.py:323
  70.3 2.2 %collective-permute-start.3 = (f32[128,256]{1,0:T(8,128)S(1)}, f32[128,256]{1,0:T(8,128)S(1)}, u32[]{:S(2)}, u32[]{:S(2)}) collective-permute-start(f32[128,256]{1,0:T(8,128)S(1)} %get-tuple-element.37), channel_id=1, source_target_pairs={{0,1},{1,2},{2,3},{3,4},{4,5},{5,6},{6,7},{7,8},{8,9},{9,10},{10,1... | collective-permute-start | bytes 393224 | tf_op jit(solution)/shard_map/ppermute | solution.py:379
  72.5 1.3 collective-permute-start.4
  73.8 1.6 collective-permute-start.5
  77.5 1.4 image_1.1
  79.0 23.8 %all_to_all.26 = f32[128,2,128]{2,1,0:T(2,128)S(1)} all-to-all(f32[128,2,128]{2,1,0:T(2,128)S(1)} %broadcast_in_dim.16), channel_id=1, replica_groups=mesh['gy'=2,'gx'=64] {'gy','gx'}, dimensions={0} | all-to-all | bytes 262144 | tf_op jit(solution)/shard_map/all_to_all | solution.py:389
  102.8 2.0 %combine_1.1 = (f32[256,256]{1,0:T(8,128)S(1)}, f32[128,256]{1,0:T(8,128)S(1)}, f32[64,256]{1,0:T(8,128)S(1)}, f32[8,256]{1,0:T(8,128)S(1)}, f32[88,128]{1,0:T(8,128)S(1)}, /*index=5*/f32[1,128]{1,0:T(1,128)}) custom-call(s32[1]{0:T(128)} %bitcast.refs_0_, f32[256,128]{1,0:T(8,128)S(1)} %bitcast.22, f32[256,256]{1,0:T(8,128)S(1)} %get-tuple-element.41.refs_2_, ...), custom_call_target="tpu_custom_call" | custom-call | tf_op jit(solution)/shard_map/combine_1/pallas_call | solution.py:323
  104.8 2.2 %collective-permute-start.6 = (f32[128,256]{1,0:T(8,128)S(1)}, f32[128,256]{1,0:T(8,128)S(1)}, u32[]{:S(2)}, u32[]{:S(2)}) collective-permute-start(f32[128,256]{1,0:T(8,128)S(1)} %get-tuple-element.44), channel_id=1, source_target_pairs={{0,1},{1,2},{2,3},{3,4},{4,5},{5,6},{6,7},{7,8},{8,9},{9,10},{10,1... | collective-permute-start | bytes 393224 | tf_op jit(solution)/shard_map/ppermute | solution.py:379
  110.3 1.7 collective-permute-done.7.refs_5_
  112.0 1.4 image_2.1
  113.5 22.9 %all_to_all.27 = f32[128,2,128]{2,1,0:T(2,128)S(1)} all-to-all(f32[128,2,128]{2,1,0:T(2,128)S(1)} %broadcast_in_dim.17), channel_id=1, replica_groups=mesh['gy'=2,'gx'=64] {'gy','gx'}, dimensions={0} | all-to-all | bytes 262144 | tf_op jit(solution)/shard_map/all_to_all | solution.py:389
  136.4 2.0 %combine_2.1 = (f32[256,256]{1,0:T(8,128)S(1)}, f32[128,256]{1,0:T(8,128)S(1)}, f32[64,256]{1,0:T(8,128)S(1)}, f32[8,256]{1,0:T(8,128)S(1)}, f32[88,128]{1,0:T(8,128)S(1)}, /*index=5*/f32[1,128]{1,0:T(1,128)}) custom-call(s32[1]{0:T(128)} %bitcast.refs_0_, f32[256,128]{1,0:T(8,128)S(1)} %bitcast.23, f32[256,256]{1,0:T(8,128)S(1)} %get-tuple-element.48.refs_2_, ...), custom_call_target="tpu_custom_call" | custom-call | tf_op jit(solution)/shard_map/combine_2/pallas_call | solution.py:323
  138.5 2.2 %collective-permute-start.9 = (f32[128,256]{1,0:T(8,128)S(1)}, f32[128,256]{1,0:T(8,128)S(1)}, u32[]{:S(2)}, u32[]{:S(2)}) collective-permute-start(f32[128,256]{1,0:T(8,128)S(1)} %get-tuple-element.51), channel_id=1, source_target_pairs={{0,1},{1,2},{2,3},{3,4},{4,5},{5,6},{6,7},{7,8},{8,9},{9,10},{10,1... | collective-permute-start | bytes 393224 | tf_op jit(solution)/shard_map/ppermute | solution.py:379
  144.0 1.6 collective-permute-done.10.refs_6_
  145.7 1.4 image_3.1
  147.1 22.9 %all_to_all.28 = f32[128,2,128]{2,1,0:T(2,128)S(1)} all-to-all(f32[128,2,128]{2,1,0:T(2,128)S(1)} %broadcast_in_dim.18), channel_id=1, replica_groups=mesh['gy'=2,'gx'=64] {'gy','gx'}, dimensions={0} | all-to-all | bytes 262144 | tf_op jit(solution)/shard_map/all_to_all | solution.py:389
  170.1 2.3 %combine_3.1 = (f32[256,256]{1,0:T(8,128)S(1)}, f32[128,256]{1,0:T(8,128)}, f32[64,256]{1,0:T(8,128)}, f32[8,256]{1,0:T(8,128)}, f32[88,128]{1,0:T(8,128)S(1)}, /*index=5*/f32[1,128]{1,0:T(1,128)S(1)}) custom-call(s32[1]{0:T(128)} %bitcast.refs_0_, f32[256,128]{1,0:T(8,128)S(1)} %bitcast.21, f32[256,256]{1,0:T(8,128)S(1)} %get-tuple-element.55.refs_2_, ...), custom_call_target="tpu_custom_call" | custom-call | tf_op jit(solution)/shard_map/combine_3/pallas_call | solution.py:323
  172.4 13.2 %all_to_all.29 = f32[128,1,128]{2,1,0:T(1,128)S(1)} all-to-all(f32[128,1,128]{2,1,0:T(1,128)S(1)} %broadcast_in_dim.19), channel_id=1, replica_groups=mesh['gy'=2,'gx'=64] {'gy','gx'}, dimensions={0} | all-to-all | bytes 131072 | tf_op jit(solution)/shard_map/all_to_all | solution.py:389
  (33 shorter events, 14.9 us)
Async XLA Ops:
  0.6 34.2 %copy-start.1 = (f32[4,64,256]{2,1,0:T(8,128)S(1)}, f32[4,64,256]{2,1,0:T(8,128)}, u32[]{:S(2)}) copy-start(f32[4,64,256]{2,1,0:T(8,128)} %param.3) | copy-start | bytes 786436
  1.5 33.3 %collective-permute-start.1 = (f32[64,256]{1,0:T(8,128)S(1)}, f32[64,256]{1,0:T(8,128)S(1)}, u32[]{:S(2)}, u32[]{:S(2)}) collective-permute-start(f32[64,256]{1,0:T(8,128)S(1)} %slice_bitcast_fusion.1), channel_id=1, source_target_pairs={{1,0},{2,1},{3,2},{4,3},{5,4},{6,5},{7,6},{8,7},{9,8},{10,9},{11,1... | collective-permute-start | bytes 196616 | tf_op jit(solution)/shard_map/ppermute | solution.py:380
  3.7 31.1 %collective-permute-start = (f32[128,256]{1,0:T(8,128)S(1)}, f32[128,256]{1,0:T(8,128)S(1)}, u32[]{:S(2)}, u32[]{:S(2)}) collective-permute-start(f32[128,256]{1,0:T(8,128)S(1)} %bitcast.26), channel_id=1, source_target_pairs={{0,1},{1,2},{2,3},{3,4},{4,5},{5,6},{6,7},{7,8},{8,9},{9,10},{10,1... | collective-permute-start | bytes 393224 | tf_op jit(solution)/shard_map/ppermute | solution.py:379
  9.3 25.4 %collective-permute-start.2 = (f32[8,256]{1,0:T(8,128)S(1)}, f32[8,256]{1,0:T(8,128)S(1)}, u32[]{:S(2)}, u32[]{:S(2)}) collective-permute-start(f32[8,256]{1,0:T(8,128)S(1)} %reshape.49), channel_id=1, source_target_pairs={{0,64},{64,0},{1,65},{65,1},{2,66},{66,2},{3,67},{67,3},{4,68},{68... | collective-permute-start | bytes 24584 | tf_op jit(solution)/shard_map/ppermute | solution.py:381
  10.8 3.7 %copy-start = (f32[36,4,64,256]{3,2,1,0:T(8,128)S(1)}, f32[36,4,64,256]{3,2,1,0:T(8,128)}, u32[]{:S(2)}) copy-start(f32[36,4,64,256]{3,2,1,0:T(8,128)} %param.2) | copy-start | bytes 28311556
  70.3 7.2 %collective-permute-start.3 = (f32[128,256]{1,0:T(8,128)S(1)}, f32[128,256]{1,0:T(8,128)S(1)}, u32[]{:S(2)}, u32[]{:S(2)}) collective-permute-start(f32[128,256]{1,0:T(8,128)S(1)} %get-tuple-element.37), channel_id=1, source_target_pairs={{0,1},{1,2},{2,3},{3,4},{4,5},{5,6},{6,7},{7,8},{8,9},{9,10},{10,1... | collective-permute-start | bytes 393224 | tf_op jit(solution)/shard_map/ppermute | solution.py:379
  72.5 5.0 %collective-permute-start.4 = (f32[64,256]{1,0:T(8,128)S(1)}, f32[64,256]{1,0:T(8,128)S(1)}, u32[]{:S(2)}, u32[]{:S(2)}) collective-permute-start(f32[64,256]{1,0:T(8,128)S(1)} %get-tuple-element.38), channel_id=1, source_target_pairs={{1,0},{2,1},{3,2},{4,3},{5,4},{6,5},{7,6},{8,7},{9,8},{10,9},{11,1... | collective-permute-start | bytes 196616 | tf_op jit(solution)/shard_map/ppermute | solution.py:380
  73.8 2.7 %collective-permute-start.5 = (f32[8,256]{1,0:T(8,128)S(1)}, f32[8,256]{1,0:T(8,128)S(1)}, u32[]{:S(2)}, u32[]{:S(2)}) collective-permute-start(f32[8,256]{1,0:T(8,128)S(1)} %get-tuple-element.39), channel_id=1, source_target_pairs={{0,64},{64,0},{1,65},{65,1},{2,66},{66,2},{3,67},{67,3},{4,68},{68... | collective-permute-start | bytes 24584 | tf_op jit(solution)/shard_map/ppermute | solution.py:381
  104.8 7.2 %collective-permute-start.6 = (f32[128,256]{1,0:T(8,128)S(1)}, f32[128,256]{1,0:T(8,128)S(1)}, u32[]{:S(2)}, u32[]{:S(2)}) collective-permute-start(f32[128,256]{1,0:T(8,128)S(1)} %get-tuple-element.44), channel_id=1, source_target_pairs={{0,1},{1,2},{2,3},{3,4},{4,5},{5,6},{6,7},{7,8},{8,9},{9,10},{10,1... | collective-permute-start | bytes 393224 | tf_op jit(solution)/shard_map/ppermute | solution.py:379
  107.0 5.0 %collective-permute-start.7 = (f32[64,256]{1,0:T(8,128)S(1)}, f32[64,256]{1,0:T(8,128)S(1)}, u32[]{:S(2)}, u32[]{:S(2)}) collective-permute-start(f32[64,256]{1,0:T(8,128)S(1)} %get-tuple-element.45), channel_id=1, source_target_pairs={{1,0},{2,1},{3,2},{4,3},{5,4},{6,5},{7,6},{8,7},{9,8},{10,9},{11,1... | collective-permute-start | bytes 196616 | tf_op jit(solution)/shard_map/ppermute | solution.py:380
  108.3 2.0 %collective-permute-start.8 = (f32[8,256]{1,0:T(8,128)S(1)}, f32[8,256]{1,0:T(8,128)S(1)}, u32[]{:S(2)}, u32[]{:S(2)}) collective-permute-start(f32[8,256]{1,0:T(8,128)S(1)} %get-tuple-element.46), channel_id=1, source_target_pairs={{0,64},{64,0},{1,65},{65,1},{2,66},{66,2},{3,67},{67,3},{4,68},{68... | collective-permute-start | bytes 24584 | tf_op jit(solution)/shard_map/ppermute | solution.py:381
  138.5 7.2 %collective-permute-start.9 = (f32[128,256]{1,0:T(8,128)S(1)}, f32[128,256]{1,0:T(8,128)S(1)}, u32[]{:S(2)}, u32[]{:S(2)}) collective-permute-start(f32[128,256]{1,0:T(8,128)S(1)} %get-tuple-element.51), channel_id=1, source_target_pairs={{0,1},{1,2},{2,3},{3,4},{4,5},{5,6},{6,7},{7,8},{8,9},{9,10},{10,1... | collective-permute-start | bytes 393224 | tf_op jit(solution)/shard_map/ppermute | solution.py:379
  140.6 5.0 %collective-permute-start.10 = (f32[64,256]{1,0:T(8,128)S(1)}, f32[64,256]{1,0:T(8,128)S(1)}, u32[]{:S(2)}, u32[]{:S(2)}) collective-permute-start(f32[64,256]{1,0:T(8,128)S(1)} %get-tuple-element.52), channel_id=1, source_target_pairs={{1,0},{2,1},{3,2},{4,3},{5,4},{6,5},{7,6},{8,7},{9,8},{10,9},{11,1... | collective-permute-start | bytes 196616 | tf_op jit(solution)/shard_map/ppermute | solution.py:380
  141.9 2.1 %collective-permute-start.11 = (f32[8,256]{1,0:T(8,128)S(1)}, f32[8,256]{1,0:T(8,128)S(1)}, u32[]{:S(2)}, u32[]{:S(2)}) collective-permute-start(f32[8,256]{1,0:T(8,128)S(1)} %get-tuple-element.53), channel_id=1, source_target_pairs={{0,64},{64,0},{1,65},{65,1},{2,66},{66,2},{3,67},{67,3},{4,68},{68... | collective-permute-start | bytes 24584 | tf_op jit(solution)/shard_map/ppermute | solution.py:381

commit v2 on v1

v2 whole, which is shorter than its diff:
```python
import functools

import jax
import jax.numpy as jnp
from jax import lax
from jax.experimental import pallas as pl
from jax.experimental.pallas import tpu as pltpu
from jax.sharding import PartitionSpec as P

KEEP = 36
STEPS = 4
BASIS = KEEP + STEPS
WIND_SPEEDS = (0.9, 0.6, 0.4)
EPSILON = 1e-06
F32 = jnp.float32

XS, YS, ZS = 4, 64, 256
ROWS = XS * YS
GROUP = 4
GRAM_ROWS = 32
HALF = KEEP // 2
PACK = 6
PACK_LANES = 40
CHUNK = 32
SOUND_SHARE = 0.05

PARAMS = pltpu.CompilerParams(vmem_limit_bytes=16 * 2**20)
SMEM_SPEC = pl.BlockSpec(memory_space=pltpu.SMEM)
VMEM_SPEC = pl.BlockSpec(memory_space=pltpu.VMEM)


def iota(shape, axis):
    return lax.broadcasted_iota(jnp.int32, shape, axis)


def to_column(row):
    pick = iota((BASIS, 128), 0) == iota((BASIS, 128), 1)
    return jnp.sum(jnp.where(pick, row, 0.0), axis=1, keepdims=True)


def to_row(column):
    pick = iota((BASIS, 128), 0) == iota((BASIS, 128), 1)
    return jnp.sum(jnp.where(pick, column, 0.0), axis=0, keepdims=True)


def fold_tiles(block):
    return jnp.sum(block.reshape(-1, 8, ZS), axis=0)


def fold_row(acc):
    return jnp.sum(acc[:, :128] + acc[:, 128:], axis=0, keepdims=True)


def gram_kernel(v_hbm, v_ref, out_ref, sums_ref, matrix_ref, sems):
    groups = KEEP // GROUP
    copies = [
        pltpu.make_async_copy(
            v_hbm.at[pl.ds(g * GROUP, GROUP)], v_ref.at[pl.ds(g * GROUP, GROUP)], sems.at[g]
        )
        for g in range(groups)
    ]
    for c in copies:
        c.start()

    def block(ga, gb):
        pairs = [(a, b) for a in range(GROUP) for b in range(GROUP) if ga != gb or a <= b]

        def step(t, accs):
            accs = list(accs)
            for part in range(GRAM_ROWS // 8):
                rows = pl.ds(pl.multiple_of(t * GRAM_ROWS, GRAM_ROWS) + 8 * part, 8)
                for half in range(2):
                    lanes = pl.ds(half * 128, 128)
                    left = [v_ref[ga * GROUP + a, rows, lanes] for a in range(GROUP)]
                    right = left
                    if ga != gb:
                        right = [v_ref[gb * GROUP + b, rows, lanes] for b in range(GROUP)]
                    for n, (a, b) in enumerate(pairs):
                        accs[n] = accs[n] + left[a] * right[b]
            return tuple(accs)

        zero = jnp.zeros((8, 128), F32)
        accs = lax.fori_loop(0, ROWS // GRAM_ROWS, step, tuple(zero for _ in pairs))
        for (a, b), acc in zip(pairs, accs):
            row = jnp.sum(acc, axis=0, keepdims=True)
            i, j = ga * GROUP + a, gb * GROUP + b
            sums_ref[i, pl.ds(j, 1), :] = row
            if i != j:
                sums_ref[j, pl.ds(i, 1), :] = row

    for gb in range(groups):
        copies[gb].wait()
        for ga in range(gb + 1):
            block(ga, gb)
    lane = iota((KEEP, 128), 1)
    matrix = jnp.zeros((KEEP, 128), F32)
    for i in range(KEEP):
        column = jnp.sum(sums_ref[i], axis=1, keepdims=True)
        matrix = jnp.where(lane == i, column, matrix)
    matrix_ref[pl.ds(0, KEEP), :] = matrix
    top = matrix_ref[pl.ds(0, HALF), :]
    bottom = pltpu.roll(matrix_ref[pl.ds(HALF, HALF), :], 128 - HALF, 1)
    lane = iota((HALF, 128), 1)
    sub = iota((HALF, 128), 0)
    diagonal = jnp.sum(jnp.where(lane == sub, top, 0.0), axis=1, keepdims=True)
    packed = jnp.where((lane > sub) | (lane >= HALF), top, bottom)
    packed = jnp.where(lane < KEEP, packed, jnp.where(lane == KEEP, diagonal, 0.0))
    matrix_ref[pl.ds(0, HALF), :] = packed
    packed = matrix_ref[pl.ds(0, PACK), :]
    for p in range(1, HALF // PACK):
        packed = packed + pltpu.roll(matrix_ref[pl.ds(p * PACK, PACK), :], p * PACK_LANES, 1)
    for r in range(PACK):
        out_ref[:, pl.ds(r * 128, 128)] = packed[r : r + 1]


def gram_call(basis):
    return pl.pallas_call(
        gram_kernel,
        in_specs=[pl.BlockSpec(memory_space=pltpu.HBM)],
        out_specs=(VMEM_SPEC, VMEM_SPEC),
        out_shape=(
            pltpu.VMEM((KEEP, ROWS, ZS), F32),
            jax.ShapeDtypeStruct((1, PACK * 128), F32),
        ),
        scratch_shapes=[
            pltpu.VMEM((KEEP, KEEP, 128), F32),
            pltpu.VMEM((BASIS, 128), F32),
            pltpu.SemaphoreType.DMA((KEEP // GROUP,)),
        ],
        compiler_params=PARAMS,
        name="gram",
    )(pltpu.with_memory_space_constraint(basis, pltpu.HBM))


def dot_all(v_ref, others, x_ref, dots_ref):
    dots_ref[...] = jnp.zeros((BASIS, 128), F32)
    batch = 12

    def run(reads, base):
        def step(c, accs):
            rows = pl.ds(pl.multiple_of(c * CHUNK, CHUNK), CHUNK)
            x = x_ref[rows, :]
            return tuple(acc + fold_tiles(read(rows) * x) for acc, read in zip(accs, reads))

        zero = jnp.zeros((8, ZS), F32)
        accs = lax.fori_loop(0, ROWS // CHUNK, step, tuple(zero for _ in reads))
        for n, acc in enumerate(accs):
            dots_ref[pl.ds(base + n, 1), :] = fold_row(acc)

    for first in range(0, KEEP, batch):
        run([lambda rows, i=i: v_ref[i, rows, :] for i in range(first, first + batch)], first)
    if others:
        run([lambda rows, r=r: r[rows, :] for r in others], KEEP)
    return to_row(jnp.sum(dots_ref[...], axis=1, keepdims=True))


def self_dots_kernel(count, *refs):
    v_ref, *others = refs[: 1 + count]
    out_ref, dots_ref = refs[1 + count :]
    out_ref[...] = dot_all(v_ref, others, others[-1], dots_ref)


def self_dots_call(v, created):
    count = len(created)
    return pl.pallas_call(
        functools.partial(self_dots_kernel, count),
        in_specs=[VMEM_SPEC] * (1 + count),
        out_specs=VMEM_SPEC,
        out_shape=jax.ShapeDtypeStruct((1, 128), F32),
        scratch_shapes=[pltpu.VMEM((BASIS, 128), F32)],
        compiler_params=PARAMS,
        name="self_dots_%d" % count,
    )(v, *created)


def write_edges(place_ref, u_ref, first_ref, second_ref, swap_ref):
    odd = place_ref[1] == 1
    upper = place_ref[0] == 1
    for x in range(2):
        low = u_ref[pl.ds(x * YS, YS), :]
        high = u_ref[pl.ds((XS - 2 + x) * YS, YS), :]
        first_ref[pl.ds(x * YS, YS), :] = jnp.where(odd, low, high)
        second_ref[pl.ds(x * YS, YS), :] = jnp.where(odd, high, low)
    for x in range(XS):
        low = u_ref[pl.ds(x * YS, 2), :]
        high = u_ref[pl.ds(x * YS + YS - 2, 2), :]
        swap_ref[pl.ds(2 * x, 2), :] = jnp.where(upper, low, high)


EDGE_SHAPES = (
    jax.ShapeDtypeStruct((2 * YS, ZS), F32),
    jax.ShapeDtypeStruct((2 * YS, ZS), F32),
    jax.ShapeDtypeStruct((2 * XS, ZS), F32),
)


LAST_SHAPES = (
    jax.ShapeDtypeStruct((1, 128), F32),
    jax.ShapeDtypeStruct((1, 128), F32),
    jax.ShapeDtypeStruct((1,), jnp.int32),
)


def edges_kernel(place_ref, v_hbm, first_ref, second_ref, swap_ref, u_ref, sem):
    copy = pltpu.make_async_copy(v_hbm.at[KEEP - 1], u_ref, sem)
    copy.start()
    copy.wait()
    write_edges(place_ref, u_ref, first_ref, second_ref, swap_ref)


def edges_call(place, basis):
    return pl.pallas_call(
        edges_kernel,
        in_specs=[SMEM_SPEC, pl.BlockSpec(memory_space=pltpu.HBM)],
        out_specs=(VMEM_SPEC,) * 3,
        out_shape=EDGE_SHAPES,
        scratch_shapes=[pltpu.VMEM((ROWS, ZS), F32), pltpu.SemaphoreType.DMA],
        compiler_params=PARAMS,
        name="edges",
    )(place, pltpu.with_memory_space_constraint(basis, pltpu.HBM))


def write_for_all(out_ref, rows):
    count = len(rows)
    period = count
    while period % 8:
        period += count
    for tile in range(period // 8):
        sub = iota((8, 128), 0)
        block = jnp.zeros((8, 128), F32)
        for r in range(8):
            block = jnp.where(sub == r, rows[(8 * tile + r) % count], block)
        for p in range(out_ref.shape[0] // period):
            out_ref[pl.ds(p * period + 8 * tile, 8), :] = block


def payload_rows(count):
    return 2 if count else 1 + PACK


def image_kernel(count, *refs):
    place_ref, v_ref, *others = refs[: 2 + count]
    first_ref, second_ref, swap_ref, reaction_ref, extra_ref = refs[2 + count : 7 + count]
    w_ref, out_ref, dots_ref, pad_ref = refs[7 + count :]
    odd = place_ref[1] == 1
    upper = place_ref[0].astype(F32)
    lower = 1.0 - upper
    source = others[-1] if others else v_ref.at[KEEP - 1]
    lane = iota((YS, ZS), 1)
    center = -6.0 - 1.5 * sum(WIND_SPEEDS)
    near = [1.0 + 2.0 * s for s in WIND_SPEEDS]
    far = [-0.5 * s for s in WIND_SPEEDS]

    def plane(x):
        if x < 0:
            rows = pl.ds((x + 2) * YS, YS)
            return jnp.where(odd, first_ref[rows, :], second_ref[rows, :])
        if x >= XS:
            rows = pl.ds(0, YS)
            return jnp.where(odd, second_ref[rows, :], first_ref[rows, :])
        return source[pl.ds(x * YS, YS), :]

    for x in range(XS):
        mine = plane(x)
        pad_ref[x, pl.ds(8, YS), :] = mine
        edge = swap_ref[pl.ds(2 * x, 2), :]
        pad_ref[x, pl.ds(6, 2), :] = edge * upper
        pad_ref[x, pl.ds(72, 1), :] = edge[0:1] * lower
        image = (center - reaction_ref[pl.ds(x * YS, YS), :]) * mine
        image = image + plane(x + 1) + near[0] * plane(x - 1) + far[0] * plane(x - 2)
        image = (
            image
            + pad_ref[x, pl.ds(9, YS), :]
            + near[1] * pad_ref[x, pl.ds(7, YS), :]
            + far[1] * pad_ref[x, pl.ds(6, YS), :]
        )
        image = (
            image
            + jnp.where(lane < ZS - 1, pltpu.roll(mine, ZS - 1, 1), 0.0)
            + near[2] * jnp.where(lane >= 1, pltpu.roll(mine, 1, 1), 0.0)
            + far[2] * jnp.where(lane >= 2, pltpu.roll(mine, 2, 1), 0.0)
        )
        w_ref[pl.ds(x * YS, YS), :] = image
    more = [w_ref] if count == STEPS - 1 else []
    rows = [dot_all(v_ref, others + more, w_ref, dots_ref)]
    rows += [extra_ref[:, pl.ds(128 * r, 128)] for r in range(payload_rows(count) - 1)]
    write_for_all(out_ref, rows)


def image_call(place, v, created, halo, reaction, extra, devices):
    count = len(created)
    return pl.pallas_call(
        functools.partial(image_kernel, count),
        in_specs=[SMEM_SPEC] + [VMEM_SPEC] * (6 + count),
        out_specs=(VMEM_SPEC, VMEM_SPEC),
        out_shape=(
            pltpu.VMEM((ROWS, ZS), F32),
            jax.ShapeDtypeStruct((devices * payload_rows(count), 128), F32),
        ),
        scratch_shapes=[
            pltpu.VMEM((BASIS, 128), F32),
            pltpu.VMEM((XS, YS + 16, ZS), F32),
        ],
        compiler_params=PARAMS,
        name="image_%d" % count,
    )(place, v, *created, *halo, reaction, extra)


STATE_G, STATE_H, STATE_D, STATE_ROWS = 0, BASIS, 2 * BASIS, 2 * BASIS + 8


def summed_rows(recv_ref, count):
    period = count
    while period % 8:
        period += count
    total = jnp.sum(recv_ref[...].reshape(-1, period, 128), axis=0)
    if count in (1, 2):
        while count < 8:
            total = total + pltpu.roll(total, 8 - count, 0)
            count *= 2
        return total
    return sum(total[p : p + count] for p in range(0, period, count))


def unpacked_gram(packed, pack_ref):
    pack_ref[...] = jnp.zeros((128, 128), F32)
    for p in range(HALF // PACK):
        part = packed
        if p:
            part = pltpu.roll(part, 128 - p * PACK_LANES, 1)
        pack_ref[pl.ds(p * PACK, PACK), :] = part
    turned = jnp.transpose(pack_ref[...])
    plain = pack_ref[pl.ds(0, HALF), :]
    lane = iota((HALF, 128), 1)
    sub = iota((HALF, 128), 0)
    diagonal = jnp.sum(jnp.where(lane == KEEP, plain, 0.0), axis=1, keepdims=True)
    top = jnp.where((lane > sub) | (lane >= HALF), plain, turned[:HALF])
    top = jnp.where(lane == sub, diagonal, top)
    last = jnp.where(lane <= sub, plain, turned[:HALF])
    pack_ref[...] = turned
    bottom = jnp.where(lane < HALF, pack_ref[pl.ds(HALF, HALF), :], pltpu.roll(last, HALF, 1))
    pack_ref[pl.ds(0, HALF), :] = jnp.where(lane < KEEP, top, 0.0)
    pack_ref[pl.ds(HALF, HALF), :] = jnp.where(lane < KEEP, bottom, 0.0)
    pack_ref[pl.ds(KEEP, STEPS), :] = jnp.zeros((STEPS, 128), F32)


def combine_kernel(count, cells, *refs):
    place_ref, recv_ref, w_ref, v_ref, *others = refs[: 4 + count]
    pos = 4 + count
    if count:
        state_in = refs[pos]
        pos += 1
    u_ref, state_ref, *outs, weight_ref, pack_ref = refs[pos:]
    final = count == STEPS - 1
    if final:
        square_ref, guess_ref, sound_ref = outs
    lane = iota((1, 128), 1)
    lanes = iota((BASIS, 128), 1)
    subs = iota((BASIS, 128), 0)
    scale = 1.0 / cells
    if count == 0:
        total = summed_rows(recv_ref, 1 + PACK) * scale
        unpacked_gram(total[1 : 1 + PACK], pack_ref)
        gram = pack_ref[pl.ds(0, BASIS), :]
        hess = jnp.zeros((BASIS, 128), F32)
        inverse_row = jnp.where(lane < KEEP, 1.0, 0.0)
        first_row = total[0:1]
        inverse = jnp.ones((1, 1), F32)
    else:
        total = summed_rows(recv_ref, 2) * scale
        newest = KEEP + count - 1
        raw_first, raw_gram = total[0:1], total[1:2]
        square = jnp.sum(jnp.where(lane == newest, raw_gram, 0.0), axis=1, keepdims=True)
        norm = jnp.sqrt(square + EPSILON)
        inverse = 1.0 / norm
        inverse_row = jnp.where(lane == newest, inverse, state_in[pl.ds(STATE_D, 1), :])
        gram_row = raw_gram * inverse_row * inverse
        first_row = raw_first * inverse_row * inverse
        gram = state_in[pl.ds(STATE_G, BASIS), :]
        gram = jnp.where(lanes == newest, to_column(gram_row), gram)
        gram = jnp.where(subs == newest, gram_row, gram)
        hess = state_in[pl.ds(STATE_H, BASIS), :]
        hess = jnp.where((subs == newest) & (lanes == count - 1), norm, hess)
    first = to_column(first_row)
    folded = jnp.sum(gram * first_row, axis=1, keepdims=True)
    weights = first + (first - folded)
    hess = jnp.where((lanes == count) & (subs < KEEP + count), weights, hess)
    if final:
        image_square = jnp.sum(jnp.where(lane == BASIS - 1, raw_first, 0.0), axis=1, keepdims=True)
        image_square = image_square * inverse * inverse
        again = jnp.sum(gram * to_row(weights), axis=1, keepdims=True)
        guess = image_square - jnp.sum(weights * (2.0 * first - again), axis=0, keepdims=True)
        guess_ref[...] = jnp.where(lane == 0, guess, 0.0)
        sound = jnp.where(guess > SOUND_SHARE * image_square, 1, 0)
        sound_ref[0] = sound[0, 0]
    state_ref[pl.ds(STATE_G, BASIS), :] = gram
    state_ref[pl.ds(STATE_H, BASIS), :] = hess
    state_ref[pl.ds(STATE_D, 8), :] = jnp.broadcast_to(inverse_row, (8, 128))
    weight_ref[...] = jnp.broadcast_to(weights * to_column(inverse_row), (BASIS, ZS))

    def step(c, acc):
        rows = pl.ds(pl.multiple_of(c * CHUNK, CHUNK), CHUNK)
        value = w_ref[rows, :] * inverse
        for i in range(KEEP):
            value = value - weight_ref[pl.ds(i, 1), :] * v_ref[i, rows, :]
        for i, other in enumerate(others):
            value = value - weight_ref[pl.ds(KEEP + i, 1), :] * other[rows, :]
        u_ref[rows, :] = value
        return acc + fold_tiles(value * value)

    acc = lax.fori_loop(0, ROWS // CHUNK, step, jnp.zeros((8, ZS), F32))
    if final:
        square_ref[...] = fold_row(acc)
    else:
        write_edges(place_ref, u_ref, *outs)


def combine_call(place, recv, w, v, created, state, cells):
    count = len(created)
    states = [state] if created else []
    final = count == STEPS - 1
    return pl.pallas_call(
        functools.partial(combine_kernel, count, cells),
        in_specs=[SMEM_SPEC] + [VMEM_SPEC] * (3 + count + len(states)),
        out_specs=(VMEM_SPEC,) * 4 + (SMEM_SPEC if final else VMEM_SPEC,),
        out_shape=(
            pltpu.VMEM((ROWS, ZS), F32),
            jax.ShapeDtypeStruct((STATE_ROWS, 128), F32),
            *(LAST_SHAPES if final else EDGE_SHAPES),
        ),
        scratch_shapes=[pltpu.VMEM((BASIS, ZS), F32), pltpu.VMEM((128, 128), F32)],
        compiler_params=PARAMS,
        name="combine_%d" % count,
    )(place, recv, w, v, *created, *states)


def finish_kernel(*refs):
    square_ref, state_ref, *created = refs[: 2 + STEPS]
    new_ref, hess_ref = refs[2 + STEPS :]
    lane = iota((1, 128), 1)
    norm = jnp.sqrt(jnp.sum(square_ref[...], axis=1, keepdims=True) + EPSILON)
    lanes = iota((BASIS, 128), 1)
    subs = iota((BASIS, 128), 0)
    hess = state_ref[pl.ds(STATE_H, BASIS), :]
    hess = jnp.where((subs == BASIS - 1) & (lanes == STEPS - 1), norm, hess)
    hess_ref[...] = jnp.transpose(jnp.concatenate([hess, jnp.zeros((128 - BASIS, 128), F32)], axis=0))[:STEPS, :BASIS]
    inverse_row = state_ref[pl.ds(STATE_D, 1), :]
    for j, u_ref in enumerate(created):
        if j == STEPS - 1:
            inverse = 1.0 / norm
        else:
            inverse = jnp.sum(jnp.where(lane == KEEP + j, inverse_row, 0.0), axis=1, keepdims=True)
        for c in range(ROWS // CHUNK):
            rows = pl.ds(c * CHUNK, CHUNK)
            new_ref[j, rows, :] = u_ref[rows, :] * inverse


def finish_call(square, state, created):
    return pl.pallas_call(
        finish_kernel,
        in_specs=[VMEM_SPEC] * (2 + STEPS),
        out_specs=(VMEM_SPEC, VMEM_SPEC),
        out_shape=(
            jax.ShapeDtypeStruct((STEPS, ROWS, ZS), F32),
            jax.ShapeDtypeStruct((STEPS, BASIS), F32),
        ),
        compiler_params=PARAMS,
        name="finish",
    )(square, state, *created)


def exchange(first, second, swap):
    count = lax.axis_size("gx")

    def pairs(start):
        lower = range(start, count - 1, 2)
        return [(i, i + 1) for i in lower] + [(i + 1, i) for i in lower]

    second = lax.ppermute(second, "gx", pairs(1))
    first = lax.ppermute(first, "gx", pairs(0))
    swap = lax.ppermute(swap, "gy", [(0, 1), (1, 0)])
    return first, second, swap


def from_all(payload):
    axes = ("gy", "gx")
    devices = lax.axis_size(axes)
    copies = payload.reshape(devices, 1, -1)
    got = lax.all_to_all(copies, axes, split_axis=0, concat_axis=0, tiled=True)
    return got.reshape(-1, 128)


def body(basis_vectors, reaction):
    devices = lax.axis_size(("gy", "gx"))
    cells = float(ROWS * ZS * devices)
    place = jnp.stack([lax.axis_index("gy"), lax.axis_index("gx") % 2]).astype(jnp.int32)
    basis = basis_vectors.reshape(KEEP, ROWS, ZS)
    halo = exchange(*edges_call(place, basis))
    reaction = reaction.reshape(ROWS, ZS)
    v, extra = gram_call(basis)
    created = []
    state = None
    for j in range(STEPS):
        if j:
            extra = self_dots_call(v, created)
        w, payload = image_call(place, v, created, halo, reaction, extra, devices)
        recv = from_all(payload)
        u, state, *edges = combine_call(place, recv, w, v, created, state, cells)
        created.append(u)
        if j + 1 < STEPS:
            halo = exchange(*edges)
    square, guess, sound = edges
    square = lax.cond(
        sound[0] == 1,
        lambda guess, square: guess,
        lambda guess, square: jnp.sum(from_all(square), axis=0, keepdims=True) * (1.0 / cells),
        guess,
        jnp.broadcast_to(square, (devices, 128)),
    )
    new, hessenberg = finish_call(square, state, created)
    return new.reshape(STEPS, XS, YS, ZS), hessenberg.T


def solution(mesh):
    return jax.shard_map(
        body,
        mesh=mesh,
        in_specs=(P(None, "gx", "gy", None), P("gx", "gy", None)),
        out_specs=(P(None, "gx", "gy", None), P()),
        check_vma=False,
    )
```

time: 188 us -> 140 us (0.74)
  blocking collectives: 115 us -> 87 us
  starting transfers between devices: 21.2 us -> 9.92 us
  local copies, waits for them, and re-layouts: 7.34 us -> 0.01 us
    all_to_all x5 -> x4, blocking collectives: 115 us -> 87 us  [from_all(): got = lax.all_to_all(copies, axes, split_axis=0, concat_axis=0, tiled=True)]
    ppermute x8, starting transfers between devices: 16.3 us -> 5.84 us  [the longest x4 3.21 us: exchange(): first = lax.ppermute(first, 'gx', pairs(0))]
    unnamed x5 -> x2, local copies, waits for them, and re-layouts: 4.33 us -> 0.01 us
    pallas_call x6 -> x7, Pallas kernels: 27 us -> 26.9 us  [the longest x1 16.4 us: gram_call(): pl.pallas_call(gram_kernel, in_specs=[pl.BlockSpec(memory_space=pltpu.HBM...]
  transfers between devices with their start and end apart: 12 -> 12, of which waited for: 3 -> 3; matrix products, arithmetic and copies ran while one was open for 1% -> 0% of each run, Pallas kernels for 13% -> 14%
where the time goes in v2:
time: 140 us
  blocking collectives  87 us (62%)
  Pallas kernels  37.7 us (27%)
  starting transfers between devices  9.92 us (7%)
  waiting for transfers between devices  4.07 us (3%)
  between operations  1.44 us (1%)
    all_to_all x4, blocking collectives, from_all(): got = lax.all_to_all(copies, axes, split_axis=0, concat_axis=0, tiled=True)  87 us
    pallas_call x1, Pallas kernels, gram_call(): pl.pallas_call(gram_kernel, in_specs=[pl.BlockSpec(memory_space=pltpu.HBM...  16.4 us
    pallas_call x4, Pallas kernels, image_call(): pl.pallas_call(functools.partial(image_kernel, count), in_specs=[SMEM_SPE...  7.86 us
    pallas_call x4, Pallas kernels, combine_call(): pl.pallas_call(functools.partial(combine_kernel, count, cells), in_specs=...  7.49 us
    ppermute x4, starting transfers between devices, exchange(): swap = lax.ppermute(swap, 'gy', [(0, 1), (1, 0)])  4.09 us
    ppermute x4, waiting for transfers between devices, exchange(): first = lax.ppermute(first, 'gx', pairs(0))  4.05 us
    pallas_call x3, Pallas kernels, self_dots_call(): pl.pallas_call(functools.partial(self_dots_kernel, count), in_specs=[VMEM...  3.3 us
    ppermute x4, starting transfers between devices, exchange(): first = lax.ppermute(first, 'gx', pairs(0))  3.21 us
  transfers between devices with their start and end apart: 12, of which 3 were waited for; matrix products, arithmetic and copies ran while one was open for 0% of the time, Pallas kernels for 14%

profile of v2, /device:TPU:1, one launch (start us, length us, event | category | flops | bytes accessed | tf_op | source)
XLA Modules:
  0.0 140.2 jit_solution(5929664820028457650)
XLA Ops:
  0.7 1.5 %edges.1 = (f32[128,256]{1,0:T(8,128)S(1)}, f32[128,256]{1,0:T(8,128)S(1)}, f32[8,256]{1,0:T(8,128)S(1)}) custom-call(s32[2]{0:T(128)S(1)} %pad_add_fusion.place_ref.refs_0_, f32[36,256,256]{2,1,0:T(8,128)} %bitcast.31), custom_call_target="tpu_custom_call" | custom-call | tf_op jit(solution)/shard_map/edges/pallas_call | solution.py:212
  2.2 2.1 %collective-permute-start = (f32[128,256]{1,0:T(8,128)S(1)}, f32[128,256]{1,0:T(8,128)S(1)}, u32[]{:S(2)}, u32[]{:S(2)}) collective-permute-start(f32[128,256]{1,0:T(8,128)S(1)} %get-tuple-element.45), channel_id=1, source_target_pairs={{0,1},{2,3},{4,5},{6,7},{8,9},{10,11},{12,13},{14,15},{16,17},{18,... | collective-permute-start | bytes 393224 | tf_op jit(solution)/shard_map/ppermute | solution.py:480
  5.0 1.0 collective-permute-start.2
  6.1 16.4 %gram.1 = (f32[36,256,256]{2,1,0:T(8,128)S(1)}, f32[1,768]{1,0:T(1,128)S(1)}) custom-call(f32[36,256,256]{2,1,0:T(8,128)} %bitcast.32), custom_call_target="tpu_custom_call" | custom-call | tf_op jit(solution)/shard_map/gram/pallas_call | solution.py:117
  22.5 1.9 %image_0.1 = (f32[256,256]{1,0:T(8,128)S(1)}, f32[896,128]{1,0:T(8,128)S(1)}) custom-call(s32[2]{0:T(128)S(1)} %pad_add_fusion.place_ref.refs_0_, f32[36,256,256]{2,1,0:T(8,128)S(1)} %get-tuple-element.44.refs_1_.refs_3_.refs_0_, f32[128,256]{1,0:T(8,128)S(1)} %collective-permute-done.refs_2_, f32[128,256]{1,0:T(8,128)S(1)} %collective-permute-done.1.refs_3_, ...), custom_call_target="tpu_custom_call" | custom-call | tf_op jit(solution)/shard_map/image_0/pallas_call | solution.py:292
  24.4 24.9 %all_to_all.25 = f32[128,1,896]{2,1,0:T(1,128)S(1)} all-to-all(f32[128,1,896]{2,1,0:T(1,128)S(1)} %bitcast.27), channel_id=1, replica_groups=mesh['gy'=2,'gx'=64] {'gy','gx'}, dimensions={0} | all-to-all | bytes 917504 | tf_op jit(solution)/shard_map/all_to_all | solution.py:489
  49.3 1.7 %combine_0.1 = (f32[256,256]{1,0:T(8,128)S(1)}, f32[88,128]{1,0:T(8,128)S(1)}, f32[128,256]{1,0:T(8,128)S(1)}, f32[128,256]{1,0:T(8,128)S(1)}, f32[8,256]{1,0:T(8,128)S(1)}) custom-call(s32[2]{0:T(128)S(1)} %pad_add_fusion.place_ref.refs_0_, f32[896,128]{1,0:T(8,128)S(1)} %bitcast.23, f32[256,256]{1,0:T(8,128)S(1)} %get-tuple-element.50.refs_2_, ...), custom_call_target="tpu_custom_call" | custom-call | tf_op jit(solution)/shard_map/combine_0/pallas_call | solution.py:422
  52.0 1.2 collective-permute-start.5
  53.2 1.1 self_dots_1.1.refs_7_
  54.3 1.1 collective-permute-done.3.refs_3_
  55.3 2.0 %image_1.1 = (f32[256,256]{1,0:T(8,128)S(1)}, f32[256,128]{1,0:T(8,128)S(1)}) custom-call(s32[2]{0:T(128)S(1)} %pad_add_fusion.place_ref.refs_0_, f32[36,256,256]{2,1,0:T(8,128)S(1)} %get-tuple-element.44.refs_1_.refs_3_.refs_0_, f32[256,256]{1,0:T(8,128)S(1)} %get-tuple-element.51.refs_1_.refs_2_.refs_4_, f32[128,256]{1,0:T(8,128)S(1)} %collective-permute-done.3.refs_3_, ...), custom_call_target="tpu_custom_call" | custom-call | tf_op jit(solution)/shard_map/image_1/pallas_call | solution.py:292
  57.3 21.0 %all_to_all.26 = f32[128,1,256]{2,1,0:T(1,128)S(1)} all-to-all(f32[128,1,256]{2,1,0:T(1,128)S(1)} %bitcast.28), channel_id=1, replica_groups=mesh['gy'=2,'gx'=64] {'gy','gx'}, dimensions={0} | all-to-all | bytes 262144 | tf_op jit(solution)/shard_map/all_to_all | solution.py:489
  78.3 1.7 %combine_1.1 = (f32[256,256]{1,0:T(8,128)S(1)}, f32[88,128]{1,0:T(8,128)S(1)}, f32[128,256]{1,0:T(8,128)S(1)}, f32[128,256]{1,0:T(8,128)S(1)}, f32[8,256]{1,0:T(8,128)S(1)}) custom-call(s32[2]{0:T(128)S(1)} %pad_add_fusion.place_ref.refs_0_, f32[256,128]{1,0:T(8,128)S(1)} %bitcast.25, f32[256,256]{1,0:T(8,128)S(1)} %get-tuple-element.56.refs_2_, ...), custom_call_target="tpu_custom_call" | custom-call | tf_op jit(solution)/shard_map/combine_1/pallas_call | solution.py:422
  82.0 1.1 self_dots_2.1.refs_8_
  83.1 1.5 %collective-permute-done.6.refs_4_ = f32[128,256]{1,0:T(8,128)S(1)} collective-permute-done((f32[128,256]{1,0:T(8,128)S(1)}, f32[128,256]{1,0:T(8,128)S(1)}, u32[]{:S(2)}, u32[]{:S(2)}) %collective-permute-start.6) | collective-permute-done | bytes 131104 | tf_op jit(solution)/shard_map/ppermute | solution.py:480
  84.6 2.0 %image_2.1 = (f32[256,256]{1,0:T(8,128)S(1)}, f32[256,128]{1,0:T(8,128)S(1)}) custom-call(s32[2]{0:T(128)S(1)} %pad_add_fusion.place_ref.refs_0_, f32[36,256,256]{2,1,0:T(8,128)S(1)} %get-tuple-element.44.refs_1_.refs_3_.refs_0_, f32[256,256]{1,0:T(8,128)S(1)} %get-tuple-element.51.refs_1_.refs_2_.refs_4_, ...), custom_call_target="tpu_custom_call" | custom-call | tf_op jit(solution)/shard_map/image_2/pallas_call | solution.py:292
  86.6 20.5 %all_to_all.27 = f32[128,1,256]{2,1,0:T(1,128)S(1)} all-to-all(f32[128,1,256]{2,1,0:T(1,128)S(1)} %bitcast.29), channel_id=1, replica_groups=mesh['gy'=2,'gx'=64] {'gy','gx'}, dimensions={0} | all-to-all | bytes 262144 | tf_op jit(solution)/shard_map/all_to_all | solution.py:489
  107.1 1.7 %combine_2.1 = (f32[256,256]{1,0:T(8,128)S(1)}, f32[88,128]{1,0:T(8,128)S(1)}, f32[128,256]{1,0:T(8,128)S(1)}, f32[128,256]{1,0:T(8,128)S(1)}, f32[8,256]{1,0:T(8,128)S(1)}) custom-call(s32[2]{0:T(128)S(1)} %pad_add_fusion.place_ref.refs_0_, f32[256,128]{1,0:T(8,128)S(1)} %bitcast.26, f32[256,256]{1,0:T(8,128)S(1)} %get-tuple-element.63.refs_2_, ...), custom_call_target="tpu_custom_call" | custom-call | tf_op jit(solution)/shard_map/combine_2/pallas_call | solution.py:422
  110.8 1.1 self_dots_3.1.refs_9_
  111.9 1.5 %collective-permute-done.9.refs_5_ = f32[128,256]{1,0:T(8,128)S(1)} collective-permute-done((f32[128,256]{1,0:T(8,128)S(1)}, f32[128,256]{1,0:T(8,128)S(1)}, u32[]{:S(2)}, u32[]{:S(2)}) %collective-permute-start.9) | collective-permute-done | bytes 131104 | tf_op jit(solution)/shard_map/ppermute | solution.py:480
  113.4 2.0 %image_3.1 = (f32[256,256]{1,0:T(8,128)S(1)}, f32[256,128]{1,0:T(8,128)S(1)}) custom-call(s32[2]{0:T(128)S(1)} %pad_add_fusion.place_ref.refs_0_, f32[36,256,256]{2,1,0:T(8,128)S(1)} %get-tuple-element.44.refs_1_.refs_3_.refs_0_, f32[256,256]{1,0:T(8,128)S(1)} %get-tuple-element.51.refs_1_.refs_2_.refs_4_, ...), custom_call_target="tpu_custom_call" | custom-call | tf_op jit(solution)/shard_map/image_3/pallas_call | solution.py:292
  115.4 20.5 %all_to_all.28 = f32[128,1,256]{2,1,0:T(1,128)S(1)} all-to-all(f32[128,1,256]{2,1,0:T(1,128)S(1)} %bitcast.30), channel_id=1, replica_groups=mesh['gy'=2,'gx'=64] {'gy','gx'}, dimensions={0} | all-to-all | bytes 262144 | tf_op jit(solution)/shard_map/all_to_all | solution.py:489
  136.0 2.4 %combine_3.1 = (f32[256,256]{1,0:T(8,128)S(1)}, f32[88,128]{1,0:T(8,128)S(1)}, f32[1,128]{1,0:T(1,128)S(1)}, f32[1,128]{1,0:T(1,128)S(1)}, s32[1]{0:T(128)}) custom-call(s32[2]{0:T(128)S(1)} %pad_add_fusion.place_ref.refs_0_, f32[256,128]{1,0:T(8,128)S(1)} %bitcast.24, f32[256,256]{1,0:T(8,128)S(1)} %get-tuple-element.70.refs_2_, ...), custom_call_target="tpu_custom_call" | custom-call | tf_op jit(solution)/shard_map/combine_3/pallas_call | solution.py:422
  139.0 1.1 finish.1
  (22 shorter events, 5.7 us)
Async XLA Ops:
  0.7 21.7 %copy-start = (f32[4,64,256]{2,1,0:T(8,128)S(1)}, f32[4,64,256]{2,1,0:T(8,128)}, u32[]{:S(2)}) copy-start(f32[4,64,256]{2,1,0:T(8,128)} %param.5) | copy-start | bytes 786436
  2.2 20.2 %collective-permute-start = (f32[128,256]{1,0:T(8,128)S(1)}, f32[128,256]{1,0:T(8,128)S(1)}, u32[]{:S(2)}, u32[]{:S(2)}) collective-permute-start(f32[128,256]{1,0:T(8,128)S(1)} %get-tuple-element.45), channel_id=1, source_target_pairs={{0,1},{2,3},{4,5},{6,7},{8,9},{10,11},{12,13},{14,15},{16,17},{18,... | collective-permute-start | bytes 393224 | tf_op jit(solution)/shard_map/ppermute | solution.py:480
  4.4 18.1 %collective-permute-start.1 = (f32[128,256]{1,0:T(8,128)S(1)}, f32[128,256]{1,0:T(8,128)S(1)}, u32[]{:S(2)}, u32[]{:S(2)}) collective-permute-start(f32[128,256]{1,0:T(8,128)S(1)} %get-tuple-element.46), channel_id=1, source_target_pairs={{1,2},{3,4},{5,6},{7,8},{9,10},{11,12},{13,14},{15,16},{17,18},{19... | collective-permute-start | bytes 393224 | tf_op jit(solution)/shard_map/ppermute | solution.py:479
  5.0 17.4 %collective-permute-start.2 = (f32[8,256]{1,0:T(8,128)S(1)}, f32[8,256]{1,0:T(8,128)S(1)}, u32[]{:S(2)}, u32[]{:S(2)}) collective-permute-start(f32[8,256]{1,0:T(8,128)S(1)} %get-tuple-element.47), channel_id=1, source_target_pairs={{0,64},{64,0},{1,65},{65,1},{2,66},{66,2},{3,67},{67,3},{4,68},{68... | collective-permute-start | bytes 24584 | tf_op jit(solution)/shard_map/ppermute | solution.py:481
  51.0 4.4 %collective-permute-start.3 = (f32[128,256]{1,0:T(8,128)S(1)}, f32[128,256]{1,0:T(8,128)S(1)}, u32[]{:S(2)}, u32[]{:S(2)}) collective-permute-start(f32[128,256]{1,0:T(8,128)S(1)} %get-tuple-element.52), channel_id=1, source_target_pairs={{0,1},{2,3},{4,5},{6,7},{8,9},{10,11},{12,13},{14,15},{16,17},{18,... | collective-permute-start | bytes 393224 | tf_op jit(solution)/shard_map/ppermute | solution.py:480
  51.4 4.0 %collective-permute-start.4 = (f32[128,256]{1,0:T(8,128)S(1)}, f32[128,256]{1,0:T(8,128)S(1)}, u32[]{:S(2)}, u32[]{:S(2)}) collective-permute-start(f32[128,256]{1,0:T(8,128)S(1)} %get-tuple-element.53), channel_id=1, source_target_pairs={{1,2},{3,4},{5,6},{7,8},{9,10},{11,12},{13,14},{15,16},{17,18},{19... | collective-permute-start | bytes 393224 | tf_op jit(solution)/shard_map/ppermute | solution.py:479
  52.0 2.3 %collective-permute-start.5 = (f32[8,256]{1,0:T(8,128)S(1)}, f32[8,256]{1,0:T(8,128)S(1)}, u32[]{:S(2)}, u32[]{:S(2)}) collective-permute-start(f32[8,256]{1,0:T(8,128)S(1)} %get-tuple-element.54), channel_id=1, source_target_pairs={{0,64},{64,0},{1,65},{65,1},{2,66},{66,2},{3,67},{67,3},{4,68},{68... | collective-permute-start | bytes 24584 | tf_op jit(solution)/shard_map/ppermute | solution.py:481
  80.0 4.6 %collective-permute-start.6 = (f32[128,256]{1,0:T(8,128)S(1)}, f32[128,256]{1,0:T(8,128)S(1)}, u32[]{:S(2)}, u32[]{:S(2)}) collective-permute-start(f32[128,256]{1,0:T(8,128)S(1)} %get-tuple-element.59), channel_id=1, source_target_pairs={{0,1},{2,3},{4,5},{6,7},{8,9},{10,11},{12,13},{14,15},{16,17},{18,... | collective-permute-start | bytes 393224 | tf_op jit(solution)/shard_map/ppermute | solution.py:480
  80.4 4.2 %collective-permute-start.7 = (f32[128,256]{1,0:T(8,128)S(1)}, f32[128,256]{1,0:T(8,128)S(1)}, u32[]{:S(2)}, u32[]{:S(2)}) collective-permute-start(f32[128,256]{1,0:T(8,128)S(1)} %get-tuple-element.60), channel_id=1, source_target_pairs={{1,2},{3,4},{5,6},{7,8},{9,10},{11,12},{13,14},{15,16},{17,18},{19... | collective-permute-start | bytes 393224 | tf_op jit(solution)/shard_map/ppermute | solution.py:479
  81.0 2.0 %collective-permute-start.8 = (f32[8,256]{1,0:T(8,128)S(1)}, f32[8,256]{1,0:T(8,128)S(1)}, u32[]{:S(2)}, u32[]{:S(2)}) collective-permute-start(f32[8,256]{1,0:T(8,128)S(1)} %get-tuple-element.61), channel_id=1, source_target_pairs={{0,64},{64,0},{1,65},{65,1},{2,66},{66,2},{3,67},{67,3},{4,68},{68... | collective-permute-start | bytes 24584 | tf_op jit(solution)/shard_map/ppermute | solution.py:481
  108.8 4.6 %collective-permute-start.9 = (f32[128,256]{1,0:T(8,128)S(1)}, f32[128,256]{1,0:T(8,128)S(1)}, u32[]{:S(2)}, u32[]{:S(2)}) collective-permute-start(f32[128,256]{1,0:T(8,128)S(1)} %get-tuple-element.66), channel_id=1, source_target_pairs={{0,1},{2,3},{4,5},{6,7},{8,9},{10,11},{12,13},{14,15},{16,17},{18,... | collective-permute-start | bytes 393224 | tf_op jit(solution)/shard_map/ppermute | solution.py:480
  109.2 4.2 %collective-permute-start.10 = (f32[128,256]{1,0:T(8,128)S(1)}, f32[128,256]{1,0:T(8,128)S(1)}, u32[]{:S(2)}, u32[]{:S(2)}) collective-permute-start(f32[128,256]{1,0:T(8,128)S(1)} %get-tuple-element.67), channel_id=1, source_target_pairs={{1,2},{3,4},{5,6},{7,8},{9,10},{11,12},{13,14},{15,16},{17,18},{19... | collective-permute-start | bytes 393224 | tf_op jit(solution)/shard_map/ppermute | solution.py:479
  109.9 2.1 %collective-permute-start.11 = (f32[8,256]{1,0:T(8,128)S(1)}, f32[8,256]{1,0:T(8,128)S(1)}, u32[]{:S(2)}, u32[]{:S(2)}) collective-permute-start(f32[8,256]{1,0:T(8,128)S(1)} %get-tuple-element.68), channel_id=1, source_target_pairs={{0,64},{64,0},{1,65},{65,1},{2,66},{66,2},{3,67},{67,3},{4,68},{68... | collective-permute-start | bytes 24584 | tf_op jit(solution)/shard_map/ppermute | solution.py:481

commit v3 on v2

--- a/solution.py
+++ b/solution.py
@@ -6,6 +6,7 @@
 from jax.experimental import pallas as pl
 from jax.experimental.pallas import tpu as pltpu
 from jax.sharding import PartitionSpec as P
+
 
 KEEP = 36
 STEPS = 4
@@ -169,13 +170,12 @@
         out_shape=jax.ShapeDtypeStruct((1, 128), F32),
         scratch_shapes=[pltpu.VMEM((BASIS, 128), F32)],
         compiler_params=PARAMS,
-        name="self_dots_%d" % count,
     )(v, *created)
 
 
-def write_edges(place_ref, u_ref, first_ref, second_ref, swap_ref):
-    odd = place_ref[1] == 1
-    upper = place_ref[0] == 1
+def write_edges(u_ref, first_ref, second_ref, swap_ref):
+    odd = lax.axis_index("gx") % 2 == 1
+    upper = lax.axis_index("gy") == 1
     for x in range(2):
         low = u_ref[pl.ds(x * YS, YS), :]
         high = u_ref[pl.ds((XS - 2 + x) * YS, YS), :]
@@ -201,23 +201,23 @@
 )
 
 
-def edges_kernel(place_ref, v_hbm, first_ref, second_ref, swap_ref, u_ref, sem):
+def edges_kernel(v_hbm, first_ref, second_ref, swap_ref, u_ref, sem):
     copy = pltpu.make_async_copy(v_hbm.at[KEEP - 1], u_ref, sem)
     copy.start()
     copy.wait()
-    write_edges(place_ref, u_ref, first_ref, second_ref, swap_ref)
-
-
-def edges_call(place, basis):
+    write_edges(u_ref, first_ref, second_ref, swap_ref)
+
+
+def edges_call(basis):
     return pl.pallas_call(
         edges_kernel,
-        in_specs=[SMEM_SPEC, pl.BlockSpec(memory_space=pltpu.HBM)],
+        in_specs=[pl.BlockSpec(memory_space=pltpu.HBM)],
         out_specs=(VMEM_SPEC,) * 3,
         out_shape=EDGE_SHAPES,
         scratch_shapes=[pltpu.VMEM((ROWS, ZS), F32), pltpu.SemaphoreType.DMA],
         compiler_params=PARAMS,
         name="edges",
-    )(place, pltpu.with_memory_space_constraint(basis, pltpu.HBM))
+    )(pltpu.with_memory_space_constraint(basis, pltpu.HBM))
 
 
 def write_for_all(out_ref, rows):
@@ -239,11 +239,11 @@
 
 
 def image_kernel(count, *refs):
-    place_ref, v_ref, *others = refs[: 2 + count]
-    first_ref, second_ref, swap_ref, reaction_ref, extra_ref = refs[2 + count : 7 + count]
-    w_ref, out_ref, dots_ref, pad_ref = refs[7 + count :]
-    odd = place_ref[1] == 1
-    upper = place_ref[0].astype(F32)
+    v_ref, *others = refs[: 1 + count]
+    first_ref, second_ref, swap_ref, reaction_ref, extra_ref = refs[1 + count : 6 + count]
+    w_ref, out_ref, dots_ref, pad_ref = refs[6 + count :]
+    odd = lax.axis_index("gx") % 2 == 1
+    upper = lax.axis_index("gy").astype(F32)
     lower = 1.0 - upper
     source = others[-1] if others else v_ref.at[KEEP - 1]
     lane = iota((YS, ZS), 1)
@@ -287,11 +287,11 @@
     write_for_all(out_ref, rows)
 
 
-def image_call(place, v, created, halo, reaction, extra, devices):
+def image_call(v, created, halo, reaction, extra, devices):
     count = len(created)
     return pl.pallas_call(
         functools.partial(image_kernel, count),
-        in_specs=[SMEM_SPEC] + [VMEM_SPEC] * (6 + count),
+        in_specs=[VMEM_SPEC] * (6 + count),
         out_specs=(VMEM_SPEC, VMEM_SPEC),
         out_shape=(
             pltpu.VMEM((ROWS, ZS), F32),
@@ -302,8 +302,7 @@
             pltpu.VMEM((XS, YS + 16, ZS), F32),
         ],
         compiler_params=PARAMS,
-        name="image_%d" % count,
-    )(place, v, *created, *halo, reaction, extra)
+    )(v, *created, *halo, reaction, extra)
 
 
 STATE_G, STATE_H, STATE_D, STATE_ROWS = 0, BASIS, 2 * BASIS, 2 * BASIS + 8
@@ -345,8 +344,8 @@
 
 
 def combine_kernel(count, cells, *refs):
-    place_ref, recv_ref, w_ref, v_ref, *others = refs[: 4 + count]
-    pos = 4 + count
+    recv_ref, w_ref, v_ref, *others = refs[: 3 + count]
+    pos = 3 + count
     if count:
         state_in = refs[pos]
         pos += 1
@@ -412,16 +411,16 @@
     if final:
         square_ref[...] = fold_row(acc)
     else:
-        write_edges(place_ref, u_ref, *outs)
-
-
-def combine_call(place, recv, w, v, created, state, cells):
+        write_edges(u_ref, *outs)
+
+
+def combine_call(recv, w, v, created, state, cells):
     count = len(created)
     states = [state] if created else []
     final = count == STEPS - 1
     return pl.pallas_call(
         functools.partial(combine_kernel, count, cells),
-        in_specs=[SMEM_SPEC] + [VMEM_SPEC] * (3 + count + len(states)),
+        in_specs=[VMEM_SPEC] * (3 + count + len(states)),
         out_specs=(VMEM_SPEC,) * 4 + (SMEM_SPEC if final else VMEM_SPEC,),
         out_shape=(
             pltpu.VMEM((ROWS, ZS), F32),
@@ -430,8 +429,7 @@
         ),
         scratch_shapes=[pltpu.VMEM((BASIS, ZS), F32), pltpu.VMEM((128, 128), F32)],
         compiler_params=PARAMS,
-        name="combine_%d" % count,
-    )(place, recv, w, v, *created, *states)
+    )(recv, w, v, *created, *states)
 
 
 def finish_kernel(*refs):
@@ -493,9 +491,8 @@
 def body(basis_vectors, reaction):
     devices = lax.axis_size(("gy", "gx"))
     cells = float(ROWS * ZS * devices)
-    place = jnp.stack([lax.axis_index("gy"), lax.axis_index("gx") % 2]).astype(jnp.int32)
     basis = basis_vectors.reshape(KEEP, ROWS, ZS)
-    halo = exchange(*edges_call(place, basis))
+    halo = exchange(*edges_call(basis))
     reaction = reaction.reshape(ROWS, ZS)
     v, extra = gram_call(basis)
     created = []
@@ -503,9 +500,9 @@
     for j in range(STEPS):
         if j:
             extra = self_dots_call(v, created)
-        w, payload = image_call(place, v, created, halo, reaction, extra, devices)
+        w, payload = image_call(v, created, halo, reaction, extra, devices)
         recv = from_all(payload)
-        u, state, *edges = combine_call(place, recv, w, v, created, state, cells)
+        u, state, *edges = combine_call(recv, w, v, created, state, cells)
         created.append(u)
         if j + 1 < STEPS:
             halo = exchange(*edges)

time: 140 us -> 137 us (0.979)
  Pallas kernels: 37.7 us -> 33.8 us
    pallas_call x5, Pallas kernels: 9.38 us -> 6.74 us  [the longest x4 5.71 us: image_call(): pl.pallas_call(functools.partial(image_kernel, count), in_specs=[VMEM_SPE...]
where the time goes in v3:
time: 137 us; the launch traced here: 136 us
  blocking collectives  87 us (64%)
  Pallas kernels  33.8 us (25%)
  starting transfers between devices  9.92 us (7%)
  waiting for transfers between devices  4.07 us (3%)
  between operations  1.43 us (1%)
    all_to_all x4, blocking collectives, from_all(): got = lax.all_to_all(copies, axes, split_axis=0, concat_axis=0, tiled=True)  87 us
    pallas_call x1, Pallas kernels, gram_call(): pl.pallas_call(gram_kernel, in_specs=[pl.BlockSpec(memory_space=pltpu.HBM...  16.4 us
    pallas_call x4, Pallas kernels, combine_call(): pl.pallas_call(functools.partial(combine_kernel, count, cells), in_specs=...  6.26 us
    pallas_call x4, Pallas kernels, image_call(): pl.pallas_call(functools.partial(image_kernel, count), in_specs=[VMEM_SPE...  5.71 us
    ppermute x4, starting transfers between devices, exchange(): swap = lax.ppermute(swap, 'gy', [(0, 1), (1, 0)])  4.09 us
    ppermute x4, waiting for transfers between devices, exchange(): first = lax.ppermute(first, 'gx', pairs(0))  4.05 us
    pallas_call x3, Pallas kernels, self_dots_call(): pl.pallas_call(functools.partial(self_dots_kernel, count), in_specs=[VMEM...  3.3 us
    ppermute x4, starting transfers between devices, exchange(): first = lax.ppermute(first, 'gx', pairs(0))  3.21 us
  transfers between devices with their start and end apart: 12, of which 3 were waited for; matrix products, arithmetic and copies ran while one was open for 0% of the time, Pallas kernels for 14%

profile of v3, /device:TPU:1, one launch (start us, length us, event | category | flops | bytes accessed | tf_op | source)
XLA Modules:
  0.0 136.2 jit_solution(14841751094720260888)
XLA Ops:
  0.6 1.0 edges.1
  1.7 2.1 %collective-permute-start = (f32[128,256]{1,0:T(8,128)S(1)}, f32[128,256]{1,0:T(8,128)S(1)}, u32[]{:S(2)}, u32[]{:S(2)}) collective-permute-start(f32[128,256]{1,0:T(8,128)S(1)} %get-tuple-element.45), channel_id=1, source_target_pairs={{0,1},{2,3},{4,5},{6,7},{8,9},{10,11},{12,13},{14,15},{16,17},{18,... | collective-permute-start | bytes 393224 | tf_op jit(solution)/shard_map/ppermute | solution.py:478
  4.5 1.0 collective-permute-start.2
  5.5 16.4 %gram.1 = (f32[36,256,256]{2,1,0:T(8,128)S(1)}, f32[1,768]{1,0:T(1,128)S(1)}) custom-call(f32[36,256,256]{2,1,0:T(8,128)} %bitcast.30), custom_call_target="tpu_custom_call" | custom-call | tf_op jit(solution)/shard_map/gram/pallas_call | solution.py:118
  21.9 1.4 %shard_map.41 = (f32[256,256]{1,0:T(8,128)S(1)}, f32[896,128]{1,0:T(8,128)S(1)}) custom-call(f32[36,256,256]{2,1,0:T(8,128)S(1)} %get-tuple-element.44.refs_0_.refs_2_, f32[128,256]{1,0:T(8,128)S(1)} %collective-permute-done.refs_1_, f32[128,256]{1,0:T(8,128)S(1)} %collective-permute-done.1.refs_2_, f32[8,256]{1,0:T(8,128)S(1)} %collective-permute-done.2.refs_3_, ...), custom_call_target="tpu_custom_call" | custom-call | tf_op jit(solution)/shard_map/pallas_call | solution.py:292
  23.3 24.9 %all_to_all.25 = f32[128,1,896]{2,1,0:T(1,128)S(1)} all-to-all(f32[128,1,896]{2,1,0:T(1,128)S(1)} %bitcast.25), channel_id=1, replica_groups=mesh['gy'=2,'gx'=64] {'gy','gx'}, dimensions={0} | all-to-all | bytes 917504 | tf_op jit(solution)/shard_map/all_to_all | solution.py:487
  48.2 1.4 %shard_map.42 = (f32[256,256]{1,0:T(8,128)S(1)}, f32[88,128]{1,0:T(8,128)S(1)}, f32[128,256]{1,0:T(8,128)S(1)}, f32[128,256]{1,0:T(8,128)S(1)}, f32[8,256]{1,0:T(8,128)S(1)}) custom-call(f32[896,128]{1,0:T(8,128)S(1)} %bitcast.21, f32[256,256]{1,0:T(8,128)S(1)} %get-tuple-element.50.refs_1_, f32[36,256,256]{2,1,0:T(8,128)S(1)} %get-tuple-element.44.refs_0_.refs_2_), custom_call_target="tpu_custom_call" | custom-call | tf_op jit(solution)/shard_map/pallas_call | solution.py:421
  50.6 1.2 collective-permute-start.5
  51.8 1.1 shard_map.43.refs_6_
  52.9 1.1 collective-permute-done.3.refs_2_
  54.0 1.4 %shard_map.44 = (f32[256,256]{1,0:T(8,128)S(1)}, f32[256,128]{1,0:T(8,128)S(1)}) custom-call(f32[36,256,256]{2,1,0:T(8,128)S(1)} %get-tuple-element.44.refs_0_.refs_2_, f32[256,256]{1,0:T(8,128)S(1)} %get-tuple-element.51.refs_1_.refs_3_.refs_2_, f32[128,256]{1,0:T(8,128)S(1)} %collective-permute-done.3.refs_2_, ...), custom_call_target="tpu_custom_call" | custom-call | tf_op jit(solution)/shard_map/pallas_call | solution.py:292
  55.4 21.0 %all_to_all.26 = f32[128,1,256]{2,1,0:T(1,128)S(1)} all-to-all(f32[128,1,256]{2,1,0:T(1,128)S(1)} %bitcast.26), channel_id=1, replica_groups=mesh['gy'=2,'gx'=64] {'gy','gx'}, dimensions={0} | all-to-all | bytes 262144 | tf_op jit(solution)/shard_map/all_to_all | solution.py:487
  76.4 1.4 shard_map.45
  79.7 1.1 shard_map.46.refs_7_
  80.8 1.5 %collective-permute-done.6.refs_3_ = f32[128,256]{1,0:T(8,128)S(1)} collective-permute-done((f32[128,256]{1,0:T(8,128)S(1)}, f32[128,256]{1,0:T(8,128)S(1)}, u32[]{:S(2)}, u32[]{:S(2)}) %collective-permute-start.6) | collective-permute-done | bytes 131104 | tf_op jit(solution)/shard_map/ppermute | solution.py:478
  82.3 1.4 %shard_map.47 = (f32[256,256]{1,0:T(8,128)S(1)}, f32[256,128]{1,0:T(8,128)S(1)}) custom-call(f32[36,256,256]{2,1,0:T(8,128)S(1)} %get-tuple-element.44.refs_0_.refs_2_, f32[256,256]{1,0:T(8,128)S(1)} %get-tuple-element.51.refs_1_.refs_3_.refs_2_, f32[256,256]{1,0:T(8,128)S(1)} %get-tuple-element.58.refs_2_.refs_4_.refs_3_, ...), custom_call_target="tpu_custom_call" | custom-call | tf_op jit(solution)/shard_map/pallas_call | solution.py:292
  83.8 20.5 %all_to_all.27 = f32[128,1,256]{2,1,0:T(1,128)S(1)} all-to-all(f32[128,1,256]{2,1,0:T(1,128)S(1)} %bitcast.27), channel_id=1, replica_groups=mesh['gy'=2,'gx'=64] {'gy','gx'}, dimensions={0} | all-to-all | bytes 262144 | tf_op jit(solution)/shard_map/all_to_all | solution.py:487
  104.3 1.4 %shard_map.48 = (f32[256,256]{1,0:T(8,128)S(1)}, f32[88,128]{1,0:T(8,128)S(1)}, f32[128,256]{1,0:T(8,128)S(1)}, f32[128,256]{1,0:T(8,128)S(1)}, f32[8,256]{1,0:T(8,128)S(1)}) custom-call(f32[256,128]{1,0:T(8,128)S(1)} %bitcast.24, f32[256,256]{1,0:T(8,128)S(1)} %get-tuple-element.63.refs_1_, f32[36,256,256]{2,1,0:T(8,128)S(1)} %get-tuple-element.44.refs_0_.refs_2_, ...), custom_call_target="tpu_custom_call" | custom-call | tf_op jit(solution)/shard_map/pallas_call | solution.py:421
  107.7 1.1 shard_map.49.refs_8_
  108.8 1.5 %collective-permute-done.9.refs_4_ = f32[128,256]{1,0:T(8,128)S(1)} collective-permute-done((f32[128,256]{1,0:T(8,128)S(1)}, f32[128,256]{1,0:T(8,128)S(1)}, u32[]{:S(2)}, u32[]{:S(2)}) %collective-permute-start.9) | collective-permute-done | bytes 131104 | tf_op jit(solution)/shard_map/ppermute | solution.py:478
  110.3 1.5 %shard_map.50 = (f32[256,256]{1,0:T(8,128)S(1)}, f32[256,128]{1,0:T(8,128)S(1)}) custom-call(f32[36,256,256]{2,1,0:T(8,128)S(1)} %get-tuple-element.44.refs_0_.refs_2_, f32[256,256]{1,0:T(8,128)S(1)} %get-tuple-element.51.refs_1_.refs_3_.refs_2_, f32[256,256]{1,0:T(8,128)S(1)} %get-tuple-element.58.refs_2_.refs_4_.refs_3_, ...), custom_call_target="tpu_custom_call" | custom-call | tf_op jit(solution)/shard_map/pallas_call | solution.py:292
  111.8 20.5 %all_to_all.28 = f32[128,1,256]{2,1,0:T(1,128)S(1)} all-to-all(f32[128,1,256]{2,1,0:T(1,128)S(1)} %bitcast.28), channel_id=1, replica_groups=mesh['gy'=2,'gx'=64] {'gy','gx'}, dimensions={0} | all-to-all | bytes 262144 | tf_op jit(solution)/shard_map/all_to_all | solution.py:487
  132.3 2.1 %shard_map.51 = (f32[256,256]{1,0:T(8,128)S(1)}, f32[88,128]{1,0:T(8,128)S(1)}, f32[1,128]{1,0:T(1,128)S(1)}, f32[1,128]{1,0:T(1,128)S(1)}, s32[1]{0:T(128)}) custom-call(f32[256,128]{1,0:T(8,128)S(1)} %bitcast.22, f32[256,256]{1,0:T(8,128)S(1)} %get-tuple-element.70.refs_1_, f32[36,256,256]{2,1,0:T(8,128)S(1)} %get-tuple-element.44.refs_0_.refs_2_, ...), custom_call_target="tpu_custom_call" | custom-call | tf_op jit(solution)/shard_map/pallas_call | solution.py:421
  135.1 1.1 finish.1
  (21 shorter events, 5.7 us)
Async XLA Ops:
  0.6 21.3 %copy-start = (f32[4,64,256]{2,1,0:T(8,128)S(1)}, f32[4,64,256]{2,1,0:T(8,128)}, u32[]{:S(2)}) copy-start(f32[4,64,256]{2,1,0:T(8,128)} %param.5) | copy-start | bytes 786436
  1.7 20.2 %collective-permute-start = (f32[128,256]{1,0:T(8,128)S(1)}, f32[128,256]{1,0:T(8,128)S(1)}, u32[]{:S(2)}, u32[]{:S(2)}) collective-permute-start(f32[128,256]{1,0:T(8,128)S(1)} %get-tuple-element.45), channel_id=1, source_target_pairs={{0,1},{2,3},{4,5},{6,7},{8,9},{10,11},{12,13},{14,15},{16,17},{18,... | collective-permute-start | bytes 393224 | tf_op jit(solution)/shard_map/ppermute | solution.py:478
  3.8 18.1 %collective-permute-start.1 = (f32[128,256]{1,0:T(8,128)S(1)}, f32[128,256]{1,0:T(8,128)S(1)}, u32[]{:S(2)}, u32[]{:S(2)}) collective-permute-start(f32[128,256]{1,0:T(8,128)S(1)} %get-tuple-element.46), channel_id=1, source_target_pairs={{1,2},{3,4},{5,6},{7,8},{9,10},{11,12},{13,14},{15,16},{17,18},{19... | collective-permute-start | bytes 393224 | tf_op jit(solution)/shard_map/ppermute | solution.py:477
  4.5 17.4 %collective-permute-start.2 = (f32[8,256]{1,0:T(8,128)S(1)}, f32[8,256]{1,0:T(8,128)S(1)}, u32[]{:S(2)}, u32[]{:S(2)}) collective-permute-start(f32[8,256]{1,0:T(8,128)S(1)} %get-tuple-element.47), channel_id=1, source_target_pairs={{0,64},{64,0},{1,65},{65,1},{2,66},{66,2},{3,67},{67,3},{4,68},{68... | collective-permute-start | bytes 24584 | tf_op jit(solution)/shard_map/ppermute | solution.py:479
  49.6 4.4 %collective-permute-start.3 = (f32[128,256]{1,0:T(8,128)S(1)}, f32[128,256]{1,0:T(8,128)S(1)}, u32[]{:S(2)}, u32[]{:S(2)}) collective-permute-start(f32[128,256]{1,0:T(8,128)S(1)} %get-tuple-element.52), channel_id=1, source_target_pairs={{0,1},{2,3},{4,5},{6,7},{8,9},{10,11},{12,13},{14,15},{16,17},{18,... | collective-permute-start | bytes 393224 | tf_op jit(solution)/shard_map/ppermute | solution.py:478
  50.0 4.0 %collective-permute-start.4 = (f32[128,256]{1,0:T(8,128)S(1)}, f32[128,256]{1,0:T(8,128)S(1)}, u32[]{:S(2)}, u32[]{:S(2)}) collective-permute-start(f32[128,256]{1,0:T(8,128)S(1)} %get-tuple-element.53), channel_id=1, source_target_pairs={{1,2},{3,4},{5,6},{7,8},{9,10},{11,12},{13,14},{15,16},{17,18},{19... | collective-permute-start | bytes 393224 | tf_op jit(solution)/shard_map/ppermute | solution.py:477
  50.6 2.3 %collective-permute-start.5 = (f32[8,256]{1,0:T(8,128)S(1)}, f32[8,256]{1,0:T(8,128)S(1)}, u32[]{:S(2)}, u32[]{:S(2)}) collective-permute-start(f32[8,256]{1,0:T(8,128)S(1)} %get-tuple-element.54), channel_id=1, source_target_pairs={{0,64},{64,0},{1,65},{65,1},{2,66},{66,2},{3,67},{67,3},{4,68},{68... | collective-permute-start | bytes 24584 | tf_op jit(solution)/shard_map/ppermute | solution.py:479
  77.7 4.6 %collective-permute-start.6 = (f32[128,256]{1,0:T(8,128)S(1)}, f32[128,256]{1,0:T(8,128)S(1)}, u32[]{:S(2)}, u32[]{:S(2)}) collective-permute-start(f32[128,256]{1,0:T(8,128)S(1)} %get-tuple-element.59), channel_id=1, source_target_pairs={{0,1},{2,3},{4,5},{6,7},{8,9},{10,11},{12,13},{14,15},{16,17},{18,... | collective-permute-start | bytes 393224 | tf_op jit(solution)/shard_map/ppermute | solution.py:478
  78.1 4.2 %collective-permute-start.7 = (f32[128,256]{1,0:T(8,128)S(1)}, f32[128,256]{1,0:T(8,128)S(1)}, u32[]{:S(2)}, u32[]{:S(2)}) collective-permute-start(f32[128,256]{1,0:T(8,128)S(1)} %get-tuple-element.60), channel_id=1, source_target_pairs={{1,2},{3,4},{5,6},{7,8},{9,10},{11,12},{13,14},{15,16},{17,18},{19... | collective-permute-start | bytes 393224 | tf_op jit(solution)/shard_map/ppermute | solution.py:477
  78.8 2.0 %collective-permute-start.8 = (f32[8,256]{1,0:T(8,128)S(1)}, f32[8,256]{1,0:T(8,128)S(1)}, u32[]{:S(2)}, u32[]{:S(2)}) collective-permute-start(f32[8,256]{1,0:T(8,128)S(1)} %get-tuple-element.61), channel_id=1, source_target_pairs={{0,64},{64,0},{1,65},{65,1},{2,66},{66,2},{3,67},{67,3},{4,68},{68... | collective-permute-start | bytes 24584 | tf_op jit(solution)/shard_map/ppermute | solution.py:479
  105.7 4.6 %collective-permute-start.9 = (f32[128,256]{1,0:T(8,128)S(1)}, f32[128,256]{1,0:T(8,128)S(1)}, u32[]{:S(2)}, u32[]{:S(2)}) collective-permute-start(f32[128,256]{1,0:T(8,128)S(1)} %get-tuple-element.66), channel_id=1, source_target_pairs={{0,1},{2,3},{4,5},{6,7},{8,9},{10,11},{12,13},{14,15},{16,17},{18,... | collective-permute-start | bytes 393224 | tf_op jit(solution)/shard_map/ppermute | solution.py:478
  106.1 4.2 %collective-permute-start.10 = (f32[128,256]{1,0:T(8,128)S(1)}, f32[128,256]{1,0:T(8,128)S(1)}, u32[]{:S(2)}, u32[]{:S(2)}) collective-permute-start(f32[128,256]{1,0:T(8,128)S(1)} %get-tuple-element.67), channel_id=1, source_target_pairs={{1,2},{3,4},{5,6},{7,8},{9,10},{11,12},{13,14},{15,16},{17,18},{19... | collective-permute-start | bytes 393224 | tf_op jit(solution)/shard_map/ppermute | solution.py:477
  106.8 2.1 %collective-permute-start.11 = (f32[8,256]{1,0:T(8,128)S(1)}, f32[8,256]{1,0:T(8,128)S(1)}, u32[]{:S(2)}, u32[]{:S(2)}) collective-permute-start(f32[8,256]{1,0:T(8,128)S(1)} %get-tuple-element.68), channel_id=1, source_target_pairs={{0,64},{64,0},{1,65},{65,1},{2,66},{66,2},{3,67},{67,3},{4,68},{68... | collective-permute-start | bytes 24584 | tf_op jit(solution)/shard_map/ppermute | solution.py:479

commit v4 on v3

--- a/solution.py
+++ b/solution.py
@@ -52,51 +52,106 @@
     return jnp.sum(acc[:, :128] + acc[:, 128:], axis=0, keepdims=True)
 
 
-def gram_kernel(v_hbm, v_ref, out_ref, sums_ref, matrix_ref, sems):
-    groups = KEEP // GROUP
-    copies = [
-        pltpu.make_async_copy(
-            v_hbm.at[pl.ds(g * GROUP, GROUP)], v_ref.at[pl.ds(g * GROUP, GROUP)], sems.at[g]
-        )
-        for g in range(groups)
-    ]
-    for c in copies:
-        c.start()
-
-    def block(ga, gb):
-        pairs = [(a, b) for a in range(GROUP) for b in range(GROUP) if ga != gb or a <= b]
-
-        def step(t, accs):
-            accs = list(accs)
-            for part in range(GRAM_ROWS // 8):
-                rows = pl.ds(pl.multiple_of(t * GRAM_ROWS, GRAM_ROWS) + 8 * part, 8)
-                for half in range(2):
-                    lanes = pl.ds(half * 128, 128)
-                    left = [v_ref[ga * GROUP + a, rows, lanes] for a in range(GROUP)]
-                    right = left
-                    if ga != gb:
-                        right = [v_ref[gb * GROUP + b, rows, lanes] for b in range(GROUP)]
-                    for n, (a, b) in enumerate(pairs):
-                        accs[n] = accs[n] + left[a] * right[b]
-            return tuple(accs)
-
-        zero = jnp.zeros((8, 128), F32)
-        accs = lax.fori_loop(0, ROWS // GRAM_ROWS, step, tuple(zero for _ in pairs))
-        for (a, b), acc in zip(pairs, accs):
-            row = jnp.sum(acc, axis=0, keepdims=True)
-            i, j = ga * GROUP + a, gb * GROUP + b
-            sums_ref[i, pl.ds(j, 1), :] = row
-            if i != j:
-                sums_ref[j, pl.ds(i, 1), :] = row
-
-    for gb in range(groups):
-        copies[gb].wait()
-        for ga in range(gb + 1):
-            block(ga, gb)
+def gram_block(v_ref, sums_ref, ga, gb):
+    pairs = [(a, b) for a in range(GROUP) for b in range(GROUP) if ga != gb or a <= b]
+
+    def step(t, accs):
+        accs = list(accs)
+        for part in range(GRAM_ROWS // 8):
+            rows = pl.ds(pl.multiple_of(t * GRAM_ROWS, GRAM_ROWS) + 8 * part, 8)
+            for half in range(2):
+                lanes = pl.ds(half * 128, 128)
+                left = [v_ref[ga * GROUP + a, rows, lanes] for a in range(GROUP)]
+                right = left
+                if ga != gb:
+                    right = [v_ref[gb * GROUP + b, rows, lanes] for b in range(GROUP)]
+                for n, (a, b) in enumerate(pairs):
+                    accs[n] = accs[n] + left[a] * right[b]
+        return tuple(accs)
+
+    zero = jnp.zeros((8, 128), F32)
+    accs = lax.fori_loop(0, ROWS // GRAM_ROWS, step, tuple(zero for _ in pairs))
+    for (a, b), acc in zip(pairs, accs):
+        row = jnp.sum(acc, axis=0, keepdims=True)
+        i, j = ga * GROUP + a, gb * GROUP + b
+        sums_ref[i, pl.ds(j, 1), :] = row
+        if i != j:
+            sums_ref[j, pl.ds(i, 1), :] = row
+
+
+def write_edges(u_ref, first_ref, second_ref, swap_ref):
+    odd = lax.axis_index("gx") % 2 == 1
+    upper = lax.axis_index("gy") == 1
+    for x in range(2):
+        low = u_ref[pl.ds(x * YS, YS), :]
+        high = u_ref[pl.ds((XS - 2 + x) * YS, YS), :]
+        first_ref[pl.ds(x * YS, YS), :] = jnp.where(odd, low, high)
+        second_ref[pl.ds(x * YS, YS), :] = jnp.where(odd, high, low)
+    for x in range(XS):
+        low = u_ref[pl.ds(x * YS, 2), :]
+        high = u_ref[pl.ds(x * YS + YS - 2, 2), :]
+        swap_ref[pl.ds(2 * x, 2), :] = jnp.where(upper, low, high)
+
+
+EDGE_SHAPES = (
+    jax.ShapeDtypeStruct((2 * YS, ZS), F32),
+    jax.ShapeDtypeStruct((2 * YS, ZS), F32),
+    jax.ShapeDtypeStruct((2 * XS, ZS), F32),
+)
+
+
+ARRIVAL = [KEEP // GROUP - 1, *range(KEEP // GROUP - 1)]
+EARLY = 4
+LATE_PAIRS = [
+    (ARRIVAL[m], ARRIVAL[n]) for n in range(EARLY, len(ARRIVAL)) for m in range(n + 1)
+]
+
+
+def start_kernel(v_hbm, v_ref, first_ref, second_ref, swap_ref, sums_ref, sems):
+    copies = {}
+    for g in ARRIVAL:
+        part = pl.ds(g * GROUP, GROUP)
+        copies[g] = pltpu.make_async_copy(v_hbm.at[part], v_ref.at[part], sems.at[g])
+        copies[g].start()
+    for n, g in enumerate(ARRIVAL[:EARLY]):
+        copies[g].wait()
+        if n == 0:
+            write_edges(v_ref.at[KEEP - 1], first_ref, second_ref, swap_ref)
+        for m in range(n + 1):
+            gram_block(v_ref, sums_ref, ARRIVAL[m], g)
+    for g in ARRIVAL[EARLY:]:
+        copies[g].wait()
+
+
+def start_call(basis):
+    return pl.pallas_call(
+        start_kernel,
+        in_specs=[pl.BlockSpec(memory_space=pltpu.HBM)],
+        out_specs=(VMEM_SPEC,) * 5,
+        out_shape=(
+            pltpu.VMEM((KEEP, ROWS, ZS), F32),
+            *EDGE_SHAPES,
+            pltpu.VMEM((KEEP, KEEP, 128), F32),
+        ),
+        scratch_shapes=[pltpu.SemaphoreType.DMA((KEEP // GROUP,))],
+        compiler_params=PARAMS,
+        name="start",
+    )(pltpu.with_memory_space_constraint(basis, pltpu.HBM))
+
+
+def gram_kernel(v_ref, early_ref, out_ref, sums_ref, matrix_ref):
+    for ga, gb in LATE_PAIRS:
+        gram_block(v_ref, sums_ref, ga, gb)
+    early = sorted(g * GROUP + a for g in ARRIVAL[:EARLY] for a in range(GROUP))
+    sub = iota((KEEP, 128), 0)
+    in_early = (sub < (EARLY - 1) * GROUP) | (sub >= KEEP - GROUP)
     lane = iota((KEEP, 128), 1)
     matrix = jnp.zeros((KEEP, 128), F32)
     for i in range(KEEP):
-        column = jnp.sum(sums_ref[i], axis=1, keepdims=True)
+        part = sums_ref[i]
+        if i in early:
+            part = jnp.where(in_early, early_ref[i], part)
+        column = jnp.sum(part, axis=1, keepdims=True)
         matrix = jnp.where(lane == i, column, matrix)
     matrix_ref[pl.ds(0, KEEP), :] = matrix
     top = matrix_ref[pl.ds(0, HALF), :]
@@ -114,23 +169,16 @@
         out_ref[:, pl.ds(r * 128, 128)] = packed[r : r + 1]
 
 
-def gram_call(basis):
+def gram_call(v, early):
     return pl.pallas_call(
         gram_kernel,
-        in_specs=[pl.BlockSpec(memory_space=pltpu.HBM)],
-        out_specs=(VMEM_SPEC, VMEM_SPEC),
-        out_shape=(
-            pltpu.VMEM((KEEP, ROWS, ZS), F32),
-            jax.ShapeDtypeStruct((1, PACK * 128), F32),
-        ),
-        scratch_shapes=[
-            pltpu.VMEM((KEEP, KEEP, 128), F32),
-            pltpu.VMEM((BASIS, 128), F32),
-            pltpu.SemaphoreType.DMA((KEEP // GROUP,)),
-        ],
+        in_specs=[VMEM_SPEC, VMEM_SPEC],
+        out_specs=VMEM_SPEC,
+        out_shape=jax.ShapeDtypeStruct((1, PACK * 128), F32),
+        scratch_shapes=[pltpu.VMEM((KEEP, KEEP, 128), F32), pltpu.VMEM((BASIS, 128), F32)],
         compiler_params=PARAMS,
         name="gram",
-    )(pltpu.with_memory_space_constraint(basis, pltpu.HBM))
+    )(v, early)
 
 
 def dot_all(v_ref, others, x_ref, dots_ref):
@@ -173,51 +221,11 @@
     )(v, *created)
 
 
-def write_edges(u_ref, first_ref, second_ref, swap_ref):
-    odd = lax.axis_index("gx") % 2 == 1
-    upper = lax.axis_index("gy") == 1
-    for x in range(2):
-        low = u_ref[pl.ds(x * YS, YS), :]
-        high = u_ref[pl.ds((XS - 2 + x) * YS, YS), :]
-        first_ref[pl.ds(x * YS, YS), :] = jnp.where(odd, low, high)
-        second_ref[pl.ds(x * YS, YS), :] = jnp.where(odd, high, low)
-    for x in range(XS):
-        low = u_ref[pl.ds(x * YS, 2), :]
-        high = u_ref[pl.ds(x * YS + YS - 2, 2), :]
-        swap_ref[pl.ds(2 * x, 2), :] = jnp.where(upper, low, high)
-
-
-EDGE_SHAPES = (
-    jax.ShapeDtypeStruct((2 * YS, ZS), F32),
-    jax.ShapeDtypeStruct((2 * YS, ZS), F32),
-    jax.ShapeDtypeStruct((2 * XS, ZS), F32),
-)
-
-
 LAST_SHAPES = (
     jax.ShapeDtypeStruct((1, 128), F32),
     jax.ShapeDtypeStruct((1, 128), F32),
     jax.ShapeDtypeStruct((1,), jnp.int32),
 )
-
-
-def edges_kernel(v_hbm, first_ref, second_ref, swap_ref, u_ref, sem):
-    copy = pltpu.make_async_copy(v_hbm.at[KEEP - 1], u_ref, sem)
-    copy.start()
-    copy.wait()
-    write_edges(u_ref, first_ref, second_ref, swap_ref)
-
-
-def edges_call(basis):
-    return pl.pallas_call(
-        edges_kernel,
-        in_specs=[pl.BlockSpec(memory_space=pltpu.HBM)],
-        out_specs=(VMEM_SPEC,) * 3,
-        out_shape=EDGE_SHAPES,
-        scratch_shapes=[pltpu.VMEM((ROWS, ZS), F32), pltpu.SemaphoreType.DMA],
-        compiler_params=PARAMS,
-        name="edges",
-    )(pltpu.with_memory_space_constraint(basis, pltpu.HBM))
 
 
 def write_for_all(out_ref, rows):
@@ -492,9 +500,10 @@
     devices = lax.axis_size(("gy", "gx"))
     cells = float(ROWS * ZS * devices)
     basis = basis_vectors.reshape(KEEP, ROWS, ZS)
-    halo = exchange(*edges_call(basis))
+    v, *edges, early = start_call(basis)
+    halo = exchange(*edges)
     reaction = reaction.reshape(ROWS, ZS)
-    v, extra = gram_call(basis)
+    extra = gram_call(v, early)
     created = []
     state = None
     for j in range(STEPS):

time: 137 us -> 135 us (0.985)
  transfers between devices with their start and end apart: 12 -> 12, of which waited for: 3 -> 3; matrix products, arithmetic and copies ran while one was open for 0% -> 0% of each run, Pallas kernels for 14% -> 11%
where the time goes in v4:
time: 135 us
  blocking collectives  87 us (64%)
  Pallas kernels  32.8 us (24%)
  starting transfers between devices  9.92 us (7%)
  waiting for transfers between devices  4.07 us (3%)
  between operations  1.42 us (1%)
    all_to_all x4, blocking collectives, from_all(): got = lax.all_to_all(copies, axes, split_axis=0, concat_axis=0, tiled=True)  87 us
    pallas_call x1, Pallas kernels, gram_call(): pl.pallas_call(gram_kernel, in_specs=[VMEM_SPEC, VMEM_SPEC], out_specs=VM...  12 us
    pallas_call x4, Pallas kernels, combine_call(): pl.pallas_call(functools.partial(combine_kernel, count, cells), in_specs=...  6.26 us
    pallas_call x4, Pallas kernels, image_call(): pl.pallas_call(functools.partial(image_kernel, count), in_specs=[VMEM_SPE...  5.69 us
    pallas_call x1, Pallas kernels, start_call(): pl.pallas_call(start_kernel, in_specs=[pl.BlockSpec(memory_space=pltpu.HB...  4.42 us
    ppermute x4, starting transfers between devices, exchange(): swap = lax.ppermute(swap, 'gy', [(0, 1), (1, 0)])  4.09 us
    ppermute x4, waiting for transfers between devices, exchange(): first = lax.ppermute(first, 'gx', pairs(0))  4.05 us
    pallas_call x3, Pallas kernels, self_dots_call(): pl.pallas_call(functools.partial(self_dots_kernel, count), in_specs=[VMEM...  3.3 us
  transfers between devices with their start and end apart: 12, of which 3 were waited for; matrix products, arithmetic and copies ran while one was open for 0% of the time, Pallas kernels for 11%

profile of v4, /device:TPU:1, one launch (start us, length us, event | category | flops | bytes accessed | tf_op | source)
XLA Modules:
  0.0 135.2 jit_solution(6396925223216608369)
XLA Ops:
  0.6 4.4 %start.1 = (f32[36,256,256]{2,1,0:T(8,128)S(1)}, f32[128,256]{1,0:T(8,128)S(1)}, f32[128,256]{1,0:T(8,128)S(1)}, f32[8,256]{1,0:T(8,128)S(1)}, f32[36,36,128]{2,1,0:T(8,128)S(1)}) custom-call(f32[36,256,256]{2,1,0:T(8,128)} %bitcast.29), custom_call_target="tpu_custom_call" | custom-call | tf_op jit(solution)/shard_map/start/pallas_call | solution.py:127
  5.1 2.1 %collective-permute-start = (f32[128,256]{1,0:T(8,128)S(1)}, f32[128,256]{1,0:T(8,128)S(1)}, u32[]{:S(2)}, u32[]{:S(2)}) collective-permute-start(f32[128,256]{1,0:T(8,128)S(1)} %get-tuple-element.45), channel_id=1, source_target_pairs={{0,1},{2,3},{4,5},{6,7},{8,9},{10,11},{12,13},{14,15},{16,17},{18,... | collective-permute-start | bytes 393224 | tf_op jit(solution)/shard_map/ppermute | solution.py:486
  7.8 1.0 collective-permute-start.2
  8.9 12.0 %gram.1.refs_5_ = f32[1,768]{1,0:T(1,128)S(1)} custom-call(f32[36,256,256]{2,1,0:T(8,128)S(1)} %get-tuple-element.44.v_ref.refs_0_.refs_2_, f32[36,36,128]{2,1,0:T(8,128)S(1)} %get-tuple-element.48.early_ref), custom_call_target="tpu_custom_call" | custom-call | tf_op jit(solution)/shard_map/gram/pallas_call | solution.py:173
  20.9 1.4 %shard_map.41 = (f32[256,256]{1,0:T(8,128)S(1)}, f32[896,128]{1,0:T(8,128)S(1)}) custom-call(f32[36,256,256]{2,1,0:T(8,128)S(1)} %get-tuple-element.44.v_ref.refs_0_.refs_2_, f32[128,256]{1,0:T(8,128)S(1)} %collective-permute-done.refs_1_, f32[128,256]{1,0:T(8,128)S(1)} %collective-permute-done.1.refs_2_, f32[8,256]{1,0:T(8,128)S(1)} %collective-permute-done.2.refs_3_, ...), custom_call_target="tpu_custom_call" | custom-call | tf_op jit(solution)/shard_map/pallas_call | solution.py:300
  22.3 24.9 %all_to_all.25 = f32[128,1,896]{2,1,0:T(1,128)S(1)} all-to-all(f32[128,1,896]{2,1,0:T(1,128)S(1)} %bitcast.25), channel_id=1, replica_groups=mesh['gy'=2,'gx'=64] {'gy','gx'}, dimensions={0} | all-to-all | bytes 917504 | tf_op jit(solution)/shard_map/all_to_all | solution.py:495
  47.2 1.4 %shard_map.42 = (f32[256,256]{1,0:T(8,128)S(1)}, f32[88,128]{1,0:T(8,128)S(1)}, f32[128,256]{1,0:T(8,128)S(1)}, f32[128,256]{1,0:T(8,128)S(1)}, f32[8,256]{1,0:T(8,128)S(1)}) custom-call(f32[896,128]{1,0:T(8,128)S(1)} %bitcast.21, f32[256,256]{1,0:T(8,128)S(1)} %get-tuple-element.50.refs_1_, f32[36,256,256]{2,1,0:T(8,128)S(1)} %get-tuple-element.44.v_ref.refs_0_.refs_2_), custom_call_target="tpu_custom_call" | custom-call | tf_op jit(solution)/shard_map/pallas_call | solution.py:429
  49.6 1.2 collective-permute-start.5
  50.8 1.1 shard_map.43.refs_6_
  51.9 1.1 collective-permute-done.3.refs_2_
  53.0 1.4 %shard_map.44 = (f32[256,256]{1,0:T(8,128)S(1)}, f32[256,128]{1,0:T(8,128)S(1)}) custom-call(f32[36,256,256]{2,1,0:T(8,128)S(1)} %get-tuple-element.44.v_ref.refs_0_.refs_2_, f32[256,256]{1,0:T(8,128)S(1)} %get-tuple-element.51.refs_1_.refs_3_.refs_2_, f32[128,256]{1,0:T(8,128)S(1)} %collective-permute-done.3.refs_2_, ...), custom_call_target="tpu_custom_call" | custom-call | tf_op jit(solution)/shard_map/pallas_call | solution.py:300
  54.4 21.0 %all_to_all.26 = f32[128,1,256]{2,1,0:T(1,128)S(1)} all-to-all(f32[128,1,256]{2,1,0:T(1,128)S(1)} %bitcast.26), channel_id=1, replica_groups=mesh['gy'=2,'gx'=64] {'gy','gx'}, dimensions={0} | all-to-all | bytes 262144 | tf_op jit(solution)/shard_map/all_to_all | solution.py:495
  75.4 1.4 %shard_map.45 = (f32[256,256]{1,0:T(8,128)S(1)}, f32[88,128]{1,0:T(8,128)S(1)}, f32[128,256]{1,0:T(8,128)S(1)}, f32[128,256]{1,0:T(8,128)S(1)}, f32[8,256]{1,0:T(8,128)S(1)}) custom-call(f32[256,128]{1,0:T(8,128)S(1)} %bitcast.23, f32[256,256]{1,0:T(8,128)S(1)} %get-tuple-element.56.refs_1_, f32[36,256,256]{2,1,0:T(8,128)S(1)} %get-tuple-element.44.v_ref.refs_0_.refs_2_, ...), custom_call_target="tpu_custom_call" | custom-call | tf_op jit(solution)/shard_map/pallas_call | solution.py:429
  78.7 1.1 shard_map.46.refs_7_
  79.8 1.5 %collective-permute-done.6.refs_3_ = f32[128,256]{1,0:T(8,128)S(1)} collective-permute-done((f32[128,256]{1,0:T(8,128)S(1)}, f32[128,256]{1,0:T(8,128)S(1)}, u32[]{:S(2)}, u32[]{:S(2)}) %collective-permute-start.6) | collective-permute-done | bytes 131104 | tf_op jit(solution)/shard_map/ppermute | solution.py:486
  81.3 1.4 %shard_map.47 = (f32[256,256]{1,0:T(8,128)S(1)}, f32[256,128]{1,0:T(8,128)S(1)}) custom-call(f32[36,256,256]{2,1,0:T(8,128)S(1)} %get-tuple-element.44.v_ref.refs_0_.refs_2_, f32[256,256]{1,0:T(8,128)S(1)} %get-tuple-element.51.refs_1_.refs_3_.refs_2_, f32[256,256]{1,0:T(8,128)S(1)} %get-tuple-element.58.refs_2_.refs_4_.refs_3_, ...), custom_call_target="tpu_custom_call" | custom-call | tf_op jit(solution)/shard_map/pallas_call | solution.py:300
  82.8 20.5 %all_to_all.27 = f32[128,1,256]{2,1,0:T(1,128)S(1)} all-to-all(f32[128,1,256]{2,1,0:T(1,128)S(1)} %bitcast.27), channel_id=1, replica_groups=mesh['gy'=2,'gx'=64] {'gy','gx'}, dimensions={0} | all-to-all | bytes 262144 | tf_op jit(solution)/shard_map/all_to_all | solution.py:495
  103.3 1.4 %shard_map.48 = (f32[256,256]{1,0:T(8,128)S(1)}, f32[88,128]{1,0:T(8,128)S(1)}, f32[128,256]{1,0:T(8,128)S(1)}, f32[128,256]{1,0:T(8,128)S(1)}, f32[8,256]{1,0:T(8,128)S(1)}) custom-call(f32[256,128]{1,0:T(8,128)S(1)} %bitcast.24, f32[256,256]{1,0:T(8,128)S(1)} %get-tuple-element.63.refs_1_, f32[36,256,256]{2,1,0:T(8,128)S(1)} %get-tuple-element.44.v_ref.refs_0_.refs_2_, ...), custom_call_target="tpu_custom_call" | custom-call | tf_op jit(solution)/shard_map/pallas_call | solution.py:429
  106.7 1.1 shard_map.49.refs_8_
  107.8 1.5 %collective-permute-done.9.refs_4_ = f32[128,256]{1,0:T(8,128)S(1)} collective-permute-done((f32[128,256]{1,0:T(8,128)S(1)}, f32[128,256]{1,0:T(8,128)S(1)}, u32[]{:S(2)}, u32[]{:S(2)}) %collective-permute-start.9) | collective-permute-done | bytes 131104 | tf_op jit(solution)/shard_map/ppermute | solution.py:486
  109.3 1.5 %shard_map.50 = (f32[256,256]{1,0:T(8,128)S(1)}, f32[256,128]{1,0:T(8,128)S(1)}) custom-call(f32[36,256,256]{2,1,0:T(8,128)S(1)} %get-tuple-element.44.v_ref.refs_0_.refs_2_, f32[256,256]{1,0:T(8,128)S(1)} %get-tuple-element.51.refs_1_.refs_3_.refs_2_, f32[256,256]{1,0:T(8,128)S(1)} %get-tuple-element.58.refs_2_.refs_4_.refs_3_, ...), custom_call_target="tpu_custom_call" | custom-call | tf_op jit(solution)/shard_map/pallas_call | solution.py:300
  110.8 20.5 %all_to_all.28 = f32[128,1,256]{2,1,0:T(1,128)S(1)} all-to-all(f32[128,1,256]{2,1,0:T(1,128)S(1)} %bitcast.28), channel_id=1, replica_groups=mesh['gy'=2,'gx'=64] {'gy','gx'}, dimensions={0} | all-to-all | bytes 262144 | tf_op jit(solution)/shard_map/all_to_all | solution.py:495
  131.3 2.1 %shard_map.51 = (f32[256,256]{1,0:T(8,128)S(1)}, f32[88,128]{1,0:T(8,128)S(1)}, f32[1,128]{1,0:T(1,128)S(1)}, f32[1,128]{1,0:T(1,128)S(1)}, s32[1]{0:T(128)}) custom-call(f32[256,128]{1,0:T(8,128)S(1)} %bitcast.22, f32[256,256]{1,0:T(8,128)S(1)} %get-tuple-element.70.refs_1_, f32[36,256,256]{2,1,0:T(8,128)S(1)} %get-tuple-element.44.v_ref.refs_0_.refs_2_, ...), custom_call_target="tpu_custom_call" | custom-call | tf_op jit(solution)/shard_map/pallas_call | solution.py:429
  134.1 1.1 finish.1
  (21 shorter events, 5.7 us)
Async XLA Ops:
  0.6 20.3 %copy-start = (f32[4,64,256]{2,1,0:T(8,128)S(1)}, f32[4,64,256]{2,1,0:T(8,128)}, u32[]{:S(2)}) copy-start(f32[4,64,256]{2,1,0:T(8,128)} %param.5) | copy-start | bytes 786436
  5.1 15.8 %collective-permute-start = (f32[128,256]{1,0:T(8,128)S(1)}, f32[128,256]{1,0:T(8,128)S(1)}, u32[]{:S(2)}, u32[]{:S(2)}) collective-permute-start(f32[128,256]{1,0:T(8,128)S(1)} %get-tuple-element.45), channel_id=1, source_target_pairs={{0,1},{2,3},{4,5},{6,7},{8,9},{10,11},{12,13},{14,15},{16,17},{18,... | collective-permute-start | bytes 393224 | tf_op jit(solution)/shard_map/ppermute | solution.py:486
  7.2 13.7 %collective-permute-start.1 = (f32[128,256]{1,0:T(8,128)S(1)}, f32[128,256]{1,0:T(8,128)S(1)}, u32[]{:S(2)}, u32[]{:S(2)}) collective-permute-start(f32[128,256]{1,0:T(8,128)S(1)} %get-tuple-element.46), channel_id=1, source_target_pairs={{1,2},{3,4},{5,6},{7,8},{9,10},{11,12},{13,14},{15,16},{17,18},{19... | collective-permute-start | bytes 393224 | tf_op jit(solution)/shard_map/ppermute | solution.py:485
  7.8 13.0 %collective-permute-start.2 = (f32[8,256]{1,0:T(8,128)S(1)}, f32[8,256]{1,0:T(8,128)S(1)}, u32[]{:S(2)}, u32[]{:S(2)}) collective-permute-start(f32[8,256]{1,0:T(8,128)S(1)} %get-tuple-element.47), channel_id=1, source_target_pairs={{0,64},{64,0},{1,65},{65,1},{2,66},{66,2},{3,67},{67,3},{4,68},{68... | collective-permute-start | bytes 24584 | tf_op jit(solution)/shard_map/ppermute | solution.py:487
  48.6 4.4 %collective-permute-start.3 = (f32[128,256]{1,0:T(8,128)S(1)}, f32[128,256]{1,0:T(8,128)S(1)}, u32[]{:S(2)}, u32[]{:S(2)}) collective-permute-start(f32[128,256]{1,0:T(8,128)S(1)} %get-tuple-element.52), channel_id=1, source_target_pairs={{0,1},{2,3},{4,5},{6,7},{8,9},{10,11},{12,13},{14,15},{16,17},{18,... | collective-permute-start | bytes 393224 | tf_op jit(solution)/shard_map/ppermute | solution.py:486
  49.0 4.0 %collective-permute-start.4 = (f32[128,256]{1,0:T(8,128)S(1)}, f32[128,256]{1,0:T(8,128)S(1)}, u32[]{:S(2)}, u32[]{:S(2)}) collective-permute-start(f32[128,256]{1,0:T(8,128)S(1)} %get-tuple-element.53), channel_id=1, source_target_pairs={{1,2},{3,4},{5,6},{7,8},{9,10},{11,12},{13,14},{15,16},{17,18},{19... | collective-permute-start | bytes 393224 | tf_op jit(solution)/shard_map/ppermute | solution.py:485
  49.6 2.3 %collective-permute-start.5 = (f32[8,256]{1,0:T(8,128)S(1)}, f32[8,256]{1,0:T(8,128)S(1)}, u32[]{:S(2)}, u32[]{:S(2)}) collective-permute-start(f32[8,256]{1,0:T(8,128)S(1)} %get-tuple-element.54), channel_id=1, source_target_pairs={{0,64},{64,0},{1,65},{65,1},{2,66},{66,2},{3,67},{67,3},{4,68},{68... | collective-permute-start | bytes 24584 | tf_op jit(solution)/shard_map/ppermute | solution.py:487
  76.7 4.6 %collective-permute-start.6 = (f32[128,256]{1,0:T(8,128)S(1)}, f32[128,256]{1,0:T(8,128)S(1)}, u32[]{:S(2)}, u32[]{:S(2)}) collective-permute-start(f32[128,256]{1,0:T(8,128)S(1)} %get-tuple-element.59), channel_id=1, source_target_pairs={{0,1},{2,3},{4,5},{6,7},{8,9},{10,11},{12,13},{14,15},{16,17},{18,... | collective-permute-start | bytes 393224 | tf_op jit(solution)/shard_map/ppermute | solution.py:486
  77.1 4.2 %collective-permute-start.7 = (f32[128,256]{1,0:T(8,128)S(1)}, f32[128,256]{1,0:T(8,128)S(1)}, u32[]{:S(2)}, u32[]{:S(2)}) collective-permute-start(f32[128,256]{1,0:T(8,128)S(1)} %get-tuple-element.60), channel_id=1, source_target_pairs={{1,2},{3,4},{5,6},{7,8},{9,10},{11,12},{13,14},{15,16},{17,18},{19... | collective-permute-start | bytes 393224 | tf_op jit(solution)/shard_map/ppermute | solution.py:485
  77.8 2.0 %collective-permute-start.8 = (f32[8,256]{1,0:T(8,128)S(1)}, f32[8,256]{1,0:T(8,128)S(1)}, u32[]{:S(2)}, u32[]{:S(2)}) collective-permute-start(f32[8,256]{1,0:T(8,128)S(1)} %get-tuple-element.61), channel_id=1, source_target_pairs={{0,64},{64,0},{1,65},{65,1},{2,66},{66,2},{3,67},{67,3},{4,68},{68... | collective-permute-start | bytes 24584 | tf_op jit(solution)/shard_map/ppermute | solution.py:487
  104.7 4.6 %collective-permute-start.9 = (f32[128,256]{1,0:T(8,128)S(1)}, f32[128,256]{1,0:T(8,128)S(1)}, u32[]{:S(2)}, u32[]{:S(2)}) collective-permute-start(f32[128,256]{1,0:T(8,128)S(1)} %get-tuple-element.66), channel_id=1, source_target_pairs={{0,1},{2,3},{4,5},{6,7},{8,9},{10,11},{12,13},{14,15},{16,17},{18,... | collective-permute-start | bytes 393224 | tf_op jit(solution)/shard_map/ppermute | solution.py:486
  105.1 4.2 %collective-permute-start.10 = (f32[128,256]{1,0:T(8,128)S(1)}, f32[128,256]{1,0:T(8,128)S(1)}, u32[]{:S(2)}, u32[]{:S(2)}) collective-permute-start(f32[128,256]{1,0:T(8,128)S(1)} %get-tuple-element.67), channel_id=1, source_target_pairs={{1,2},{3,4},{5,6},{7,8},{9,10},{11,12},{13,14},{15,16},{17,18},{19... | collective-permute-start | bytes 393224 | tf_op jit(solution)/shard_map/ppermute | solution.py:485
  105.8 2.1 %collective-permute-start.11 = (f32[8,256]{1,0:T(8,128)S(1)}, f32[8,256]{1,0:T(8,128)S(1)}, u32[]{:S(2)}, u32[]{:S(2)}) collective-permute-start(f32[8,256]{1,0:T(8,128)S(1)} %get-tuple-element.68), channel_id=1, source_target_pairs={{0,64},{64,0},{1,65},{65,1},{2,66},{66,2},{3,67},{67,3},{4,68},{68... | collective-permute-start | bytes 24584 | tf_op jit(solution)/shard_map/ppermute | solution.py:487

commit v5 on v4

--- a/solution.py
+++ b/solution.py
@@ -18,7 +18,7 @@
 XS, YS, ZS = 4, 64, 256
 ROWS = XS * YS
 GROUP = 4
-GRAM_ROWS = 32
+GRAM_ROWS = 64
 HALF = KEEP // 2
 PACK = 6
 PACK_LANES = 40
@@ -143,24 +143,26 @@
     for ga, gb in LATE_PAIRS:
         gram_block(v_ref, sums_ref, ga, gb)
     early = sorted(g * GROUP + a for g in ARRIVAL[:EARLY] for a in range(GROUP))
-    sub = iota((KEEP, 128), 0)
-    in_early = (sub < (EARLY - 1) * GROUP) | (sub >= KEEP - GROUP)
-    lane = iota((KEEP, 128), 1)
-    matrix = jnp.zeros((KEEP, 128), F32)
+
+    def line(i, start):
+        part = sums_ref[i, pl.ds(start, HALF), :]
+        if i in early:
+            sub = iota((HALF, 128), 0) + start
+            in_early = (sub < (EARLY - 1) * GROUP) | (sub >= KEEP - GROUP)
+            part = jnp.where(in_early, early_ref[i, pl.ds(start, HALF), :], part)
+        return part
+
+    sub = iota((HALF, 128), 0)
+    lane = iota((HALF, 128), 1)
+    packed = jnp.zeros((HALF, 128), F32)
+    diagonal = jnp.zeros((HALF, 128), F32)
     for i in range(KEEP):
-        part = sums_ref[i]
-        if i in early:
-            part = jnp.where(in_early, early_ref[i], part)
-        column = jnp.sum(part, axis=1, keepdims=True)
-        matrix = jnp.where(lane == i, column, matrix)
-    matrix_ref[pl.ds(0, KEEP), :] = matrix
-    top = matrix_ref[pl.ds(0, HALF), :]
-    bottom = pltpu.roll(matrix_ref[pl.ds(HALF, HALF), :], 128 - HALF, 1)
-    lane = iota((HALF, 128), 1)
-    sub = iota((HALF, 128), 0)
-    diagonal = jnp.sum(jnp.where(lane == sub, top, 0.0), axis=1, keepdims=True)
-    packed = jnp.where((lane > sub) | (lane >= HALF), top, bottom)
-    packed = jnp.where(lane < KEEP, packed, jnp.where(lane == KEEP, diagonal, 0.0))
+        part = line(i, 0)
+        if i < HALF:
+            diagonal = jnp.where(sub == i, part, diagonal)
+            part = jnp.where(sub < i, part, line(HALF + i, HALF))
+        packed = jnp.where(lane == i, jnp.sum(part, axis=1, keepdims=True), packed)
+    packed = jnp.where(lane == KEEP, jnp.sum(diagonal, axis=1, keepdims=True), packed)
     matrix_ref[pl.ds(0, HALF), :] = packed
     packed = matrix_ref[pl.ds(0, PACK), :]
     for p in range(1, HALF // PACK):
@@ -181,44 +183,78 @@
     )(v, early)
 
 
-def dot_all(v_ref, others, x_ref, dots_ref):
-    dots_ref[...] = jnp.zeros((BASIS, 128), F32)
-    batch = 12
+def dot_all(v_ref, others, x_refs, dots_refs, chunks=ROWS // CHUNK, skip=False):
+    batch = 12 // len(x_refs)
+    for dots_ref in dots_refs:
+        dots_ref[...] = jnp.zeros((BASIS, 128), F32)
 
     def run(reads, base):
         def step(c, accs):
-            rows = pl.ds(pl.multiple_of(c * CHUNK, CHUNK), CHUNK)
-            x = x_ref[rows, :]
-            return tuple(acc + fold_tiles(read(rows) * x) for acc, read in zip(accs, reads))
+            start = c * CHUNK
+            if skip:
+                start = start + (c // (2 * YS // CHUNK)) * YS
+            rows = pl.ds(pl.multiple_of(start, CHUNK), CHUNK)
+            xs = [x_ref[rows, :] for x_ref in x_refs]
+            new = []
+            for n, read in enumerate(reads):
+                value = read(rows)
+                new += [accs[n * len(xs) + m] + fold_tiles(value * x) for m, x in enumerate(xs)]
+            return tuple(new)
 
         zero = jnp.zeros((8, ZS), F32)
-        accs = lax.fori_loop(0, ROWS // CHUNK, step, tuple(zero for _ in reads))
+        accs = lax.fori_loop(0, chunks, step, (zero,) * (len(reads) * len(x_refs)))
         for n, acc in enumerate(accs):
-            dots_ref[pl.ds(base + n, 1), :] = fold_row(acc)
+            row = base + n // len(x_refs)
+            dots_refs[n % len(x_refs)][pl.ds(row, 1), :] = fold_row(acc)
 
     for first in range(0, KEEP, batch):
         run([lambda rows, i=i: v_ref[i, rows, :] for i in range(first, first + batch)], first)
     if others:
         run([lambda rows, r=r: r[rows, :] for r in others], KEEP)
-    return to_row(jnp.sum(dots_ref[...], axis=1, keepdims=True))
-
-
-def self_dots_kernel(count, *refs):
-    v_ref, *others = refs[: 1 + count]
-    out_ref, dots_ref = refs[1 + count :]
-    out_ref[...] = dot_all(v_ref, others, others[-1], dots_ref)
-
-
-def self_dots_call(v, created):
-    count = len(created)
-    return pl.pallas_call(
-        functools.partial(self_dots_kernel, count),
-        in_specs=[VMEM_SPEC] * (1 + count),
-        out_specs=VMEM_SPEC,
-        out_shape=jax.ShapeDtypeStruct((1, 128), F32),
-        scratch_shapes=[pltpu.VMEM((BASIS, 128), F32)],
-        compiler_params=PARAMS,
-    )(v, *created)
+    return [to_row(jnp.sum(dots_ref[...], axis=1, keepdims=True)) for dots_ref in dots_refs]
+
+
+CENTER = -6.0 - 1.5 * sum(WIND_SPEEDS)
+NEAR = [1.0 + 2.0 * s for s in WIND_SPEEDS]
+FAR = [-0.5 * s for s in WIND_SPEEDS]
+
+
+def inner_image(source, swap_ref, reaction_ref, pad_ref, x):
+    upper = lax.axis_index("gy").astype(F32)
+    lane = iota((YS, ZS), 1)
+    mine = source[pl.ds(x * YS, YS), :]
+    pad_ref[x, pl.ds(8, YS), :] = mine
+    edge = swap_ref[pl.ds(2 * x, 2), :]
+    pad_ref[x, pl.ds(6, 2), :] = edge * upper
+    pad_ref[x, pl.ds(72, 1), :] = edge[0:1] * (1.0 - upper)
+    image = (CENTER - reaction_ref[pl.ds(x * YS, YS), :]) * mine
+    for distance, factor in ((1, 1.0), (-1, NEAR[0]), (-2, FAR[0])):
+        if 0 <= x + distance < XS:
+            image = image + factor * source[pl.ds((x + distance) * YS, YS), :]
+    image = (
+        image
+        + pad_ref[x, pl.ds(9, YS), :]
+        + NEAR[1] * pad_ref[x, pl.ds(7, YS), :]
+        + FAR[1] * pad_ref[x, pl.ds(6, YS), :]
+    )
+    return (
+        image
+        + jnp.where(lane < ZS - 1, pltpu.roll(mine, ZS - 1, 1), 0.0)
+        + NEAR[2] * jnp.where(lane >= 1, pltpu.roll(mine, 1, 1), 0.0)
+        + FAR[2] * jnp.where(lane >= 2, pltpu.roll(mine, 2, 1), 0.0)
+    )
+
+
+def outer_image(first_ref, second_ref):
+    odd = lax.axis_index("gx") % 2 == 1
+
+    def below(rows):
+        return jnp.where(odd, first_ref[rows, :], second_ref[rows, :])
+
+    two, one = below(pl.ds(0, YS)), below(pl.ds(YS, YS))
+    rows = pl.ds(0, YS)
+    above = jnp.where(odd, second_ref[rows, :], first_ref[rows, :])
+    return {0: NEAR[0] * one + FAR[0] * two, 1: FAR[0] * one, XS - 1: above}
 
 
 LAST_SHAPES = (
@@ -242,75 +278,109 @@
             out_ref[pl.ds(p * period + 8 * tile, 8), :] = block
 
 
-def payload_rows(count):
-    return 2 if count else 1 + PACK
-
-
-def image_kernel(count, *refs):
-    v_ref, *others = refs[: 1 + count]
-    first_ref, second_ref, swap_ref, reaction_ref, extra_ref = refs[1 + count : 6 + count]
-    w_ref, out_ref, dots_ref, pad_ref = refs[6 + count :]
-    odd = lax.axis_index("gx") % 2 == 1
-    upper = lax.axis_index("gy").astype(F32)
-    lower = 1.0 - upper
-    source = others[-1] if others else v_ref.at[KEEP - 1]
-    lane = iota((YS, ZS), 1)
-    center = -6.0 - 1.5 * sum(WIND_SPEEDS)
-    near = [1.0 + 2.0 * s for s in WIND_SPEEDS]
-    far = [-0.5 * s for s in WIND_SPEEDS]
-
-    def plane(x):
-        if x < 0:
-            rows = pl.ds((x + 2) * YS, YS)
-            return jnp.where(odd, first_ref[rows, :], second_ref[rows, :])
-        if x >= XS:
-            rows = pl.ds(0, YS)
-            return jnp.where(odd, second_ref[rows, :], first_ref[rows, :])
-        return source[pl.ds(x * YS, YS), :]
-
+def first_image_kernel(
+    v_ref, first_ref, second_ref, swap_ref, reaction_ref, extra_ref, w_ref, out_ref, dots_ref, pad_ref
+):
+    outer = outer_image(first_ref, second_ref)
     for x in range(XS):
-        mine = plane(x)
-        pad_ref[x, pl.ds(8, YS), :] = mine
-        edge = swap_ref[pl.ds(2 * x, 2), :]
-        pad_ref[x, pl.ds(6, 2), :] = edge * upper
-        pad_ref[x, pl.ds(72, 1), :] = edge[0:1] * lower
-        image = (center - reaction_ref[pl.ds(x * YS, YS), :]) * mine
-        image = image + plane(x + 1) + near[0] * plane(x - 1) + far[0] * plane(x - 2)
-        image = (
-            image
-            + pad_ref[x, pl.ds(9, YS), :]
-            + near[1] * pad_ref[x, pl.ds(7, YS), :]
-            + far[1] * pad_ref[x, pl.ds(6, YS), :]
-        )
-        image = (
-            image
-            + jnp.where(lane < ZS - 1, pltpu.roll(mine, ZS - 1, 1), 0.0)
-            + near[2] * jnp.where(lane >= 1, pltpu.roll(mine, 1, 1), 0.0)
-            + far[2] * jnp.where(lane >= 2, pltpu.roll(mine, 2, 1), 0.0)
-        )
-        w_ref[pl.ds(x * YS, YS), :] = image
-    more = [w_ref] if count == STEPS - 1 else []
-    rows = [dot_all(v_ref, others + more, w_ref, dots_ref)]
-    rows += [extra_ref[:, pl.ds(128 * r, 128)] for r in range(payload_rows(count) - 1)]
+        image = inner_image(v_ref.at[KEEP - 1], swap_ref, reaction_ref, pad_ref, x)
+        w_ref[pl.ds(x * YS, YS), :] = image + outer[x] if x in outer else image
+    rows = dot_all(v_ref, [], [w_ref], [dots_ref])
+    rows += [extra_ref[:, pl.ds(128 * r, 128)] for r in range(PACK)]
     write_for_all(out_ref, rows)
 
 
-def image_call(v, created, halo, reaction, extra, devices):
-    count = len(created)
-    return pl.pallas_call(
-        functools.partial(image_kernel, count),
-        in_specs=[VMEM_SPEC] * (6 + count),
+def first_image_call(v, halo, reaction, extra, devices):
+    return pl.pallas_call(
+        first_image_kernel,
+        in_specs=[VMEM_SPEC] * 6,
         out_specs=(VMEM_SPEC, VMEM_SPEC),
         out_shape=(
             pltpu.VMEM((ROWS, ZS), F32),
-            jax.ShapeDtypeStruct((devices * payload_rows(count), 128), F32),
+            jax.ShapeDtypeStruct((devices * (1 + PACK), 128), F32),
         ),
         scratch_shapes=[
             pltpu.VMEM((BASIS, 128), F32),
             pltpu.VMEM((XS, YS + 16, ZS), F32),
         ],
         compiler_params=PARAMS,
-    )(v, *created, *halo, reaction, extra)
+        name="image_0",
+    )(v, *halo, reaction, extra)
+
+
+def inner_kernel(count, *refs):
+    v_ref, near_ref, far_ref, *older = refs[: 2 + count]
+    swap_ref, reaction_ref, u_ref, w_ref, out_ref, dots_ref, more_ref, pad_ref = refs[2 + count :]
+    odd = lax.axis_index("gx") % 2 == 1
+    for x in range(2):
+        rows = pl.ds(x * YS, YS)
+        near, far = near_ref[rows, :], far_ref[rows, :]
+        u_ref[pl.ds(x * YS, YS), :] = jnp.where(odd, near, far)
+        u_ref[pl.ds((2 + x) * YS, YS), :] = jnp.where(odd, far, near)
+    for x in range(XS):
+        w_ref[pl.ds(x * YS, YS), :] = inner_image(u_ref, swap_ref, reaction_ref, pad_ref, x)
+    rows = dot_all(v_ref, [*older, u_ref], [w_ref, u_ref], [dots_ref, more_ref])
+    for n, row in enumerate(rows):
+        out_ref[pl.ds(n, 1), :] = row
+
+
+def inner_call(v, near, far, older, swap, reaction):
+    count = 1 + len(older)
+    return pl.pallas_call(
+        functools.partial(inner_kernel, count),
+        in_specs=[VMEM_SPEC] * (4 + count),
+        out_specs=(VMEM_SPEC,) * 3,
+        out_shape=(
+            pltpu.VMEM((ROWS, ZS), F32),
+            pltpu.VMEM((ROWS, ZS), F32),
+            jax.ShapeDtypeStruct((2, 128), F32),
+        ),
+        scratch_shapes=[
+            pltpu.VMEM((BASIS, 128), F32),
+            pltpu.VMEM((BASIS, 128), F32),
+            pltpu.VMEM((XS, YS + 16, ZS), F32),
+        ],
+        compiler_params=PARAMS,
+    )(v, near, far, *older, swap, reaction)
+
+
+def outer_kernel(count, *refs):
+    v_ref, *others = refs[: 1 + count]
+    first_ref, second_ref, inner_ref, extra_ref = refs[1 + count : 5 + count]
+    w_ref, out_ref, dots_ref, delta_ref = refs[5 + count :]
+    outer = outer_image(first_ref, second_ref)
+    for x in range(XS):
+        rows = pl.ds(x * YS, YS)
+        image = inner_ref[rows, :]
+        if x in outer:
+            delta_ref[rows, :] = outer[x]
+            image = image + outer[x]
+        w_ref[rows, :] = image
+    (row,) = dot_all(v_ref, others, [delta_ref], [dots_ref], 3 * YS // CHUNK, True)
+    row = row + extra_ref[pl.ds(0, 1), :]
+    if count == STEPS - 1:
+        square = jnp.zeros((8, ZS), F32)
+        for c in range(ROWS // CHUNK):
+            image = w_ref[pl.ds(c * CHUNK, CHUNK), :]
+            square = square + fold_tiles(image * image)
+        square = jnp.sum(fold_row(square), axis=1, keepdims=True)
+        row = jnp.where(iota((1, 128), 1) == BASIS - 1, square, row)
+    write_for_all(out_ref, [row, extra_ref[pl.ds(1, 1), :]])
+
+
+def outer_call(v, created, first, second, inner, extra, devices):
+    count = len(created)
+    return pl.pallas_call(
+        functools.partial(outer_kernel, count),
+        in_specs=[VMEM_SPEC] * (5 + count),
+        out_specs=(VMEM_SPEC, VMEM_SPEC),
+        out_shape=(
+            pltpu.VMEM((ROWS, ZS), F32),
+            jax.ShapeDtypeStruct((2 * devices, 128), F32),
+        ),
+        scratch_shapes=[pltpu.VMEM((BASIS, 128), F32), pltpu.VMEM((ROWS, ZS), F32)],
+        compiler_params=PARAMS,
+    )(v, *created, first, second, inner, extra)
 
 
 STATE_G, STATE_H, STATE_D, STATE_ROWS = 0, BASIS, 2 * BASIS, 2 * BASIS + 8
@@ -351,93 +421,187 @@
     pack_ref[pl.ds(KEEP, STEPS), :] = jnp.zeros((STEPS, 128), F32)
 
 
-def combine_kernel(count, cells, *refs):
-    recv_ref, w_ref, v_ref, *others = refs[: 3 + count]
-    pos = 3 + count
-    if count:
-        state_in = refs[pos]
-        pos += 1
-    u_ref, state_ref, *outs, weight_ref, pack_ref = refs[pos:]
-    final = count == STEPS - 1
-    if final:
-        square_ref, guess_ref, sound_ref = outs
+def solve_weights(count, cells, recv_ref, state_in, state_ref, weight_ref, pack_ref):
     lane = iota((1, 128), 1)
     lanes = iota((BASIS, 128), 1)
     subs = iota((BASIS, 128), 0)
+    sub = iota((BASIS, 1), 0)
     scale = 1.0 / cells
+
+    def spread(values):
+        return jnp.sum(values, axis=1, keepdims=True)
+
     if count == 0:
         total = summed_rows(recv_ref, 1 + PACK) * scale
         unpacked_gram(total[1 : 1 + PACK], pack_ref)
         gram = pack_ref[pl.ds(0, BASIS), :]
         hess = jnp.zeros((BASIS, 128), F32)
         inverse_row = jnp.where(lane < KEEP, 1.0, 0.0)
+        inverse_column = jnp.where(sub < KEEP, 1.0, 0.0)
         first_row = total[0:1]
         inverse = jnp.ones((1, 1), F32)
+        image_square = None
+        first = to_column(first_row)
+        folded = spread(gram * first_row)
     else:
         total = summed_rows(recv_ref, 2) * scale
         newest = KEEP + count - 1
         raw_first, raw_gram = total[0:1], total[1:2]
-        square = jnp.sum(jnp.where(lane == newest, raw_gram, 0.0), axis=1, keepdims=True)
+        inverse_row = state_in[pl.ds(STATE_D, 1), :]
+        gram = state_in[pl.ds(STATE_G, BASIS), :]
+        hess = state_in[pl.ds(STATE_H, BASIS), :]
+        part_first, part_gram = raw_first * inverse_row, raw_gram * inverse_row
+        square = spread(jnp.where(lane == newest, raw_gram, 0.0))
+        first_newest = spread(jnp.where(lane == newest, raw_first, 0.0))
+        image_square = spread(jnp.where(lane == BASIS - 1, raw_first, 0.0))
+        crossed = spread(part_gram * part_first)
+        first_column, gram_column = to_column(part_first), to_column(part_gram)
+        inverse_column = to_column(inverse_row)
+        folded = spread(gram * part_first)
         norm = jnp.sqrt(square + EPSILON)
         inverse = 1.0 / norm
-        inverse_row = jnp.where(lane == newest, inverse, state_in[pl.ds(STATE_D, 1), :])
-        gram_row = raw_gram * inverse_row * inverse
-        first_row = raw_first * inverse_row * inverse
-        gram = state_in[pl.ds(STATE_G, BASIS), :]
-        gram = jnp.where(lanes == newest, to_column(gram_row), gram)
-        gram = jnp.where(subs == newest, gram_row, gram)
-        hess = state_in[pl.ds(STATE_H, BASIS), :]
+        own = square * inverse * inverse
+        first_newest = first_newest * inverse * inverse
+        image_square = image_square * inverse * inverse
+        mine = sub == newest
+        first = jnp.where(mine, first_newest, first_column * inverse)
+        gram_column = gram_column * inverse
+        folded = jnp.where(
+            mine,
+            crossed * inverse * inverse + own * first_newest,
+            folded * inverse + gram_column * first_newest,
+        )
+        gram = jnp.where(lanes == newest, gram_column, gram)
+        gram = jnp.where(subs == newest, part_gram * inverse, gram)
+        gram = jnp.where((lanes == newest) & (subs == newest), own, gram)
         hess = jnp.where((subs == newest) & (lanes == count - 1), norm, hess)
-    first = to_column(first_row)
-    folded = jnp.sum(gram * first_row, axis=1, keepdims=True)
+        inverse_row = jnp.where(lane == newest, inverse, inverse_row)
+        inverse_column = jnp.where(mine, inverse, inverse_column)
     weights = first + (first - folded)
+    weight_ref[pl.ds(0, BASIS), :] = jnp.broadcast_to(weights * inverse_column, (BASIS, ZS))
+    weight_ref[pl.ds(BASIS, 8), :] = jnp.broadcast_to(inverse, (8, ZS))
     hess = jnp.where((lanes == count) & (subs < KEEP + count), weights, hess)
-    if final:
-        image_square = jnp.sum(jnp.where(lane == BASIS - 1, raw_first, 0.0), axis=1, keepdims=True)
-        image_square = image_square * inverse * inverse
-        again = jnp.sum(gram * to_row(weights), axis=1, keepdims=True)
-        guess = image_square - jnp.sum(weights * (2.0 * first - again), axis=0, keepdims=True)
-        guess_ref[...] = jnp.where(lane == 0, guess, 0.0)
-        sound = jnp.where(guess > SOUND_SHARE * image_square, 1, 0)
-        sound_ref[0] = sound[0, 0]
     state_ref[pl.ds(STATE_G, BASIS), :] = gram
     state_ref[pl.ds(STATE_H, BASIS), :] = hess
     state_ref[pl.ds(STATE_D, 8), :] = jnp.broadcast_to(inverse_row, (8, 128))
-    weight_ref[...] = jnp.broadcast_to(weights * to_column(inverse_row), (BASIS, ZS))
+    return weights, first, gram, image_square
+
+
+def combined(rows, weight_ref, w_ref, v_ref, others):
+    value = w_ref[rows, :] * weight_ref[pl.ds(BASIS, 1), :]
+    for i in range(KEEP):
+        value = value - weight_ref[pl.ds(i, 1), :] * v_ref[i, rows, :]
+    for i, other in enumerate(others):
+        value = value - weight_ref[pl.ds(KEEP + i, 1), :] * other[rows, :]
+    return value
+
+
+def combine_half(out_ref, high, weight_ref, w_ref, v_ref, others):
+    start = high.astype(jnp.int32) * (ROWS // 2)
+
+    def step(c, carry):
+        rows = pl.ds(pl.multiple_of(start + c * CHUNK, CHUNK), CHUNK)
+        out_ref[pl.ds(pl.multiple_of(c * CHUNK, CHUNK), CHUNK), :] = combined(
+            rows, weight_ref, w_ref, v_ref, others
+        )
+        return carry
+
+    lax.fori_loop(0, ROWS // 2 // CHUNK, step, 0)
+
+
+HALF_SHAPE = jax.ShapeDtypeStruct((ROWS // 2, ZS), F32)
+WEIGHT_SHAPE = (BASIS + 8, ZS)
+
+
+def far_kernel(count, cells, *refs):
+    recv_ref, w_ref, v_ref, *others = refs[: 3 + count]
+    *states, far_ref, weight_ref, state_ref, pack_ref = refs[3 + count :]
+    state_in = states[0] if states else None
+    solve_weights(count, cells, recv_ref, state_in, state_ref, weight_ref, pack_ref)
+    odd = lax.axis_index("gx") % 2 == 1
+    combine_half(far_ref, odd, weight_ref, w_ref, v_ref, others)
+
+
+def far_call(recv, w, v, created, state, cells):
+    count = len(created)
+    states = [state] if created else []
+    return pl.pallas_call(
+        functools.partial(far_kernel, count, cells),
+        in_specs=[VMEM_SPEC] * (3 + count + len(states)),
+        out_specs=(VMEM_SPEC,) * 3,
+        out_shape=(
+            HALF_SHAPE,
+            pltpu.VMEM(WEIGHT_SHAPE, F32),
+            jax.ShapeDtypeStruct((STATE_ROWS, 128), F32),
+        ),
+        scratch_shapes=[pltpu.VMEM((128, 128), F32)],
+        compiler_params=PARAMS,
+    )(recv, w, v, *created, *states)
+
+
+def near_kernel(count, *refs):
+    weight_ref, far_ref, w_ref, v_ref, *others = refs[: 4 + count]
+    near_ref, swap_ref = refs[4 + count :]
+    odd = lax.axis_index("gx") % 2 == 1
+    upper = lax.axis_index("gy") == 1
+    combine_half(near_ref, jnp.logical_not(odd), weight_ref, w_ref, v_ref, others)
+    for x in range(XS):
+        sides = []
+        for y in (0, YS - 2):
+            rows = pl.ds((x % 2) * YS + y, 2)
+            low, high = (near_ref, far_ref) if x < 2 else (far_ref, near_ref)
+            sides.append(jnp.where(odd, low[rows, :], high[rows, :]))
+        swap_ref[pl.ds(2 * x, 2), :] = jnp.where(upper, *sides)
+
+
+def near_call(weight, far, w, v, created):
+    count = len(created)
+    return pl.pallas_call(
+        functools.partial(near_kernel, count),
+        in_specs=[VMEM_SPEC] * (4 + count),
+        out_specs=(VMEM_SPEC,) * 2,
+        out_shape=(HALF_SHAPE, jax.ShapeDtypeStruct((2 * XS, ZS), F32)),
+        compiler_params=PARAMS,
+    )(weight, far, w, v, *created)
+
+
+def last_kernel(cells, *refs):
+    count = STEPS - 1
+    recv_ref, w_ref, v_ref, *others = refs[: 3 + count]
+    state_in, u_ref, state_ref, square_ref, guess_ref, sound_ref, weight_ref = refs[3 + count :]
+    weights, first, gram, image_square = solve_weights(
+        count, cells, recv_ref, state_in, state_ref, weight_ref, None
+    )
+    again = jnp.sum(gram * to_row(weights), axis=1, keepdims=True)
+    guess = image_square - jnp.sum(weights * (2.0 * first - again), axis=0, keepdims=True)
+    guess_ref[...] = jnp.where(iota((1, 128), 1) == 0, guess, 0.0)
+    sound = jnp.where(guess > SOUND_SHARE * image_square, 1, 0)
+    sound_ref[0] = sound[0, 0]
 
     def step(c, acc):
         rows = pl.ds(pl.multiple_of(c * CHUNK, CHUNK), CHUNK)
-        value = w_ref[rows, :] * inverse
-        for i in range(KEEP):
-            value = value - weight_ref[pl.ds(i, 1), :] * v_ref[i, rows, :]
-        for i, other in enumerate(others):
-            value = value - weight_ref[pl.ds(KEEP + i, 1), :] * other[rows, :]
+        value = combined(rows, weight_ref, w_ref, v_ref, others)
         u_ref[rows, :] = value
         return acc + fold_tiles(value * value)
 
     acc = lax.fori_loop(0, ROWS // CHUNK, step, jnp.zeros((8, ZS), F32))
-    if final:
-        square_ref[...] = fold_row(acc)
-    else:
-        write_edges(u_ref, *outs)
-
-
-def combine_call(recv, w, v, created, state, cells):
-    count = len(created)
-    states = [state] if created else []
-    final = count == STEPS - 1
-    return pl.pallas_call(
-        functools.partial(combine_kernel, count, cells),
-        in_specs=[VMEM_SPEC] * (3 + count + len(states)),
-        out_specs=(VMEM_SPEC,) * 4 + (SMEM_SPEC if final else VMEM_SPEC,),
+    square_ref[...] = fold_row(acc)
+
+
+def last_call(recv, w, v, created, state, cells):
+    return pl.pallas_call(
+        functools.partial(last_kernel, cells),
+        in_specs=[VMEM_SPEC] * (4 + len(created)),
+        out_specs=(VMEM_SPEC,) * 4 + (SMEM_SPEC,),
         out_shape=(
             pltpu.VMEM((ROWS, ZS), F32),
             jax.ShapeDtypeStruct((STATE_ROWS, 128), F32),
-            *(LAST_SHAPES if final else EDGE_SHAPES),
+            *LAST_SHAPES,
         ),
-        scratch_shapes=[pltpu.VMEM((BASIS, ZS), F32), pltpu.VMEM((128, 128), F32)],
-        compiler_params=PARAMS,
-    )(recv, w, v, *created, *states)
+        scratch_shapes=[pltpu.VMEM(WEIGHT_SHAPE, F32)],
+        compiler_params=PARAMS,
+        name="last",
+    )(recv, w, v, *created, state)
 
 
 def finish_kernel(*refs):
@@ -475,17 +639,13 @@
     )(square, state, *created)
 
 
-def exchange(first, second, swap):
-    count = lax.axis_size("gx")
-
-    def pairs(start):
-        lower = range(start, count - 1, 2)
-        return [(i, i + 1) for i in lower] + [(i + 1, i) for i in lower]
-
-    second = lax.ppermute(second, "gx", pairs(1))
-    first = lax.ppermute(first, "gx", pairs(0))
-    swap = lax.ppermute(swap, "gy", [(0, 1), (1, 0)])
-    return first, second, swap
+def paired(half, start):
+    lower = range(start, lax.axis_size("gx") - 1, 2)
+    return lax.ppermute(half, "gx", [(i, i + 1) for i in lower] + [(i + 1, i) for i in lower])
+
+
+def across(edge):
+    return lax.ppermute(edge, "gy", [(0, 1), (1, 0)])
 
 
 def from_all(payload):
@@ -500,22 +660,27 @@
     devices = lax.axis_size(("gy", "gx"))
     cells = float(ROWS * ZS * devices)
     basis = basis_vectors.reshape(KEEP, ROWS, ZS)
-    v, *edges, early = start_call(basis)
-    halo = exchange(*edges)
+    v, near, far, swap, early = start_call(basis)
+    second = paired(far, 1)
+    first = paired(near, 0)
+    swap = across(swap)
     reaction = reaction.reshape(ROWS, ZS)
     extra = gram_call(v, early)
+    w, payload = first_image_call(v, (first, second, swap), reaction, extra, devices)
     created = []
     state = None
-    for j in range(STEPS):
-        if j:
-            extra = self_dots_call(v, created)
-        w, payload = image_call(v, created, halo, reaction, extra, devices)
+    for _ in range(1, STEPS):
         recv = from_all(payload)
-        u, state, *edges = combine_call(recv, w, v, created, state, cells)
+        far, weight, state = far_call(recv, w, v, created, state, cells)
+        second = paired(far, 1)
+        near, swap = near_call(weight, far, w, v, created)
+        first = paired(near, 0)
+        swap = across(swap)
+        u, inner, extra = inner_call(v, near, far, created, swap, reaction)
         created.append(u)
-        if j + 1 < STEPS:
-            halo = exchange(*edges)
-    square, guess, sound = edges
+        w, payload = outer_call(v, created, first, second, inner, extra, devices)
+    u, state, square, guess, sound = last_call(from_all(payload), w, v, created, state, cells)
+    created.append(u)
     square = lax.cond(
         sound[0] == 1,
         lambda guess, square: guess,

time: 135 us -> 133 us (0.985)
  blocking collectives: 87 us -> 84.5 us
  waiting for transfers between devices: 4.07 us -> 2.51 us
  Pallas kernels: 32.8 us -> 34.2 us
    pallas_call x11 -> x14, Pallas kernels: 15.3 us -> 18.1 us  [the longest x3 7.33 us: inner_call(): pl.pallas_call(functools.partial(inner_kernel, count), in_specs=[VMEM_SPE...]
    all_to_all x4, blocking collectives: 87 us -> 84.5 us  [from_all(): got = lax.all_to_all(copies, axes, split_axis=0, concat_axis=0, tiled=True)]
    ppermute x12, waiting for transfers between devices: 4.07 us -> 2.51 us  [the longest x4 2.49 us: across(): return lax.ppermute(edge, 'gy', [(0, 1), (1, 0)])]
  transfers between devices with their start and end apart: 12 -> 12, of which waited for: 3 -> 3; matrix products, arithmetic and copies ran while one was open for 0% -> 0% of each run, Pallas kernels for 11% -> 14%
where the time goes in v5:
time: 133 us
  blocking collectives  84.5 us (64%)
  Pallas kernels  34.2 us (26%)
  starting transfers between devices  10.1 us (8%)
  waiting for transfers between devices  2.51 us (2%)
  between operations  1.45 us (1%)
    all_to_all x4, blocking collectives, from_all(): got = lax.all_to_all(copies, axes, split_axis=0, concat_axis=0, tiled=True)  84.5 us
    pallas_call x1, Pallas kernels, gram_call(): pl.pallas_call(gram_kernel, in_specs=[VMEM_SPEC, VMEM_SPEC], out_specs=VM...  10.8 us
    pallas_call x3, Pallas kernels, inner_call(): pl.pallas_call(functools.partial(inner_kernel, count), in_specs=[VMEM_SPE...  7.33 us
    ppermute x8, starting transfers between devices, paired(): lax.ppermute(half, 'gx', [(i, i + 1) for i in lower] + [(i + 1, i) for i...  6.01 us
    pallas_call x1, Pallas kernels, start_call(): pl.pallas_call(start_kernel, in_specs=[pl.BlockSpec(memory_space=pltpu.HB...  4.17 us
    ppermute x4, starting transfers between devices, across(): return lax.ppermute(edge, 'gy', [(0, 1), (1, 0)])  4.09 us
    pallas_call x3, Pallas kernels, outer_call(): pl.pallas_call(functools.partial(outer_kernel, count), in_specs=[VMEM_SPE...  3.32 us
  transfers between devices with their start and end apart: 12, of which 3 were waited for; matrix products, arithmetic and copies ran while one was open for 0% of the time, Pallas kernels for 14%

profile of v5, /device:TPU:1, one launch (start us, length us, event | category | flops | bytes accessed | tf_op | source)
XLA Modules:
  0.0 132.7 jit_solution(18030105969676323965)
XLA Ops:
  0.6 4.2 %start.1 = (f32[36,256,256]{2,1,0:T(8,128)S(1)}, f32[128,256]{1,0:T(8,128)S(1)}, f32[128,256]{1,0:T(8,128)S(1)}, f32[8,256]{1,0:T(8,128)S(1)}, f32[36,36,128]{2,1,0:T(8,128)S(1)}) custom-call(f32[36,256,256]{2,1,0:T(8,128)} %bitcast.29), custom_call_target="tpu_custom_call" | custom-call | tf_op jit(solution)/shard_map/start/pallas_call | solution.py:127
  4.8 2.1 %collective-permute-start = (f32[128,256]{1,0:T(8,128)S(1)}, f32[128,256]{1,0:T(8,128)S(1)}, u32[]{:S(2)}, u32[]{:S(2)}) collective-permute-start(f32[128,256]{1,0:T(8,128)S(1)} %get-tuple-element.54), channel_id=1, source_target_pairs={{0,1},{2,3},{4,5},{6,7},{8,9},{10,11},{12,13},{14,15},{16,17},{18,... | collective-permute-start | bytes 393224 | tf_op jit(solution)/shard_map/ppermute | solution.py:644
  7.6 1.0 collective-permute-start.2
  8.6 10.8 %gram.1.extra_ref = f32[1,768]{1,0:T(1,128)S(1)} custom-call(f32[36,256,256]{2,1,0:T(8,128)S(1)} %get-tuple-element.53.v_ref.refs_2_.refs_3_.refs_0_, f32[36,36,128]{2,1,0:T(8,128)S(1)} %get-tuple-element.57.early_ref), custom_call_target="tpu_custom_call" | custom-call | tf_op jit(solution)/shard_map/gram/pallas_call | solution.py:175
  19.4 1.4 %image_0.1 = (f32[256,256]{1,0:T(8,128)S(1)}, f32[896,128]{1,0:T(8,128)S(1)}) custom-call(f32[36,256,256]{2,1,0:T(8,128)S(1)} %get-tuple-element.53.v_ref.refs_2_.refs_3_.refs_0_, f32[128,256]{1,0:T(8,128)S(1)} %collective-permute-done.first_ref, f32[128,256]{1,0:T(8,128)S(1)} %collective-permute-done.1.second_ref, ...), custom_call_target="tpu_custom_call" | custom-call | tf_op jit(solution)/shard_map/image_0/pallas_call | solution.py:294
  20.8 24.9 %all_to_all.25 = f32[128,1,896]{2,1,0:T(1,128)S(1)} all-to-all(f32[128,1,896]{2,1,0:T(1,128)S(1)} %bitcast.25), channel_id=1, replica_groups=mesh['gy'=2,'gx'=64] {'gy','gx'}, dimensions={0} | all-to-all | bytes 917504 | tf_op jit(solution)/shard_map/all_to_all | solution.py:655
  45.7 0.8 shard_map.41
  48.2 1.2 collective-permute-start.3
  49.3 0.8 collective-permute-done.3.refs_3_
  50.2 2.4 %shard_map.43 = (f32[256,256]{1,0:T(8,128)S(1)}, f32[256,256]{1,0:T(8,128)S(1)}, f32[2,128]{1,0:T(2,128)S(1)}) custom-call(f32[36,256,256]{2,1,0:T(8,128)S(1)} %get-tuple-element.53.v_ref.refs_2_.refs_3_.refs_0_, f32[128,256]{1,0:T(8,128)S(1)} %get-tuple-element.62.refs_1_, f32[128,256]{1,0:T(8,128)S(1)} %get-tuple-element.61.refs_1_.refs_2_, ...), custom_call_target="tpu_custom_call" | custom-call | tf_op jit(solution)/shard_map/pallas_call | solution.py:329
  52.6 1.1 shard_map.44
  53.7 19.9 %all_to_all.26 = f32[128,1,256]{2,1,0:T(1,128)S(1)} all-to-all(f32[128,1,256]{2,1,0:T(1,128)S(1)} %bitcast.26), channel_id=1, replica_groups=mesh['gy'=2,'gx'=64] {'gy','gx'}, dimensions={0} | all-to-all | bytes 262144 | tf_op jit(solution)/shard_map/all_to_all | solution.py:655
  75.9 0.9 collective-permute-start.6
  76.9 0.8 collective-permute-done.6.refs_4_
  77.7 2.4 %shard_map.47 = (f32[256,256]{1,0:T(8,128)S(1)}, f32[256,256]{1,0:T(8,128)S(1)}, f32[2,128]{1,0:T(2,128)S(1)}) custom-call(f32[36,256,256]{2,1,0:T(8,128)S(1)} %get-tuple-element.53.v_ref.refs_2_.refs_3_.refs_0_, f32[128,256]{1,0:T(8,128)S(1)} %get-tuple-element.72.refs_1_, f32[128,256]{1,0:T(8,128)S(1)} %get-tuple-element.71.refs_1_.refs_2_, ...), custom_call_target="tpu_custom_call" | custom-call | tf_op jit(solution)/shard_map/pallas_call | solution.py:329
  80.2 1.1 shard_map.48
  81.3 19.8 %all_to_all.27 = f32[128,1,256]{2,1,0:T(1,128)S(1)} all-to-all(f32[128,1,256]{2,1,0:T(1,128)S(1)} %bitcast.27), channel_id=1, replica_groups=mesh['gy'=2,'gx'=64] {'gy','gx'}, dimensions={0} | all-to-all | bytes 262144 | tf_op jit(solution)/shard_map/all_to_all | solution.py:655
  103.7 0.9 collective-permute-start.9
  104.6 0.8 collective-permute-done.9.refs_5_
  105.5 2.5 %shard_map.51 = (f32[256,256]{1,0:T(8,128)S(1)}, f32[256,256]{1,0:T(8,128)S(1)}, f32[2,128]{1,0:T(2,128)S(1)}) custom-call(f32[36,256,256]{2,1,0:T(8,128)S(1)} %get-tuple-element.53.v_ref.refs_2_.refs_3_.refs_0_, f32[128,256]{1,0:T(8,128)S(1)} %get-tuple-element.82.refs_1_, f32[128,256]{1,0:T(8,128)S(1)} %get-tuple-element.81.refs_1_.refs_2_, ...), custom_call_target="tpu_custom_call" | custom-call | tf_op jit(solution)/shard_map/pallas_call | solution.py:329
  107.9 1.1 shard_map.52
  109.1 19.8 %all_to_all.28 = f32[128,1,256]{2,1,0:T(1,128)S(1)} all-to-all(f32[128,1,256]{2,1,0:T(1,128)S(1)} %bitcast.28), channel_id=1, replica_groups=mesh['gy'=2,'gx'=64] {'gy','gx'}, dimensions={0} | all-to-all | bytes 262144 | tf_op jit(solution)/shard_map/all_to_all | solution.py:655
  128.9 2.0 %last.1 = (f32[256,256]{1,0:T(8,128)S(1)}, f32[88,128]{1,0:T(8,128)S(1)}, f32[1,128]{1,0:T(1,128)S(1)}, f32[1,128]{1,0:T(1,128)S(1)}, s32[1]{0:T(128)}) custom-call(f32[256,128]{1,0:T(8,128)S(1)} %bitcast.22, f32[256,256]{1,0:T(8,128)S(1)} %get-tuple-element.88.refs_1_, f32[36,256,256]{2,1,0:T(8,128)S(1)} %get-tuple-element.53.v_ref.refs_2_.refs_3_.refs_0_, ...), custom_call_target="tpu_custom_call" | custom-call | tf_op jit(solution)/shard_map/last/pallas_call | solution.py:592
  131.6 1.1 finish.1
  (24 shorter events, 7.2 us)
Async XLA Ops:
  0.6 18.8 %copy-start = (f32[4,64,256]{2,1,0:T(8,128)S(1)}, f32[4,64,256]{2,1,0:T(8,128)}, u32[]{:S(2)}) copy-start(f32[4,64,256]{2,1,0:T(8,128)} %param.5) | copy-start | bytes 786436
  4.8 14.6 %collective-permute-start = (f32[128,256]{1,0:T(8,128)S(1)}, f32[128,256]{1,0:T(8,128)S(1)}, u32[]{:S(2)}, u32[]{:S(2)}) collective-permute-start(f32[128,256]{1,0:T(8,128)S(1)} %get-tuple-element.54), channel_id=1, source_target_pairs={{0,1},{2,3},{4,5},{6,7},{8,9},{10,11},{12,13},{14,15},{16,17},{18,... | collective-permute-start | bytes 393224 | tf_op jit(solution)/shard_map/ppermute | solution.py:644
  6.9 12.5 %collective-permute-start.1 = (f32[128,256]{1,0:T(8,128)S(1)}, f32[128,256]{1,0:T(8,128)S(1)}, u32[]{:S(2)}, u32[]{:S(2)}) collective-permute-start(f32[128,256]{1,0:T(8,128)S(1)} %get-tuple-element.55), channel_id=1, source_target_pairs={{1,2},{3,4},{5,6},{7,8},{9,10},{11,12},{13,14},{15,16},{17,18},{19... | collective-permute-start | bytes 393224 | tf_op jit(solution)/shard_map/ppermute | solution.py:644
  7.6 11.8 %collective-permute-start.2 = (f32[8,256]{1,0:T(8,128)S(1)}, f32[8,256]{1,0:T(8,128)S(1)}, u32[]{:S(2)}, u32[]{:S(2)}) collective-permute-start(f32[8,256]{1,0:T(8,128)S(1)} %get-tuple-element.56), channel_id=1, source_target_pairs={{0,64},{64,0},{1,65},{65,1},{2,66},{66,2},{3,67},{67,3},{4,68},{68... | collective-permute-start | bytes 24584 | tf_op jit(solution)/shard_map/ppermute | solution.py:648
  47.1 5.4 %collective-permute-start.4 = (f32[128,256]{1,0:T(8,128)S(1)}, f32[128,256]{1,0:T(8,128)S(1)}, u32[]{:S(2)}, u32[]{:S(2)}) collective-permute-start(f32[128,256]{1,0:T(8,128)S(1)} %get-tuple-element.62.refs_1_), channel_id=1, source_target_pairs={{0,1},{2,3},{4,5},{6,7},{8,9},{10,11},{12,13},{14,15},{16,17},{18,... | collective-permute-start | bytes 393224 | tf_op jit(solution)/shard_map/ppermute | solution.py:644
  47.5 5.1 %collective-permute-start.5 = (f32[128,256]{1,0:T(8,128)S(1)}, f32[128,256]{1,0:T(8,128)S(1)}, u32[]{:S(2)}, u32[]{:S(2)}) collective-permute-start(f32[128,256]{1,0:T(8,128)S(1)} %get-tuple-element.61.refs_1_.refs_2_), channel_id=1, source_target_pairs={{1,2},{3,4},{5,6},{7,8},{9,10},{11,12},{13,14},{15,16},{17,18},{19... | collective-permute-start | bytes 393224 | tf_op jit(solution)/shard_map/ppermute | solution.py:644
  48.2 2.0 %collective-permute-start.3 = (f32[8,256]{1,0:T(8,128)S(1)}, f32[8,256]{1,0:T(8,128)S(1)}, u32[]{:S(2)}, u32[]{:S(2)}) collective-permute-start(f32[8,256]{1,0:T(8,128)S(1)} %get-tuple-element.63), channel_id=1, source_target_pairs={{0,64},{64,0},{1,65},{65,1},{2,66},{66,2},{3,67},{67,3},{4,68},{68... | collective-permute-start | bytes 24584 | tf_op jit(solution)/shard_map/ppermute | solution.py:648
  74.9 5.2 %collective-permute-start.7 = (f32[128,256]{1,0:T(8,128)S(1)}, f32[128,256]{1,0:T(8,128)S(1)}, u32[]{:S(2)}, u32[]{:S(2)}) collective-permute-start(f32[128,256]{1,0:T(8,128)S(1)} %get-tuple-element.72.refs_1_), channel_id=1, source_target_pairs={{0,1},{2,3},{4,5},{6,7},{8,9},{10,11},{12,13},{14,15},{16,17},{18,... | collective-permute-start | bytes 393224 | tf_op jit(solution)/shard_map/ppermute | solution.py:644
  75.3 4.9 %collective-permute-start.8 = (f32[128,256]{1,0:T(8,128)S(1)}, f32[128,256]{1,0:T(8,128)S(1)}, u32[]{:S(2)}, u32[]{:S(2)}) collective-permute-start(f32[128,256]{1,0:T(8,128)S(1)} %get-tuple-element.71.refs_1_.refs_2_), channel_id=1, source_target_pairs={{1,2},{3,4},{5,6},{7,8},{9,10},{11,12},{13,14},{15,16},{17,18},{19... | collective-permute-start | bytes 393224 | tf_op jit(solution)/shard_map/ppermute | solution.py:644
  75.9 1.8 %collective-permute-start.6 = (f32[8,256]{1,0:T(8,128)S(1)}, f32[8,256]{1,0:T(8,128)S(1)}, u32[]{:S(2)}, u32[]{:S(2)}) collective-permute-start(f32[8,256]{1,0:T(8,128)S(1)} %get-tuple-element.73), channel_id=1, source_target_pairs={{0,64},{64,0},{1,65},{65,1},{2,66},{66,2},{3,67},{67,3},{4,68},{68... | collective-permute-start | bytes 24584 | tf_op jit(solution)/shard_map/ppermute | solution.py:648
  102.5 5.5 %collective-permute-start.10 = (f32[128,256]{1,0:T(8,128)S(1)}, f32[128,256]{1,0:T(8,128)S(1)}, u32[]{:S(2)}, u32[]{:S(2)}) collective-permute-start(f32[128,256]{1,0:T(8,128)S(1)} %get-tuple-element.82.refs_1_), channel_id=1, source_target_pairs={{0,1},{2,3},{4,5},{6,7},{8,9},{10,11},{12,13},{14,15},{16,17},{18,... | collective-permute-start | bytes 393224 | tf_op jit(solution)/shard_map/ppermute | solution.py:644
  103.0 4.9 %collective-permute-start.11 = (f32[128,256]{1,0:T(8,128)S(1)}, f32[128,256]{1,0:T(8,128)S(1)}, u32[]{:S(2)}, u32[]{:S(2)}) collective-permute-start(f32[128,256]{1,0:T(8,128)S(1)} %get-tuple-element.81.refs_1_.refs_2_), channel_id=1, source_target_pairs={{1,2},{3,4},{5,6},{7,8},{9,10},{11,12},{13,14},{15,16},{17,18},{19... | collective-permute-start | bytes 393224 | tf_op jit(solution)/shard_map/ppermute | solution.py:644
  103.7 1.8 %collective-permute-start.9 = (f32[8,256]{1,0:T(8,128)S(1)}, f32[8,256]{1,0:T(8,128)S(1)}, u32[]{:S(2)}, u32[]{:S(2)}) collective-permute-start(f32[8,256]{1,0:T(8,128)S(1)} %get-tuple-element.83), channel_id=1, source_target_pairs={{0,64},{64,0},{1,65},{65,1},{2,66},{66,2},{3,67},{67,3},{4,68},{68... | collective-permute-start | bytes 24584 | tf_op jit(solution)/shard_map/ppermute | solution.py:648

commit v6 on v5

--- a/solution.py
+++ b/solution.py
@@ -22,7 +22,9 @@
 HALF = KEEP // 2
 PACK = 6
 PACK_LANES = 40
+FREE_LANE = 117
 CHUNK = 32
+BLOCK = 64
 SOUND_SHARE = 0.05
 
 PARAMS = pltpu.CompilerParams(vmem_limit_bytes=16 * 2**20)
@@ -183,17 +185,17 @@
     )(v, early)
 
 
-def dot_all(v_ref, others, x_refs, dots_refs, chunks=ROWS // CHUNK, skip=False):
+ALL_PLANES = ((0, XS),)
+
+
+def dot_all(v_ref, others, x_refs, dots_refs, planes=ALL_PLANES):
     batch = 12 // len(x_refs)
     for dots_ref in dots_refs:
         dots_ref[...] = jnp.zeros((BASIS, 128), F32)
 
     def run(reads, base):
         def step(c, accs):
-            start = c * CHUNK
-            if skip:
-                start = start + (c // (2 * YS // CHUNK)) * YS
-            rows = pl.ds(pl.multiple_of(start, CHUNK), CHUNK)
+            rows = pl.ds(pl.multiple_of(c * CHUNK, CHUNK), CHUNK)
             xs = [x_ref[rows, :] for x_ref in x_refs]
             new = []
             for n, read in enumerate(reads):
@@ -202,7 +204,9 @@
             return tuple(new)
 
         zero = jnp.zeros((8, ZS), F32)
-        accs = lax.fori_loop(0, chunks, step, (zero,) * (len(reads) * len(x_refs)))
+        accs = (zero,) * (len(reads) * len(x_refs))
+        for first, end in planes:
+            accs = lax.fori_loop(first * YS // CHUNK, end * YS // CHUNK, step, accs)
         for n, acc in enumerate(accs):
             row = base + n // len(x_refs)
             dots_refs[n % len(x_refs)][pl.ds(row, 1), :] = fold_row(acc)
@@ -285,8 +289,13 @@
     for x in range(XS):
         image = inner_image(v_ref.at[KEEP - 1], swap_ref, reaction_ref, pad_ref, x)
         w_ref[pl.ds(x * YS, YS), :] = image + outer[x] if x in outer else image
-    rows = dot_all(v_ref, [], [w_ref], [dots_ref])
-    rows += [extra_ref[:, pl.ds(128 * r, 128)] for r in range(PACK)]
+    (row,) = dot_all(v_ref, [], [w_ref], [dots_ref])
+    lane = iota((1, 128), 1)
+    free = (lane >= FREE_LANE) & (lane < FREE_LANE + PACK)
+    rows = []
+    for r in range(PACK):
+        part = jnp.where(free, pltpu.roll(row, FREE_LANE - r * PACK, 1), 0.0)
+        rows.append(extra_ref[:, pl.ds(128 * r, 128)] + part)
     write_for_all(out_ref, rows)
 
 
@@ -297,7 +306,7 @@
         out_specs=(VMEM_SPEC, VMEM_SPEC),
         out_shape=(
             pltpu.VMEM((ROWS, ZS), F32),
-            jax.ShapeDtypeStruct((devices * (1 + PACK), 128), F32),
+            jax.ShapeDtypeStruct((devices * PACK, 128), F32),
         ),
         scratch_shapes=[
             pltpu.VMEM((BASIS, 128), F32),
@@ -356,7 +365,7 @@
             delta_ref[rows, :] = outer[x]
             image = image + outer[x]
         w_ref[rows, :] = image
-    (row,) = dot_all(v_ref, others, [delta_ref], [dots_ref], 3 * YS // CHUNK, True)
+    (row,) = dot_all(v_ref, others, [delta_ref], [dots_ref], ((0, 2), (3, 4)))
     row = row + extra_ref[pl.ds(0, 1), :]
     if count == STEPS - 1:
         square = jnp.zeros((8, ZS), F32)
@@ -432,13 +441,17 @@
         return jnp.sum(values, axis=1, keepdims=True)
 
     if count == 0:
-        total = summed_rows(recv_ref, 1 + PACK) * scale
-        unpacked_gram(total[1 : 1 + PACK], pack_ref)
+        total = summed_rows(recv_ref, PACK) * scale
+        unpacked_gram(total[:PACK], pack_ref)
         gram = pack_ref[pl.ds(0, BASIS), :]
         hess = jnp.zeros((BASIS, 128), F32)
         inverse_row = jnp.where(lane < KEEP, 1.0, 0.0)
         inverse_column = jnp.where(sub < KEEP, 1.0, 0.0)
-        first_row = total[0:1]
+        first_row = jnp.zeros((1, 128), F32)
+        for r in range(PACK):
+            part = pltpu.roll(total[r : r + 1], 128 - FREE_LANE + r * PACK, 1)
+            mine = (lane >= r * PACK) & (lane < (r + 1) * PACK)
+            first_row = jnp.where(mine, part, first_row)
         inverse = jnp.ones((1, 1), F32)
         image_square = None
         first = to_column(first_row)
@@ -500,13 +513,13 @@
     start = high.astype(jnp.int32) * (ROWS // 2)
 
     def step(c, carry):
-        rows = pl.ds(pl.multiple_of(start + c * CHUNK, CHUNK), CHUNK)
-        out_ref[pl.ds(pl.multiple_of(c * CHUNK, CHUNK), CHUNK), :] = combined(
+        rows = pl.ds(pl.multiple_of(start + c * BLOCK, BLOCK), BLOCK)
+        out_ref[pl.ds(pl.multiple_of(c * BLOCK, BLOCK), BLOCK), :] = combined(
             rows, weight_ref, w_ref, v_ref, others
         )
         return carry
 
-    lax.fori_loop(0, ROWS // 2 // CHUNK, step, 0)
+    lax.fori_loop(0, ROWS // 2 // BLOCK, step, 0)
 
 
 HALF_SHAPE = jax.ShapeDtypeStruct((ROWS // 2, ZS), F32)
@@ -579,12 +592,12 @@
     sound_ref[0] = sound[0, 0]
 
     def step(c, acc):
-        rows = pl.ds(pl.multiple_of(c * CHUNK, CHUNK), CHUNK)
+        rows = pl.ds(pl.multiple_of(c * BLOCK, BLOCK), BLOCK)
         value = combined(rows, weight_ref, w_ref, v_ref, others)
         u_ref[rows, :] = value
         return acc + fold_tiles(value * value)
 
-    acc = lax.fori_loop(0, ROWS // CHUNK, step, jnp.zeros((8, ZS), F32))
+    acc = lax.fori_loop(0, ROWS // BLOCK, step, jnp.zeros((8, ZS), F32))
     square_ref[...] = fold_row(acc)
 
 

time: 133 us -> 132 us (level)
  no operation moved by 1% of the time
where the time goes in v6:
time: 132 us; the launch traced here: 131 us
  blocking collectives  83.8 us (63%)
  Pallas kernels  33.7 us (26%)
  starting transfers between devices  9.9 us (8%)
  waiting for transfers between devices  2.51 us (2%)
  between operations  1.45 us (1%)
    all_to_all x4, blocking collectives, from_all(): got = lax.all_to_all(copies, axes, split_axis=0, concat_axis=0, tiled=True)  83.8 us
    pallas_call x1, Pallas kernels, gram_call(): pl.pallas_call(gram_kernel, in_specs=[VMEM_SPEC, VMEM_SPEC], out_specs=VM...  10.8 us
    pallas_call x3, Pallas kernels, inner_call(): pl.pallas_call(functools.partial(inner_kernel, count), in_specs=[VMEM_SPE...  7.33 us
    ppermute x8, starting transfers between devices, paired(): lax.ppermute(half, 'gx', [(i, i + 1) for i in lower] + [(i + 1, i) for i...  5.83 us
    pallas_call x1, Pallas kernels, start_call(): pl.pallas_call(start_kernel, in_specs=[pl.BlockSpec(memory_space=pltpu.HB...  4.17 us
    ppermute x4, starting transfers between devices, across(): return lax.ppermute(edge, 'gy', [(0, 1), (1, 0)])  4.07 us
    pallas_call x3, Pallas kernels, outer_call(): pl.pallas_call(functools.partial(outer_kernel, count), in_specs=[VMEM_SPE...  2.8 us
  transfers between devices with their start and end apart: 12, of which 3 were waited for; matrix products, arithmetic and copies ran while one was open for 0% of the time, Pallas kernels for 14%

profile of v6, /device:TPU:1, one launch (start us, length us, event | category | flops | bytes accessed | tf_op | source)
XLA Modules:
  0.0 131.4 jit_solution(572125047310173040)
XLA Ops:
  0.6 4.2 %start.1 = (f32[36,256,256]{2,1,0:T(8,128)S(1)}, f32[128,256]{1,0:T(8,128)S(1)}, f32[128,256]{1,0:T(8,128)S(1)}, f32[8,256]{1,0:T(8,128)S(1)}, f32[36,36,128]{2,1,0:T(8,128)S(1)}) custom-call(f32[36,256,256]{2,1,0:T(8,128)} %bitcast.29), custom_call_target="tpu_custom_call" | custom-call | tf_op jit(solution)/shard_map/start/pallas_call | solution.py:129
  4.8 2.1 %collective-permute-start = (f32[128,256]{1,0:T(8,128)S(1)}, f32[128,256]{1,0:T(8,128)S(1)}, u32[]{:S(2)}, u32[]{:S(2)}) collective-permute-start(f32[128,256]{1,0:T(8,128)S(1)} %get-tuple-element.54), channel_id=1, source_target_pairs={{0,1},{2,3},{4,5},{6,7},{8,9},{10,11},{12,13},{14,15},{16,17},{18,... | collective-permute-start | bytes 393224 | tf_op jit(solution)/shard_map/ppermute | solution.py:657
  7.6 1.0 collective-permute-start.2
  8.6 10.8 %gram.1.extra_ref = f32[1,768]{1,0:T(1,128)S(1)} custom-call(f32[36,256,256]{2,1,0:T(8,128)S(1)} %get-tuple-element.53.v_ref.refs_2_.refs_3_.refs_0_, f32[36,36,128]{2,1,0:T(8,128)S(1)} %get-tuple-element.57.early_ref), custom_call_target="tpu_custom_call" | custom-call | tf_op jit(solution)/shard_map/gram/pallas_call | solution.py:177
  19.4 1.4 %image_0.1 = (f32[256,256]{1,0:T(8,128)S(1)}, f32[768,128]{1,0:T(8,128)S(1)}) custom-call(f32[36,256,256]{2,1,0:T(8,128)S(1)} %get-tuple-element.53.v_ref.refs_2_.refs_3_.refs_0_, f32[128,256]{1,0:T(8,128)S(1)} %collective-permute-done.first_ref, f32[128,256]{1,0:T(8,128)S(1)} %collective-permute-done.1.second_ref, ...), custom_call_target="tpu_custom_call" | custom-call | tf_op jit(solution)/shard_map/image_0/pallas_call | solution.py:303
  20.9 24.3 %all_to_all.25 = f32[128,1,768]{2,1,0:T(1,128)S(1)} all-to-all(f32[128,1,768]{2,1,0:T(1,128)S(1)} %bitcast.25), channel_id=1, replica_groups=mesh['gy'=2,'gx'=64] {'gy','gx'}, dimensions={0} | all-to-all | bytes 786432 | tf_op jit(solution)/shard_map/all_to_all | solution.py:668
  45.1 0.9 shard_map.41
  47.6 1.1 collective-permute-start.3
  48.8 0.8 collective-permute-done.3.refs_3_
  49.6 2.4 %shard_map.43 = (f32[256,256]{1,0:T(8,128)S(1)}, f32[256,256]{1,0:T(8,128)S(1)}, f32[2,128]{1,0:T(2,128)S(1)}) custom-call(f32[36,256,256]{2,1,0:T(8,128)S(1)} %get-tuple-element.53.v_ref.refs_2_.refs_3_.refs_0_, f32[128,256]{1,0:T(8,128)S(1)} %get-tuple-element.62.refs_1_, f32[128,256]{1,0:T(8,128)S(1)} %get-tuple-element.61.refs_1_.refs_2_, ...), custom_call_target="tpu_custom_call" | custom-call | tf_op jit(solution)/shard_map/pallas_call | solution.py:338
  52.0 0.9 shard_map.44
  52.9 19.9 %all_to_all.26 = f32[128,1,256]{2,1,0:T(1,128)S(1)} all-to-all(f32[128,1,256]{2,1,0:T(1,128)S(1)} %bitcast.26), channel_id=1, replica_groups=mesh['gy'=2,'gx'=64] {'gy','gx'}, dimensions={0} | all-to-all | bytes 262144 | tf_op jit(solution)/shard_map/all_to_all | solution.py:668
  75.2 0.9 collective-permute-start.6
  76.2 0.8 collective-permute-done.6.refs_4_
  77.0 2.4 %shard_map.47 = (f32[256,256]{1,0:T(8,128)S(1)}, f32[256,256]{1,0:T(8,128)S(1)}, f32[2,128]{1,0:T(2,128)S(1)}) custom-call(f32[36,256,256]{2,1,0:T(8,128)S(1)} %get-tuple-element.53.v_ref.refs_2_.refs_3_.refs_0_, f32[128,256]{1,0:T(8,128)S(1)} %get-tuple-element.72.refs_1_, f32[128,256]{1,0:T(8,128)S(1)} %get-tuple-element.71.refs_1_.refs_2_, ...), custom_call_target="tpu_custom_call" | custom-call | tf_op jit(solution)/shard_map/pallas_call | solution.py:338
  79.5 0.9 shard_map.48
  80.4 19.8 %all_to_all.27 = f32[128,1,256]{2,1,0:T(1,128)S(1)} all-to-all(f32[128,1,256]{2,1,0:T(1,128)S(1)} %bitcast.27), channel_id=1, replica_groups=mesh['gy'=2,'gx'=64] {'gy','gx'}, dimensions={0} | all-to-all | bytes 262144 | tf_op jit(solution)/shard_map/all_to_all | solution.py:668
  102.7 0.9 collective-permute-start.9
  103.6 0.8 collective-permute-done.9.refs_5_
  104.4 2.5 %shard_map.51 = (f32[256,256]{1,0:T(8,128)S(1)}, f32[256,256]{1,0:T(8,128)S(1)}, f32[2,128]{1,0:T(2,128)S(1)}) custom-call(f32[36,256,256]{2,1,0:T(8,128)S(1)} %get-tuple-element.53.v_ref.refs_2_.refs_3_.refs_0_, f32[128,256]{1,0:T(8,128)S(1)} %get-tuple-element.82.refs_1_, f32[128,256]{1,0:T(8,128)S(1)} %get-tuple-element.81.refs_1_.refs_2_, ...), custom_call_target="tpu_custom_call" | custom-call | tf_op jit(solution)/shard_map/pallas_call | solution.py:338
  106.9 1.0 shard_map.52
  107.9 19.8 %all_to_all.28 = f32[128,1,256]{2,1,0:T(1,128)S(1)} all-to-all(f32[128,1,256]{2,1,0:T(1,128)S(1)} %bitcast.28), channel_id=1, replica_groups=mesh['gy'=2,'gx'=64] {'gy','gx'}, dimensions={0} | all-to-all | bytes 262144 | tf_op jit(solution)/shard_map/all_to_all | solution.py:668
  127.7 1.8 %last.1 = (f32[256,256]{1,0:T(8,128)S(1)}, f32[88,128]{1,0:T(8,128)S(1)}, f32[1,128]{1,0:T(1,128)S(1)}, f32[1,128]{1,0:T(1,128)S(1)}, s32[1]{0:T(128)}) custom-call(f32[256,128]{1,0:T(8,128)S(1)} %bitcast.22, f32[256,256]{1,0:T(8,128)S(1)} %get-tuple-element.88.refs_1_, f32[36,256,256]{2,1,0:T(8,128)S(1)} %get-tuple-element.53.v_ref.refs_2_.refs_3_.refs_0_, ...), custom_call_target="tpu_custom_call" | custom-call | tf_op jit(solution)/shard_map/last/pallas_call | solution.py:605
  130.2 1.1 finish.1
  (24 shorter events, 7.1 us)
Async XLA Ops:
  0.6 18.8 %copy-start = (f32[4,64,256]{2,1,0:T(8,128)S(1)}, f32[4,64,256]{2,1,0:T(8,128)}, u32[]{:S(2)}) copy-start(f32[4,64,256]{2,1,0:T(8,128)} %param.5) | copy-start | bytes 786436
  4.8 14.6 %collective-permute-start = (f32[128,256]{1,0:T(8,128)S(1)}, f32[128,256]{1,0:T(8,128)S(1)}, u32[]{:S(2)}, u32[]{:S(2)}) collective-permute-start(f32[128,256]{1,0:T(8,128)S(1)} %get-tuple-element.54), channel_id=1, source_target_pairs={{0,1},{2,3},{4,5},{6,7},{8,9},{10,11},{12,13},{14,15},{16,17},{18,... | collective-permute-start | bytes 393224 | tf_op jit(solution)/shard_map/ppermute | solution.py:657
  6.9 12.5 %collective-permute-start.1 = (f32[128,256]{1,0:T(8,128)S(1)}, f32[128,256]{1,0:T(8,128)S(1)}, u32[]{:S(2)}, u32[]{:S(2)}) collective-permute-start(f32[128,256]{1,0:T(8,128)S(1)} %get-tuple-element.55), channel_id=1, source_target_pairs={{1,2},{3,4},{5,6},{7,8},{9,10},{11,12},{13,14},{15,16},{17,18},{19... | collective-permute-start | bytes 393224 | tf_op jit(solution)/shard_map/ppermute | solution.py:657
  7.6 11.8 %collective-permute-start.2 = (f32[8,256]{1,0:T(8,128)S(1)}, f32[8,256]{1,0:T(8,128)S(1)}, u32[]{:S(2)}, u32[]{:S(2)}) collective-permute-start(f32[8,256]{1,0:T(8,128)S(1)} %get-tuple-element.56), channel_id=1, source_target_pairs={{0,64},{64,0},{1,65},{65,1},{2,66},{66,2},{3,67},{67,3},{4,68},{68... | collective-permute-start | bytes 24584 | tf_op jit(solution)/shard_map/ppermute | solution.py:661
  46.6 5.4 %collective-permute-start.4 = (f32[128,256]{1,0:T(8,128)S(1)}, f32[128,256]{1,0:T(8,128)S(1)}, u32[]{:S(2)}, u32[]{:S(2)}) collective-permute-start(f32[128,256]{1,0:T(8,128)S(1)} %get-tuple-element.62.refs_1_), channel_id=1, source_target_pairs={{0,1},{2,3},{4,5},{6,7},{8,9},{10,11},{12,13},{14,15},{16,17},{18,... | collective-permute-start | bytes 393224 | tf_op jit(solution)/shard_map/ppermute | solution.py:657
  47.0 5.1 %collective-permute-start.5 = (f32[128,256]{1,0:T(8,128)S(1)}, f32[128,256]{1,0:T(8,128)S(1)}, u32[]{:S(2)}, u32[]{:S(2)}) collective-permute-start(f32[128,256]{1,0:T(8,128)S(1)} %get-tuple-element.61.refs_1_.refs_2_), channel_id=1, source_target_pairs={{1,2},{3,4},{5,6},{7,8},{9,10},{11,12},{13,14},{15,16},{17,18},{19... | collective-permute-start | bytes 393224 | tf_op jit(solution)/shard_map/ppermute | solution.py:657
  47.6 2.0 %collective-permute-start.3 = (f32[8,256]{1,0:T(8,128)S(1)}, f32[8,256]{1,0:T(8,128)S(1)}, u32[]{:S(2)}, u32[]{:S(2)}) collective-permute-start(f32[8,256]{1,0:T(8,128)S(1)} %get-tuple-element.63), channel_id=1, source_target_pairs={{0,64},{64,0},{1,65},{65,1},{2,66},{66,2},{3,67},{67,3},{4,68},{68... | collective-permute-start | bytes 24584 | tf_op jit(solution)/shard_map/ppermute | solution.py:661
  74.2 5.2 %collective-permute-start.7 = (f32[128,256]{1,0:T(8,128)S(1)}, f32[128,256]{1,0:T(8,128)S(1)}, u32[]{:S(2)}, u32[]{:S(2)}) collective-permute-start(f32[128,256]{1,0:T(8,128)S(1)} %get-tuple-element.72.refs_1_), channel_id=1, source_target_pairs={{0,1},{2,3},{4,5},{6,7},{8,9},{10,11},{12,13},{14,15},{16,17},{18,... | collective-permute-start | bytes 393224 | tf_op jit(solution)/shard_map/ppermute | solution.py:657
  74.6 4.9 %collective-permute-start.8 = (f32[128,256]{1,0:T(8,128)S(1)}, f32[128,256]{1,0:T(8,128)S(1)}, u32[]{:S(2)}, u32[]{:S(2)}) collective-permute-start(f32[128,256]{1,0:T(8,128)S(1)} %get-tuple-element.71.refs_1_.refs_2_), channel_id=1, source_target_pairs={{1,2},{3,4},{5,6},{7,8},{9,10},{11,12},{13,14},{15,16},{17,18},{19... | collective-permute-start | bytes 393224 | tf_op jit(solution)/shard_map/ppermute | solution.py:657
  75.2 1.8 %collective-permute-start.6 = (f32[8,256]{1,0:T(8,128)S(1)}, f32[8,256]{1,0:T(8,128)S(1)}, u32[]{:S(2)}, u32[]{:S(2)}) collective-permute-start(f32[8,256]{1,0:T(8,128)S(1)} %get-tuple-element.73), channel_id=1, source_target_pairs={{0,64},{64,0},{1,65},{65,1},{2,66},{66,2},{3,67},{67,3},{4,68},{68... | collective-permute-start | bytes 24584 | tf_op jit(solution)/shard_map/ppermute | solution.py:661
  101.6 5.3 %collective-permute-start.10 = (f32[128,256]{1,0:T(8,128)S(1)}, f32[128,256]{1,0:T(8,128)S(1)}, u32[]{:S(2)}, u32[]{:S(2)}) collective-permute-start(f32[128,256]{1,0:T(8,128)S(1)} %get-tuple-element.82.refs_1_), channel_id=1, source_target_pairs={{0,1},{2,3},{4,5},{6,7},{8,9},{10,11},{12,13},{14,15},{16,17},{18,... | collective-permute-start | bytes 393224 | tf_op jit(solution)/shard_map/ppermute | solution.py:657
  102.0 4.9 %collective-permute-start.11 = (f32[128,256]{1,0:T(8,128)S(1)}, f32[128,256]{1,0:T(8,128)S(1)}, u32[]{:S(2)}, u32[]{:S(2)}) collective-permute-start(f32[128,256]{1,0:T(8,128)S(1)} %get-tuple-element.81.refs_1_.refs_2_), channel_id=1, source_target_pairs={{1,2},{3,4},{5,6},{7,8},{9,10},{11,12},{13,14},{15,16},{17,18},{19... | collective-permute-start | bytes 393224 | tf_op jit(solution)/shard_map/ppermute | solution.py:657
  102.7 1.8 %collective-permute-start.9 = (f32[8,256]{1,0:T(8,128)S(1)}, f32[8,256]{1,0:T(8,128)S(1)}, u32[]{:S(2)}, u32[]{:S(2)}) collective-permute-start(f32[8,256]{1,0:T(8,128)S(1)} %get-tuple-element.83), channel_id=1, source_target_pairs={{0,64},{64,0},{1,65},{65,1},{2,66},{66,2},{3,67},{67,3},{4,68},{68... | collective-permute-start | bytes 24584 | tf_op jit(solution)/shard_map/ppermute | solution.py:661

commit v7 on v6

--- a/solution.py
+++ b/solution.py
@@ -23,6 +23,7 @@
 PACK = 6
 PACK_LANES = 40
 FREE_LANE = 117
+OWN_LANE = 64
 CHUNK = 32
 BLOCK = 64
 SOUND_SHARE = 0.05
@@ -328,9 +329,8 @@
         u_ref[pl.ds((2 + x) * YS, YS), :] = jnp.where(odd, far, near)
     for x in range(XS):
         w_ref[pl.ds(x * YS, YS), :] = inner_image(u_ref, swap_ref, reaction_ref, pad_ref, x)
-    rows = dot_all(v_ref, [*older, u_ref], [w_ref, u_ref], [dots_ref, more_ref])
-    for n, row in enumerate(rows):
-        out_ref[pl.ds(n, 1), :] = row
+    row, own = dot_all(v_ref, [*older, u_ref], [w_ref, u_ref], [dots_ref, more_ref])
+    out_ref[...] = row + pltpu.roll(own, OWN_LANE, 1)
 
 
 def inner_call(v, near, far, older, swap, reaction):
@@ -342,7 +342,7 @@
         out_shape=(
             pltpu.VMEM((ROWS, ZS), F32),
             pltpu.VMEM((ROWS, ZS), F32),
-            jax.ShapeDtypeStruct((2, 128), F32),
+            jax.ShapeDtypeStruct((1, 128), F32),
         ),
         scratch_shapes=[
             pltpu.VMEM((BASIS, 128), F32),
@@ -366,7 +366,7 @@
             image = image + outer[x]
         w_ref[rows, :] = image
     (row,) = dot_all(v_ref, others, [delta_ref], [dots_ref], ((0, 2), (3, 4)))
-    row = row + extra_ref[pl.ds(0, 1), :]
+    row = row + extra_ref[...]
     if count == STEPS - 1:
         square = jnp.zeros((8, ZS), F32)
         for c in range(ROWS // CHUNK):
@@ -374,7 +374,7 @@
             square = square + fold_tiles(image * image)
         square = jnp.sum(fold_row(square), axis=1, keepdims=True)
         row = jnp.where(iota((1, 128), 1) == BASIS - 1, square, row)
-    write_for_all(out_ref, [row, extra_ref[pl.ds(1, 1), :]])
+    write_for_all(out_ref, [row])
 
 
 def outer_call(v, created, first, second, inner, extra, devices):
@@ -385,7 +385,7 @@
         out_specs=(VMEM_SPEC, VMEM_SPEC),
         out_shape=(
             pltpu.VMEM((ROWS, ZS), F32),
-            jax.ShapeDtypeStruct((2 * devices, 128), F32),
+            jax.ShapeDtypeStruct((devices, 128), F32),
         ),
         scratch_shapes=[pltpu.VMEM((BASIS, 128), F32), pltpu.VMEM((ROWS, ZS), F32)],
         compiler_params=PARAMS,
@@ -457,9 +457,10 @@
         first = to_column(first_row)
         folded = spread(gram * first_row)
     else:
-        total = summed_rows(recv_ref, 2) * scale
+        total = summed_rows(recv_ref, 1)[0:1] * scale
         newest = KEEP + count - 1
-        raw_first, raw_gram = total[0:1], total[1:2]
+        raw_first = total
+        raw_gram = pltpu.roll(total, 128 - OWN_LANE, 1)
         inverse_row = state_in[pl.ds(STATE_D, 1), :]
         gram = state_in[pl.ds(STATE_G, BASIS), :]
         hess = state_in[pl.ds(STATE_H, BASIS), :]
@@ -513,13 +514,13 @@
     start = high.astype(jnp.int32) * (ROWS // 2)
 
     def step(c, carry):
-        rows = pl.ds(pl.multiple_of(start + c * BLOCK, BLOCK), BLOCK)
-        out_ref[pl.ds(pl.multiple_of(c * BLOCK, BLOCK), BLOCK), :] = combined(
+        rows = pl.ds(pl.multiple_of(start + c * CHUNK, CHUNK), CHUNK)
+        out_ref[pl.ds(pl.multiple_of(c * CHUNK, CHUNK), CHUNK), :] = combined(
             rows, weight_ref, w_ref, v_ref, others
         )
         return carry
 
-    lax.fori_loop(0, ROWS // 2 // BLOCK, step, 0)
+    lax.fori_loop(0, ROWS // 2 // CHUNK, step, 0)
 
 
 HALF_SHAPE = jax.ShapeDtypeStruct((ROWS // 2, ZS), F32)

time: 132 us -> 130 us (0.985)
  blocking collectives: 83.8 us -> 82.3 us
    all_to_all x4, blocking collectives: 83.8 us -> 82.3 us  [from_all(): got = lax.all_to_all(copies, axes, split_axis=0, concat_axis=0, tiled=True)]
where the time goes in v7:
time: 130 us
  blocking collectives  82.3 us (63%)
  Pallas kernels  33.6 us (26%)
  starting transfers between devices  10.4 us (8%)
  waiting for transfers between devices  2.51 us (2%)
  between operations  1.41 us (1%)
    all_to_all x4, blocking collectives, from_all(): got = lax.all_to_all(copies, axes, split_axis=0, concat_axis=0, tiled=True)  82.3 us
    pallas_call x1, Pallas kernels, gram_call(): pl.pallas_call(gram_kernel, in_specs=[VMEM_SPEC, VMEM_SPEC], out_specs=VM...  10.8 us
    pallas_call x3, Pallas kernels, inner_call(): pl.pallas_call(functools.partial(inner_kernel, count), in_specs=[VMEM_SPE...  7.52 us
    ppermute x8, starting transfers between devices, paired(): lax.ppermute(half, 'gx', [(i, i + 1) for i in lower] + [(i + 1, i) for i...  6.06 us
    ppermute x4, starting transfers between devices, across(): return lax.ppermute(edge, 'gy', [(0, 1), (1, 0)])  4.36 us
    pallas_call x1, Pallas kernels, start_call(): pl.pallas_call(start_kernel, in_specs=[pl.BlockSpec(memory_space=pltpu.HB...  4.17 us
    pallas_call x3, Pallas kernels, outer_call(): pl.pallas_call(functools.partial(outer_kernel, count), in_specs=[VMEM_SPE...  2.79 us
  transfers between devices with their start and end apart: 12, of which 3 were waited for; matrix products, arithmetic and copies ran while one was open for 0% of the time, Pallas kernels for 14%

profile of v7, /device:TPU:1, one launch (start us, length us, event | category | flops | bytes accessed | tf_op | source)
XLA Modules:
  0.0 130.2 jit_solution(4080297711127582197)
XLA Ops:
  0.6 4.2 %start.1 = (f32[36,256,256]{2,1,0:T(8,128)S(1)}, f32[128,256]{1,0:T(8,128)S(1)}, f32[128,256]{1,0:T(8,128)S(1)}, f32[8,256]{1,0:T(8,128)S(1)}, f32[36,36,128]{2,1,0:T(8,128)S(1)}) custom-call(f32[36,256,256]{2,1,0:T(8,128)} %bitcast.35), custom_call_target="tpu_custom_call" | custom-call | tf_op jit(solution)/shard_map/start/pallas_call | solution.py:130
  4.8 2.1 %collective-permute-start = (f32[128,256]{1,0:T(8,128)S(1)}, f32[128,256]{1,0:T(8,128)S(1)}, u32[]{:S(2)}, u32[]{:S(2)}) collective-permute-start(f32[128,256]{1,0:T(8,128)S(1)} %get-tuple-element.54), channel_id=1, source_target_pairs={{0,1},{2,3},{4,5},{6,7},{8,9},{10,11},{12,13},{14,15},{16,17},{18,... | collective-permute-start | bytes 393224 | tf_op jit(solution)/shard_map/ppermute | solution.py:658
  7.6 1.0 collective-permute-start.2
  8.6 10.8 %gram.1.extra_ref = f32[1,768]{1,0:T(1,128)S(1)} custom-call(f32[36,256,256]{2,1,0:T(8,128)S(1)} %get-tuple-element.53.v_ref.refs_2_.refs_3_.refs_0_, f32[36,36,128]{2,1,0:T(8,128)S(1)} %get-tuple-element.57.early_ref), custom_call_target="tpu_custom_call" | custom-call | tf_op jit(solution)/shard_map/gram/pallas_call | solution.py:178
  19.4 1.4 %image_0.1 = (f32[256,256]{1,0:T(8,128)S(1)}, f32[768,128]{1,0:T(8,128)S(1)}) custom-call(f32[36,256,256]{2,1,0:T(8,128)S(1)} %get-tuple-element.53.v_ref.refs_2_.refs_3_.refs_0_, f32[128,256]{1,0:T(8,128)S(1)} %collective-permute-done.first_ref, f32[128,256]{1,0:T(8,128)S(1)} %collective-permute-done.1.second_ref, ...), custom_call_target="tpu_custom_call" | custom-call | tf_op jit(solution)/shard_map/image_0/pallas_call | solution.py:304
  20.9 24.3 %all_to_all.25 = f32[128,1,768]{2,1,0:T(1,128)S(1)} all-to-all(f32[128,1,768]{2,1,0:T(1,128)S(1)} %bitcast.28), channel_id=1, replica_groups=mesh['gy'=2,'gx'=64] {'gy','gx'}, dimensions={0} | all-to-all | bytes 786432 | tf_op jit(solution)/shard_map/all_to_all | solution.py:669
  45.1 0.8 shard_map.41
  47.6 1.1 collective-permute-start.3
  48.7 0.8 collective-permute-done.3.refs_3_
  49.5 2.5 %shard_map.43 = (f32[256,256]{1,0:T(8,128)S(1)}, f32[256,256]{1,0:T(8,128)S(1)}, f32[1,128]{1,0:T(1,128)S(1)}) custom-call(f32[36,256,256]{2,1,0:T(8,128)S(1)} %get-tuple-element.53.v_ref.refs_2_.refs_3_.refs_0_, f32[128,256]{1,0:T(8,128)S(1)} %get-tuple-element.62.refs_1_, f32[128,256]{1,0:T(8,128)S(1)} %get-tuple-element.61.refs_1_.refs_2_, ...), custom_call_target="tpu_custom_call" | custom-call | tf_op jit(solution)/shard_map/pallas_call | solution.py:338
  52.0 0.9 shard_map.44
  52.9 19.3 %all_to_all.26 = f32[128,1,128]{2,1,0:T(1,128)S(1)} all-to-all(f32[128,1,128]{2,1,0:T(1,128)S(1)} %bitcast.32), channel_id=1, replica_groups=mesh['gy'=2,'gx'=64] {'gy','gx'}, dimensions={0} | all-to-all | bytes 131072 | tf_op jit(solution)/shard_map/all_to_all | solution.py:669
  74.6 1.1 collective-permute-start.6
  75.7 0.8 collective-permute-done.6.refs_4_
  76.5 2.5 %shard_map.47 = (f32[256,256]{1,0:T(8,128)S(1)}, f32[256,256]{1,0:T(8,128)S(1)}, f32[1,128]{1,0:T(1,128)S(1)}) custom-call(f32[36,256,256]{2,1,0:T(8,128)S(1)} %get-tuple-element.53.v_ref.refs_2_.refs_3_.refs_0_, f32[128,256]{1,0:T(8,128)S(1)} %get-tuple-element.72.refs_1_, f32[128,256]{1,0:T(8,128)S(1)} %get-tuple-element.71.refs_1_.refs_2_, ...), custom_call_target="tpu_custom_call" | custom-call | tf_op jit(solution)/shard_map/pallas_call | solution.py:338
  79.0 0.9 shard_map.48
  80.0 19.3 %all_to_all.27 = f32[128,1,128]{2,1,0:T(1,128)S(1)} all-to-all(f32[128,1,128]{2,1,0:T(1,128)S(1)} %bitcast.33), channel_id=1, replica_groups=mesh['gy'=2,'gx'=64] {'gy','gx'}, dimensions={0} | all-to-all | bytes 131072 | tf_op jit(solution)/shard_map/all_to_all | solution.py:669
  101.9 1.1 collective-permute-start.9
  103.0 0.8 collective-permute-done.9.refs_5_
  103.8 2.5 %shard_map.51 = (f32[256,256]{1,0:T(8,128)S(1)}, f32[256,256]{1,0:T(8,128)S(1)}, f32[1,128]{1,0:T(1,128)S(1)}) custom-call(f32[36,256,256]{2,1,0:T(8,128)S(1)} %get-tuple-element.53.v_ref.refs_2_.refs_3_.refs_0_, f32[128,256]{1,0:T(8,128)S(1)} %get-tuple-element.82.refs_1_, f32[128,256]{1,0:T(8,128)S(1)} %get-tuple-element.81.refs_1_.refs_2_, ...), custom_call_target="tpu_custom_call" | custom-call | tf_op jit(solution)/shard_map/pallas_call | solution.py:338
  106.3 0.9 shard_map.52
  107.3 19.3 %all_to_all.28 = f32[128,1,128]{2,1,0:T(1,128)S(1)} all-to-all(f32[128,1,128]{2,1,0:T(1,128)S(1)} %bitcast.34), channel_id=1, replica_groups=mesh['gy'=2,'gx'=64] {'gy','gx'}, dimensions={0} | all-to-all | bytes 131072 | tf_op jit(solution)/shard_map/all_to_all | solution.py:669
  126.6 1.8 %last.1 = (f32[256,256]{1,0:T(8,128)S(1)}, f32[88,128]{1,0:T(8,128)S(1)}, f32[1,128]{1,0:T(1,128)S(1)}, f32[1,128]{1,0:T(1,128)S(1)}, s32[1]{0:T(128)}) custom-call(f32[128,128]{1,0:T(8,128)S(1)} %bitcast.29, f32[256,256]{1,0:T(8,128)S(1)} %get-tuple-element.88.refs_1_, f32[36,256,256]{2,1,0:T(8,128)S(1)} %get-tuple-element.53.v_ref.refs_2_.refs_3_.refs_0_, ...), custom_call_target="tpu_custom_call" | custom-call | tf_op jit(solution)/shard_map/last/pallas_call | solution.py:606
  129.1 1.1 finish.1
  (24 shorter events, 7.1 us)
Async XLA Ops:
  0.6 18.8 %copy-start = (f32[4,64,256]{2,1,0:T(8,128)S(1)}, f32[4,64,256]{2,1,0:T(8,128)}, u32[]{:S(2)}) copy-start(f32[4,64,256]{2,1,0:T(8,128)} %param.5) | copy-start | bytes 786436
  4.8 14.6 %collective-permute-start = (f32[128,256]{1,0:T(8,128)S(1)}, f32[128,256]{1,0:T(8,128)S(1)}, u32[]{:S(2)}, u32[]{:S(2)}) collective-permute-start(f32[128,256]{1,0:T(8,128)S(1)} %get-tuple-element.54), channel_id=1, source_target_pairs={{0,1},{2,3},{4,5},{6,7},{8,9},{10,11},{12,13},{14,15},{16,17},{18,... | collective-permute-start | bytes 393224 | tf_op jit(solution)/shard_map/ppermute | solution.py:658
  6.9 12.5 %collective-permute-start.1 = (f32[128,256]{1,0:T(8,128)S(1)}, f32[128,256]{1,0:T(8,128)S(1)}, u32[]{:S(2)}, u32[]{:S(2)}) collective-permute-start(f32[128,256]{1,0:T(8,128)S(1)} %get-tuple-element.55), channel_id=1, source_target_pairs={{1,2},{3,4},{5,6},{7,8},{9,10},{11,12},{13,14},{15,16},{17,18},{19... | collective-permute-start | bytes 393224 | tf_op jit(solution)/shard_map/ppermute | solution.py:658
  7.6 11.8 %collective-permute-start.2 = (f32[8,256]{1,0:T(8,128)S(1)}, f32[8,256]{1,0:T(8,128)S(1)}, u32[]{:S(2)}, u32[]{:S(2)}) collective-permute-start(f32[8,256]{1,0:T(8,128)S(1)} %get-tuple-element.56), channel_id=1, source_target_pairs={{0,64},{64,0},{1,65},{65,1},{2,66},{66,2},{3,67},{67,3},{4,68},{68... | collective-permute-start | bytes 24584 | tf_op jit(solution)/shard_map/ppermute | solution.py:662
  46.5 5.5 %collective-permute-start.4 = (f32[128,256]{1,0:T(8,128)S(1)}, f32[128,256]{1,0:T(8,128)S(1)}, u32[]{:S(2)}, u32[]{:S(2)}) collective-permute-start(f32[128,256]{1,0:T(8,128)S(1)} %get-tuple-element.62.refs_1_), channel_id=1, source_target_pairs={{0,1},{2,3},{4,5},{6,7},{8,9},{10,11},{12,13},{14,15},{16,17},{18,... | collective-permute-start | bytes 393224 | tf_op jit(solution)/shard_map/ppermute | solution.py:658
  46.9 5.1 %collective-permute-start.5 = (f32[128,256]{1,0:T(8,128)S(1)}, f32[128,256]{1,0:T(8,128)S(1)}, u32[]{:S(2)}, u32[]{:S(2)}) collective-permute-start(f32[128,256]{1,0:T(8,128)S(1)} %get-tuple-element.61.refs_1_.refs_2_), channel_id=1, source_target_pairs={{1,2},{3,4},{5,6},{7,8},{9,10},{11,12},{13,14},{15,16},{17,18},{19... | collective-permute-start | bytes 393224 | tf_op jit(solution)/shard_map/ppermute | solution.py:658
  47.6 2.0 %collective-permute-start.3 = (f32[8,256]{1,0:T(8,128)S(1)}, f32[8,256]{1,0:T(8,128)S(1)}, u32[]{:S(2)}, u32[]{:S(2)}) collective-permute-start(f32[8,256]{1,0:T(8,128)S(1)} %get-tuple-element.63), channel_id=1, source_target_pairs={{0,64},{64,0},{1,65},{65,1},{2,66},{66,2},{3,67},{67,3},{4,68},{68... | collective-permute-start | bytes 24584 | tf_op jit(solution)/shard_map/ppermute | solution.py:662
  73.6 5.5 %collective-permute-start.7 = (f32[128,256]{1,0:T(8,128)S(1)}, f32[128,256]{1,0:T(8,128)S(1)}, u32[]{:S(2)}, u32[]{:S(2)}) collective-permute-start(f32[128,256]{1,0:T(8,128)S(1)} %get-tuple-element.72.refs_1_), channel_id=1, source_target_pairs={{0,1},{2,3},{4,5},{6,7},{8,9},{10,11},{12,13},{14,15},{16,17},{18,... | collective-permute-start | bytes 393224 | tf_op jit(solution)/shard_map/ppermute | solution.py:658
  73.9 5.1 %collective-permute-start.8 = (f32[128,256]{1,0:T(8,128)S(1)}, f32[128,256]{1,0:T(8,128)S(1)}, u32[]{:S(2)}, u32[]{:S(2)}) collective-permute-start(f32[128,256]{1,0:T(8,128)S(1)} %get-tuple-element.71.refs_1_.refs_2_), channel_id=1, source_target_pairs={{1,2},{3,4},{5,6},{7,8},{9,10},{11,12},{13,14},{15,16},{17,18},{19... | collective-permute-start | bytes 393224 | tf_op jit(solution)/shard_map/ppermute | solution.py:658
  74.6 1.9 %collective-permute-start.6 = (f32[8,256]{1,0:T(8,128)S(1)}, f32[8,256]{1,0:T(8,128)S(1)}, u32[]{:S(2)}, u32[]{:S(2)}) collective-permute-start(f32[8,256]{1,0:T(8,128)S(1)} %get-tuple-element.73), channel_id=1, source_target_pairs={{0,64},{64,0},{1,65},{65,1},{2,66},{66,2},{3,67},{67,3},{4,68},{68... | collective-permute-start | bytes 24584 | tf_op jit(solution)/shard_map/ppermute | solution.py:662
  100.6 5.7 %collective-permute-start.10 = (f32[128,256]{1,0:T(8,128)S(1)}, f32[128,256]{1,0:T(8,128)S(1)}, u32[]{:S(2)}, u32[]{:S(2)}) collective-permute-start(f32[128,256]{1,0:T(8,128)S(1)} %get-tuple-element.82.refs_1_), channel_id=1, source_target_pairs={{0,1},{2,3},{4,5},{6,7},{8,9},{10,11},{12,13},{14,15},{16,17},{18,... | collective-permute-start | bytes 393224 | tf_op jit(solution)/shard_map/ppermute | solution.py:658
  101.2 5.1 %collective-permute-start.11 = (f32[128,256]{1,0:T(8,128)S(1)}, f32[128,256]{1,0:T(8,128)S(1)}, u32[]{:S(2)}, u32[]{:S(2)}) collective-permute-start(f32[128,256]{1,0:T(8,128)S(1)} %get-tuple-element.81.refs_1_.refs_2_), channel_id=1, source_target_pairs={{1,2},{3,4},{5,6},{7,8},{9,10},{11,12},{13,14},{15,16},{17,18},{19... | collective-permute-start | bytes 393224 | tf_op jit(solution)/shard_map/ppermute | solution.py:658
  101.9 1.9 %collective-permute-start.9 = (f32[8,256]{1,0:T(8,128)S(1)}, f32[8,256]{1,0:T(8,128)S(1)}, u32[]{:S(2)}, u32[]{:S(2)}) collective-permute-start(f32[8,256]{1,0:T(8,128)S(1)} %get-tuple-element.83), channel_id=1, source_target_pairs={{0,64},{64,0},{1,65},{65,1},{2,66},{66,2},{3,67},{67,3},{4,68},{68... | collective-permute-start | bytes 24584 | tf_op jit(solution)/shard_map/ppermute | solution.py:662

commit v8 on v7

--- a/solution.py
+++ b/solution.py
@@ -21,8 +21,10 @@
 GRAM_ROWS = 64
 HALF = KEEP // 2
 PACK = 6
-PACK_LANES = 40
-FREE_LANE = 117
+PACK_LANES = 38
+FREE_LANE = 113
+SHARE = PACK // 2
+FREE = KEEP // SHARE
 OWN_LANE = 64
 CHUNK = 32
 BLOCK = 64
@@ -142,7 +144,7 @@
     )(pltpu.with_memory_space_constraint(basis, pltpu.HBM))
 
 
-def gram_kernel(v_ref, early_ref, out_ref, sums_ref, matrix_ref):
+def gram_kernel(v_ref, early_ref, keep_ref, give_ref, sums_ref, matrix_ref):
     for ga, gb in LATE_PAIRS:
         gram_block(v_ref, sums_ref, ga, gb)
     early = sorted(g * GROUP + a for g in ARRIVAL[:EARLY] for a in range(GROUP))
@@ -170,16 +172,18 @@
     packed = matrix_ref[pl.ds(0, PACK), :]
     for p in range(1, HALF // PACK):
         packed = packed + pltpu.roll(matrix_ref[pl.ds(p * PACK, PACK), :], p * PACK_LANES, 1)
-    for r in range(PACK):
-        out_ref[:, pl.ds(r * 128, 128)] = packed[r : r + 1]
+    upper = lax.axis_index("gy") == 1
+    low, high = packed[:SHARE], packed[SHARE:]
+    keep_ref[...] = jnp.where(upper, high, low)
+    give_ref[...] = jnp.where(upper, low, high)
 
 
 def gram_call(v, early):
     return pl.pallas_call(
         gram_kernel,
         in_specs=[VMEM_SPEC, VMEM_SPEC],
-        out_specs=VMEM_SPEC,
-        out_shape=jax.ShapeDtypeStruct((1, PACK * 128), F32),
+        out_specs=(VMEM_SPEC, VMEM_SPEC),
+        out_shape=(jax.ShapeDtypeStruct((SHARE, 128), F32),) * 2,
         scratch_shapes=[pltpu.VMEM((KEEP, KEEP, 128), F32), pltpu.VMEM((BASIS, 128), F32)],
         compiler_params=PARAMS,
         name="gram",
@@ -284,38 +288,51 @@
 
 
 def first_image_kernel(
-    v_ref, first_ref, second_ref, swap_ref, reaction_ref, extra_ref, w_ref, out_ref, dots_ref, pad_ref
+    v_ref, first_ref, second_ref, swap_ref, reaction_ref, w_ref, out_ref, dots_ref, pad_ref
 ):
     outer = outer_image(first_ref, second_ref)
     for x in range(XS):
         image = inner_image(v_ref.at[KEEP - 1], swap_ref, reaction_ref, pad_ref, x)
         w_ref[pl.ds(x * YS, YS), :] = image + outer[x] if x in outer else image
-    (row,) = dot_all(v_ref, [], [w_ref], [dots_ref])
-    lane = iota((1, 128), 1)
-    free = (lane >= FREE_LANE) & (lane < FREE_LANE + PACK)
-    rows = []
-    for r in range(PACK):
-        part = jnp.where(free, pltpu.roll(row, FREE_LANE - r * PACK, 1), 0.0)
-        rows.append(extra_ref[:, pl.ds(128 * r, 128)] + part)
-    write_for_all(out_ref, rows)
-
-
-def first_image_call(v, halo, reaction, extra, devices):
+    (out_ref[...],) = dot_all(v_ref, [], [w_ref], [dots_ref])
+
+
+def first_image_call(v, halo, reaction):
     return pl.pallas_call(
         first_image_kernel,
-        in_specs=[VMEM_SPEC] * 6,
+        in_specs=[VMEM_SPEC] * 5,
         out_specs=(VMEM_SPEC, VMEM_SPEC),
-        out_shape=(
-            pltpu.VMEM((ROWS, ZS), F32),
-            jax.ShapeDtypeStruct((devices * PACK, 128), F32),
-        ),
+        out_shape=(pltpu.VMEM((ROWS, ZS), F32), jax.ShapeDtypeStruct((1, 128), F32)),
         scratch_shapes=[
             pltpu.VMEM((BASIS, 128), F32),
             pltpu.VMEM((XS, YS + 16, ZS), F32),
         ],
         compiler_params=PARAMS,
         name="image_0",
-    )(v, *halo, reaction, extra)
+    )(v, *halo, reaction)
+
+
+def first_payload_kernel(row_ref, keep_ref, got_ref, out_ref):
+    gram = keep_ref[...] + got_ref[...]
+    row = row_ref[...]
+    lane = iota((1, 128), 1)
+    free = (lane >= FREE_LANE) & (lane < FREE_LANE + FREE)
+    rows = []
+    for r in range(SHARE):
+        part = jnp.where(free, pltpu.roll(row, FREE_LANE - r * FREE, 1), 0.0)
+        rows.append(gram[r : r + 1] + part)
+    write_for_all(out_ref, rows)
+
+
+def first_payload_call(row, keep, got, devices):
+    return pl.pallas_call(
+        first_payload_kernel,
+        in_specs=[VMEM_SPEC] * 3,
+        out_specs=VMEM_SPEC,
+        out_shape=jax.ShapeDtypeStruct((devices * SHARE, 128), F32),
+        compiler_params=PARAMS,
+        name="payload_0",
+    )(row, keep, got)
 
 
 def inner_kernel(count, *refs):
@@ -441,16 +458,21 @@
         return jnp.sum(values, axis=1, keepdims=True)
 
     if count == 0:
-        total = summed_rows(recv_ref, PACK) * scale
-        unpacked_gram(total[:PACK], pack_ref)
+        half = recv_ref.shape[0] // 2
+        low = summed_rows(recv_ref.at[pl.ds(0, half)], SHARE) * scale
+        high = summed_rows(recv_ref.at[pl.ds(half, half)], SHARE) * scale
+        pack_ref[pl.ds(0, SHARE), :] = low
+        pack_ref[pl.ds(SHARE, SHARE), :] = high
+        total = low + high
+        unpacked_gram(pack_ref[pl.ds(0, PACK), :], pack_ref)
         gram = pack_ref[pl.ds(0, BASIS), :]
         hess = jnp.zeros((BASIS, 128), F32)
         inverse_row = jnp.where(lane < KEEP, 1.0, 0.0)
         inverse_column = jnp.where(sub < KEEP, 1.0, 0.0)
         first_row = jnp.zeros((1, 128), F32)
-        for r in range(PACK):
-            part = pltpu.roll(total[r : r + 1], 128 - FREE_LANE + r * PACK, 1)
-            mine = (lane >= r * PACK) & (lane < (r + 1) * PACK)
+        for r in range(SHARE):
+            part = pltpu.roll(total[r : r + 1], 128 - FREE_LANE + r * FREE, 1)
+            mine = (lane >= r * FREE) & (lane < (r + 1) * FREE)
             first_row = jnp.where(mine, part, first_row)
         inverse = jnp.ones((1, 1), F32)
         image_square = None
@@ -679,8 +701,10 @@
     first = paired(near, 0)
     swap = across(swap)
     reaction = reaction.reshape(ROWS, ZS)
-    extra = gram_call(v, early)
-    w, payload = first_image_call(v, (first, second, swap), reaction, extra, devices)
+    keep, give = gram_call(v, early)
+    got = across(give)
+    w, row = first_image_call(v, (first, second, swap), reaction)
+    payload = first_payload_call(row, keep, got, devices)
     created = []
     state = None
     for _ in range(1, STEPS):

time: 130 us -> 129 us (level)
  blocking collectives: 82.3 us -> 80.8 us
    all_to_all x4, blocking collectives: 82.3 us -> 80.8 us  [from_all(): got = lax.all_to_all(copies, axes, split_axis=0, concat_axis=0, tiled=True)]
    ppermute x4 -> x5, starting transfers between devices: 4.36 us -> 4.21 us  [across(): return lax.ppermute(edge, 'gy', [(0, 1), (1, 0)])]
    pallas_call x2 -> x3, Pallas kernels: 12.2 us -> 12.2 us  [the longest x1 10.8 us: gram_call(): pl.pallas_call(gram_kernel, in_specs=[VMEM_SPEC, VMEM_SPEC], out_specs=(V...]
  transfers between devices with their start and end apart: 12 -> 13, of which waited for: 3 -> 3; matrix products, arithmetic and copies ran while one was open for 0% -> 0% of each run, Pallas kernels for 14% -> 15%
where the time goes in v8:
time: 129 us; the launch traced here: 128 us
  blocking collectives  80.8 us (63%)
  Pallas kernels  33.6 us (26%)
  starting transfers between devices  10.1 us (8%)
  waiting for transfers between devices  2.51 us (2%)
  between operations  1.41 us (1%)
    all_to_all x4, blocking collectives, from_all(): got = lax.all_to_all(copies, axes, split_axis=0, concat_axis=0, tiled=True)  80.8 us
    pallas_call x1, Pallas kernels, gram_call(): pl.pallas_call(gram_kernel, in_specs=[VMEM_SPEC, VMEM_SPEC], out_specs=(V...  10.8 us
    pallas_call x3, Pallas kernels, inner_call(): pl.pallas_call(functools.partial(inner_kernel, count), in_specs=[VMEM_SPE...  7.53 us
    ppermute x8, starting transfers between devices, paired(): lax.ppermute(half, 'gx', [(i, i + 1) for i in lower] + [(i + 1, i) for i...  5.87 us
    ppermute x5, starting transfers between devices, across(): return lax.ppermute(edge, 'gy', [(0, 1), (1, 0)])  4.21 us
    pallas_call x1, Pallas kernels, start_call(): pl.pallas_call(start_kernel, in_specs=[pl.BlockSpec(memory_space=pltpu.HB...  4.17 us
    pallas_call x3, Pallas kernels, outer_call(): pl.pallas_call(functools.partial(outer_kernel, count), in_specs=[VMEM_SPE...  2.79 us
  transfers between devices with their start and end apart: 13, of which 3 were waited for; matrix products, arithmetic and copies ran while one was open for 0% of the time, Pallas kernels for 15%

profile of v8, /device:TPU:1, one launch (start us, length us, event | category | flops | bytes accessed | tf_op | source)
XLA Modules:
  0.0 128.4 jit_solution(2583994508142292759)
XLA Ops:
  0.6 4.2 %start.1 = (f32[36,256,256]{2,1,0:T(8,128)S(1)}, f32[128,256]{1,0:T(8,128)S(1)}, f32[128,256]{1,0:T(8,128)S(1)}, f32[8,256]{1,0:T(8,128)S(1)}, f32[36,36,128]{2,1,0:T(8,128)S(1)}) custom-call(f32[36,256,256]{2,1,0:T(8,128)} %bitcast.35), custom_call_target="tpu_custom_call" | custom-call | tf_op jit(solution)/shard_map/start/pallas_call | solution.py:132
  4.8 2.1 %collective-permute-start = (f32[128,256]{1,0:T(8,128)S(1)}, f32[128,256]{1,0:T(8,128)S(1)}, u32[]{:S(2)}, u32[]{:S(2)}) collective-permute-start(f32[128,256]{1,0:T(8,128)S(1)} %get-tuple-element.56), channel_id=1, source_target_pairs={{0,1},{2,3},{4,5},{6,7},{8,9},{10,11},{12,13},{14,15},{16,17},{18,... | collective-permute-start | bytes 393224 | tf_op jit(solution)/shard_map/ppermute | solution.py:680
  7.6 1.0 collective-permute-start.2
  8.6 10.8 %gram.1 = (f32[3,128]{1,0:T(4,128)S(1)}, f32[3,128]{1,0:T(4,128)S(1)}) custom-call(f32[36,256,256]{2,1,0:T(8,128)S(1)} %get-tuple-element.55.v_ref.refs_2_.refs_3_.refs_0_, f32[36,36,128]{2,1,0:T(8,128)S(1)} %get-tuple-element.60.early_ref), custom_call_target="tpu_custom_call" | custom-call | tf_op jit(solution)/shard_map/gram/pallas_call | solution.py:182
  19.5 1.3 %image_0.1 = (f32[256,256]{1,0:T(8,128)S(1)}, f32[1,128]{1,0:T(1,128)S(1)}) custom-call(f32[36,256,256]{2,1,0:T(8,128)S(1)} %get-tuple-element.55.v_ref.refs_2_.refs_3_.refs_0_, f32[128,256]{1,0:T(8,128)S(1)} %collective-permute-done.first_ref, f32[128,256]{1,0:T(8,128)S(1)} %collective-permute-done.1.second_ref, ...), custom_call_target="tpu_custom_call" | custom-call | tf_op jit(solution)/shard_map/image_0/pallas_call | solution.py:301
  20.9 22.8 %all_to_all.25 = f32[128,1,384]{2,1,0:T(1,128)S(1)} all-to-all(f32[128,1,384]{2,1,0:T(1,128)S(1)} %bitcast.27), channel_id=1, replica_groups=mesh['gy'=2,'gx'=64] {'gy','gx'}, dimensions={0} | all-to-all | bytes 393216 | tf_op jit(solution)/shard_map/all_to_all | solution.py:691
  43.7 0.8 shard_map.41
  46.1 1.0 collective-permute-start.4
  47.1 0.8 collective-permute-done.4.refs_3_
  47.9 2.5 %shard_map.43 = (f32[256,256]{1,0:T(8,128)S(1)}, f32[256,256]{1,0:T(8,128)S(1)}, f32[1,128]{1,0:T(1,128)S(1)}) custom-call(f32[36,256,256]{2,1,0:T(8,128)S(1)} %get-tuple-element.55.v_ref.refs_2_.refs_3_.refs_0_, f32[128,256]{1,0:T(8,128)S(1)} %get-tuple-element.66.refs_1_, f32[128,256]{1,0:T(8,128)S(1)} %get-tuple-element.65.refs_1_.refs_2_, ...), custom_call_target="tpu_custom_call" | custom-call | tf_op jit(solution)/shard_map/pallas_call | solution.py:355
  50.4 0.9 shard_map.44
  51.3 19.4 %all_to_all.26 = f32[128,1,128]{2,1,0:T(1,128)S(1)} all-to-all(f32[128,1,128]{2,1,0:T(1,128)S(1)} %bitcast.32), channel_id=1, replica_groups=mesh['gy'=2,'gx'=64] {'gy','gx'}, dimensions={0} | all-to-all | bytes 131072 | tf_op jit(solution)/shard_map/all_to_all | solution.py:691
  73.0 1.1 collective-permute-start.7
  74.1 0.8 collective-permute-done.7.refs_4_
  74.9 2.5 %shard_map.47 = (f32[256,256]{1,0:T(8,128)S(1)}, f32[256,256]{1,0:T(8,128)S(1)}, f32[1,128]{1,0:T(1,128)S(1)}) custom-call(f32[36,256,256]{2,1,0:T(8,128)S(1)} %get-tuple-element.55.v_ref.refs_2_.refs_3_.refs_0_, f32[128,256]{1,0:T(8,128)S(1)} %get-tuple-element.76.refs_1_, f32[128,256]{1,0:T(8,128)S(1)} %get-tuple-element.75.refs_1_.refs_2_, ...), custom_call_target="tpu_custom_call" | custom-call | tf_op jit(solution)/shard_map/pallas_call | solution.py:355
  77.4 0.9 shard_map.48
  78.4 19.3 %all_to_all.27 = f32[128,1,128]{2,1,0:T(1,128)S(1)} all-to-all(f32[128,1,128]{2,1,0:T(1,128)S(1)} %bitcast.33), channel_id=1, replica_groups=mesh['gy'=2,'gx'=64] {'gy','gx'}, dimensions={0} | all-to-all | bytes 131072 | tf_op jit(solution)/shard_map/all_to_all | solution.py:691
  100.1 1.1 collective-permute-start.10
  101.2 0.8 collective-permute-done.10.refs_5_
  102.0 2.5 %shard_map.51 = (f32[256,256]{1,0:T(8,128)S(1)}, f32[256,256]{1,0:T(8,128)S(1)}, f32[1,128]{1,0:T(1,128)S(1)}) custom-call(f32[36,256,256]{2,1,0:T(8,128)S(1)} %get-tuple-element.55.v_ref.refs_2_.refs_3_.refs_0_, f32[128,256]{1,0:T(8,128)S(1)} %get-tuple-element.86.refs_1_, f32[128,256]{1,0:T(8,128)S(1)} %get-tuple-element.85.refs_1_.refs_2_, ...), custom_call_target="tpu_custom_call" | custom-call | tf_op jit(solution)/shard_map/pallas_call | solution.py:355
  104.6 0.9 shard_map.52
  105.5 19.3 %all_to_all.28 = f32[128,1,128]{2,1,0:T(1,128)S(1)} all-to-all(f32[128,1,128]{2,1,0:T(1,128)S(1)} %bitcast.34), channel_id=1, replica_groups=mesh['gy'=2,'gx'=64] {'gy','gx'}, dimensions={0} | all-to-all | bytes 131072 | tf_op jit(solution)/shard_map/all_to_all | solution.py:691
  124.8 1.8 %last.1 = (f32[256,256]{1,0:T(8,128)S(1)}, f32[88,128]{1,0:T(8,128)S(1)}, f32[1,128]{1,0:T(1,128)S(1)}, f32[1,128]{1,0:T(1,128)S(1)}, s32[1]{0:T(128)}) custom-call(f32[128,128]{1,0:T(8,128)S(1)} %bitcast.29, f32[256,256]{1,0:T(8,128)S(1)} %get-tuple-element.92.refs_1_, f32[36,256,256]{2,1,0:T(8,128)S(1)} %get-tuple-element.55.v_ref.refs_2_.refs_3_.refs_0_, ...), custom_call_target="tpu_custom_call" | custom-call | tf_op jit(solution)/shard_map/last/pallas_call | solution.py:628
  127.3 1.1 finish.1
  (27 shorter events, 7.1 us)
Async XLA Ops:
  0.6 18.8 %copy-start = (f32[4,64,256]{2,1,0:T(8,128)S(1)}, f32[4,64,256]{2,1,0:T(8,128)}, u32[]{:S(2)}) copy-start(f32[4,64,256]{2,1,0:T(8,128)} %param.5) | copy-start | bytes 786436
  4.8 14.6 %collective-permute-start = (f32[128,256]{1,0:T(8,128)S(1)}, f32[128,256]{1,0:T(8,128)S(1)}, u32[]{:S(2)}, u32[]{:S(2)}) collective-permute-start(f32[128,256]{1,0:T(8,128)S(1)} %get-tuple-element.56), channel_id=1, source_target_pairs={{0,1},{2,3},{4,5},{6,7},{8,9},{10,11},{12,13},{14,15},{16,17},{18,... | collective-permute-start | bytes 393224 | tf_op jit(solution)/shard_map/ppermute | solution.py:680
  6.9 12.5 %collective-permute-start.1 = (f32[128,256]{1,0:T(8,128)S(1)}, f32[128,256]{1,0:T(8,128)S(1)}, u32[]{:S(2)}, u32[]{:S(2)}) collective-permute-start(f32[128,256]{1,0:T(8,128)S(1)} %get-tuple-element.57), channel_id=1, source_target_pairs={{1,2},{3,4},{5,6},{7,8},{9,10},{11,12},{13,14},{15,16},{17,18},{19... | collective-permute-start | bytes 393224 | tf_op jit(solution)/shard_map/ppermute | solution.py:680
  7.6 11.8 %collective-permute-start.2 = (f32[8,256]{1,0:T(8,128)S(1)}, f32[8,256]{1,0:T(8,128)S(1)}, u32[]{:S(2)}, u32[]{:S(2)}) collective-permute-start(f32[8,256]{1,0:T(8,128)S(1)} %get-tuple-element.58), channel_id=1, source_target_pairs={{0,64},{64,0},{1,65},{65,1},{2,66},{66,2},{3,67},{67,3},{4,68},{68... | collective-permute-start | bytes 24584 | tf_op jit(solution)/shard_map/ppermute | solution.py:684
  19.4 1.4 %collective-permute-start.3 = (f32[3,128]{1,0:T(4,128)S(1)}, f32[3,128]{1,0:T(4,128)S(1)}, u32[]{:S(2)}, u32[]{:S(2)}) collective-permute-start(f32[3,128]{1,0:T(4,128)S(1)} %get-tuple-element.62), channel_id=1, source_target_pairs={{0,64},{64,0},{1,65},{65,1},{2,66},{66,2},{3,67},{67,3},{4,68},{68... | collective-permute-start | bytes 4616 | tf_op jit(solution)/shard_map/ppermute | solution.py:684
  45.1 5.3 %collective-permute-start.5 = (f32[128,256]{1,0:T(8,128)S(1)}, f32[128,256]{1,0:T(8,128)S(1)}, u32[]{:S(2)}, u32[]{:S(2)}) collective-permute-start(f32[128,256]{1,0:T(8,128)S(1)} %get-tuple-element.66.refs_1_), channel_id=1, source_target_pairs={{0,1},{2,3},{4,5},{6,7},{8,9},{10,11},{12,13},{14,15},{16,17},{18,... | collective-permute-start | bytes 393224 | tf_op jit(solution)/shard_map/ppermute | solution.py:680
  45.5 4.9 %collective-permute-start.6 = (f32[128,256]{1,0:T(8,128)S(1)}, f32[128,256]{1,0:T(8,128)S(1)}, u32[]{:S(2)}, u32[]{:S(2)}) collective-permute-start(f32[128,256]{1,0:T(8,128)S(1)} %get-tuple-element.65.refs_1_.refs_2_), channel_id=1, source_target_pairs={{1,2},{3,4},{5,6},{7,8},{9,10},{11,12},{13,14},{15,16},{17,18},{19... | collective-permute-start | bytes 393224 | tf_op jit(solution)/shard_map/ppermute | solution.py:680
  46.1 1.8 %collective-permute-start.4 = (f32[8,256]{1,0:T(8,128)S(1)}, f32[8,256]{1,0:T(8,128)S(1)}, u32[]{:S(2)}, u32[]{:S(2)}) collective-permute-start(f32[8,256]{1,0:T(8,128)S(1)} %get-tuple-element.67), channel_id=1, source_target_pairs={{0,64},{64,0},{1,65},{65,1},{2,66},{66,2},{3,67},{67,3},{4,68},{68... | collective-permute-start | bytes 24584 | tf_op jit(solution)/shard_map/ppermute | solution.py:684
  72.0 5.5 %collective-permute-start.8 = (f32[128,256]{1,0:T(8,128)S(1)}, f32[128,256]{1,0:T(8,128)S(1)}, u32[]{:S(2)}, u32[]{:S(2)}) collective-permute-start(f32[128,256]{1,0:T(8,128)S(1)} %get-tuple-element.76.refs_1_), channel_id=1, source_target_pairs={{0,1},{2,3},{4,5},{6,7},{8,9},{10,11},{12,13},{14,15},{16,17},{18,... | collective-permute-start | bytes 393224 | tf_op jit(solution)/shard_map/ppermute | solution.py:680
  72.3 5.1 %collective-permute-start.9 = (f32[128,256]{1,0:T(8,128)S(1)}, f32[128,256]{1,0:T(8,128)S(1)}, u32[]{:S(2)}, u32[]{:S(2)}) collective-permute-start(f32[128,256]{1,0:T(8,128)S(1)} %get-tuple-element.75.refs_1_.refs_2_), channel_id=1, source_target_pairs={{1,2},{3,4},{5,6},{7,8},{9,10},{11,12},{13,14},{15,16},{17,18},{19... | collective-permute-start | bytes 393224 | tf_op jit(solution)/shard_map/ppermute | solution.py:680
  73.0 1.9 %collective-permute-start.7 = (f32[8,256]{1,0:T(8,128)S(1)}, f32[8,256]{1,0:T(8,128)S(1)}, u32[]{:S(2)}, u32[]{:S(2)}) collective-permute-start(f32[8,256]{1,0:T(8,128)S(1)} %get-tuple-element.77), channel_id=1, source_target_pairs={{0,64},{64,0},{1,65},{65,1},{2,66},{66,2},{3,67},{67,3},{4,68},{68... | collective-permute-start | bytes 24584 | tf_op jit(solution)/shard_map/ppermute | solution.py:684
  99.1 5.5 %collective-permute-start.11 = (f32[128,256]{1,0:T(8,128)S(1)}, f32[128,256]{1,0:T(8,128)S(1)}, u32[]{:S(2)}, u32[]{:S(2)}) collective-permute-start(f32[128,256]{1,0:T(8,128)S(1)} %get-tuple-element.86.refs_1_), channel_id=1, source_target_pairs={{0,1},{2,3},{4,5},{6,7},{8,9},{10,11},{12,13},{14,15},{16,17},{18,... | collective-permute-start | bytes 393224 | tf_op jit(solution)/shard_map/ppermute | solution.py:680
  99.4 5.1 %collective-permute-start.12 = (f32[128,256]{1,0:T(8,128)S(1)}, f32[128,256]{1,0:T(8,128)S(1)}, u32[]{:S(2)}, u32[]{:S(2)}) collective-permute-start(f32[128,256]{1,0:T(8,128)S(1)} %get-tuple-element.85.refs_1_.refs_2_), channel_id=1, source_target_pairs={{1,2},{3,4},{5,6},{7,8},{9,10},{11,12},{13,14},{15,16},{17,18},{19... | collective-permute-start | bytes 393224 | tf_op jit(solution)/shard_map/ppermute | solution.py:680
  100.1 1.9 %collective-permute-start.10 = (f32[8,256]{1,0:T(8,128)S(1)}, f32[8,256]{1,0:T(8,128)S(1)}, u32[]{:S(2)}, u32[]{:S(2)}) collective-permute-start(f32[8,256]{1,0:T(8,128)S(1)} %get-tuple-element.87), channel_id=1, source_target_pairs={{0,64},{64,0},{1,65},{65,1},{2,66},{66,2},{3,67},{67,3},{4,68},{68... | collective-permute-start | bytes 24584 | tf_op jit(solution)/shard_map/ppermute | solution.py:684

commit v9 on v8

--- a/solution.py
+++ b/solution.py
@@ -335,39 +335,52 @@
     )(row, keep, got)
 
 
-def inner_kernel(count, *refs):
+def own_kernel(count, *refs):
     v_ref, near_ref, far_ref, *older = refs[: 2 + count]
-    swap_ref, reaction_ref, u_ref, w_ref, out_ref, dots_ref, more_ref, pad_ref = refs[2 + count :]
+    u_ref, out_ref, dots_ref = refs[2 + count :]
     odd = lax.axis_index("gx") % 2 == 1
     for x in range(2):
         rows = pl.ds(x * YS, YS)
         near, far = near_ref[rows, :], far_ref[rows, :]
         u_ref[pl.ds(x * YS, YS), :] = jnp.where(odd, near, far)
         u_ref[pl.ds((2 + x) * YS, YS), :] = jnp.where(odd, far, near)
+    (out_ref[...],) = dot_all(v_ref, [*older, u_ref], [u_ref], [dots_ref])
+
+
+def own_call(v, near, far, older):
+    count = 1 + len(older)
+    return pl.pallas_call(
+        functools.partial(own_kernel, count),
+        in_specs=[VMEM_SPEC] * (2 + count),
+        out_specs=(VMEM_SPEC,) * 2,
+        out_shape=(pltpu.VMEM((ROWS, ZS), F32), jax.ShapeDtypeStruct((1, 128), F32)),
+        scratch_shapes=[pltpu.VMEM((BASIS, 128), F32)],
+        compiler_params=PARAMS,
+    )(v, near, far, *older)
+
+
+def inner_kernel(count, *refs):
+    v_ref, *others = refs[: 1 + count]
+    swap_ref, reaction_ref, own_ref, w_ref, out_ref, dots_ref, pad_ref = refs[1 + count :]
     for x in range(XS):
-        w_ref[pl.ds(x * YS, YS), :] = inner_image(u_ref, swap_ref, reaction_ref, pad_ref, x)
-    row, own = dot_all(v_ref, [*older, u_ref], [w_ref, u_ref], [dots_ref, more_ref])
-    out_ref[...] = row + pltpu.roll(own, OWN_LANE, 1)
-
-
-def inner_call(v, near, far, older, swap, reaction):
-    count = 1 + len(older)
+        w_ref[pl.ds(x * YS, YS), :] = inner_image(others[-1], swap_ref, reaction_ref, pad_ref, x)
+    (row,) = dot_all(v_ref, others, [w_ref], [dots_ref])
+    out_ref[...] = row + pltpu.roll(own_ref[...], OWN_LANE, 1)
+
+
+def inner_call(v, created, swap, reaction, own):
+    count = len(created)
     return pl.pallas_call(
         functools.partial(inner_kernel, count),
         in_specs=[VMEM_SPEC] * (4 + count),
-        out_specs=(VMEM_SPEC,) * 3,
-        out_shape=(
-            pltpu.VMEM((ROWS, ZS), F32),
-            pltpu.VMEM((ROWS, ZS), F32),
-            jax.ShapeDtypeStruct((1, 128), F32),
-        ),
+        out_specs=(VMEM_SPEC,) * 2,
+        out_shape=(pltpu.VMEM((ROWS, ZS), F32), jax.ShapeDtypeStruct((1, 128), F32)),
         scratch_shapes=[
-            pltpu.VMEM((BASIS, 128), F32),
             pltpu.VMEM((BASIS, 128), F32),
             pltpu.VMEM((XS, YS + 16, ZS), F32),
         ],
         compiler_params=PARAMS,
-    )(v, near, far, *older, swap, reaction)
+    )(v, *created, swap, reaction, own)
 
 
 def outer_kernel(count, *refs):
@@ -714,8 +727,9 @@
         near, swap = near_call(weight, far, w, v, created)
         first = paired(near, 0)
         swap = across(swap)
-        u, inner, extra = inner_call(v, near, far, created, swap, reaction)
+        u, own = own_call(v, near, far, created)
         created.append(u)
+        inner, extra = inner_call(v, created, swap, reaction, own)
         w, payload = outer_call(v, created, first, second, inner, extra, devices)
     u, state, square, guess, sound = last_call(from_all(payload), w, v, created, state, cells)
     created.append(u)

time: 129 us -> 129 us (level)
  waiting for transfers between devices: 2.51 us -> 0.04 us
  blocking collectives: 80.8 us -> 83.2 us
    pallas_call x0 -> x3, Pallas kernels: none -> 3.38 us  [own_call(): pl.pallas_call(functools.partial(own_kernel, count), in_specs=[VMEM_SPEC]...]
    pallas_call x3, Pallas kernels: 7.53 us -> 4.25 us  [inner_call(): pl.pallas_call(functools.partial(inner_kernel, count), in_specs=[VMEM_SPE...]
    ppermute x5, waiting for transfers between devices: 2.49 us -> 0.01 us  [across(): return lax.ppermute(edge, 'gy', [(0, 1), (1, 0)])]
    all_to_all x4, blocking collectives: 80.8 us -> 83.2 us  [from_all(): got = lax.all_to_all(copies, axes, split_axis=0, concat_axis=0, tiled=True)]
  transfers between devices with their start and end apart: 13 -> 13, of which waited for: 3 -> 0; matrix products, arithmetic and copies ran while one was open for 0% -> 0% of each run, Pallas kernels for 15% -> 15%
where the time goes in v9:
time: 129 us; the launch traced here: 128 us
  blocking collectives  83.2 us (64%)
  Pallas kernels  33.7 us (26%)
  starting transfers between devices  10.1 us (8%)
  between operations  1.42 us (1%)
    all_to_all x4, blocking collectives, from_all(): got = lax.all_to_all(copies, axes, split_axis=0, concat_axis=0, tiled=True)  83.2 us
    pallas_call x1, Pallas kernels, gram_call(): pl.pallas_call(gram_kernel, in_specs=[VMEM_SPEC, VMEM_SPEC], out_specs=(V...  10.8 us
    ppermute x8, starting transfers between devices, paired(): lax.ppermute(half, 'gx', [(i, i + 1) for i in lower] + [(i + 1, i) for i...  5.87 us
    pallas_call x3, Pallas kernels, inner_call(): pl.pallas_call(functools.partial(inner_kernel, count), in_specs=[VMEM_SPE...  4.25 us
    ppermute x5, starting transfers between devices, across(): return lax.ppermute(edge, 'gy', [(0, 1), (1, 0)])  4.21 us
    pallas_call x1, Pallas kernels, start_call(): pl.pallas_call(start_kernel, in_specs=[pl.BlockSpec(memory_space=pltpu.HB...  4.17 us
    pallas_call x3, Pallas kernels, own_call(): pl.pallas_call(functools.partial(own_kernel, count), in_specs=[VMEM_SPEC]...  3.38 us
    pallas_call x3, Pallas kernels, outer_call(): pl.pallas_call(functools.partial(outer_kernel, count), in_specs=[VMEM_SPE...  2.79 us
  transfers between devices with their start and end apart: 13, of which 0 were waited for; matrix products, arithmetic and copies ran while one was open for 0% of the time, Pallas kernels for 15%

profile of v9, /device:TPU:1, one launch (start us, length us, event | category | flops | bytes accessed | tf_op | source)
XLA Modules:
  0.0 128.5 jit_solution(5425163032017726090)
XLA Ops:
  0.6 4.2 %start.1 = (f32[36,256,256]{2,1,0:T(8,128)S(1)}, f32[128,256]{1,0:T(8,128)S(1)}, f32[128,256]{1,0:T(8,128)S(1)}, f32[8,256]{1,0:T(8,128)S(1)}, f32[36,36,128]{2,1,0:T(8,128)S(1)}) custom-call(f32[36,256,256]{2,1,0:T(8,128)} %bitcast.35), custom_call_target="tpu_custom_call" | custom-call | tf_op jit(solution)/shard_map/start/pallas_call | solution.py:132
  4.8 2.1 %collective-permute-start = (f32[128,256]{1,0:T(8,128)S(1)}, f32[128,256]{1,0:T(8,128)S(1)}, u32[]{:S(2)}, u32[]{:S(2)}) collective-permute-start(f32[128,256]{1,0:T(8,128)S(1)} %get-tuple-element.59), channel_id=1, source_target_pairs={{0,1},{2,3},{4,5},{6,7},{8,9},{10,11},{12,13},{14,15},{16,17},{18,... | collective-permute-start | bytes 393224 | tf_op jit(solution)/shard_map/ppermute | solution.py:693
  7.6 1.0 collective-permute-start.2
  8.6 10.8 %gram.1 = (f32[3,128]{1,0:T(4,128)S(1)}, f32[3,128]{1,0:T(4,128)S(1)}) custom-call(f32[36,256,256]{2,1,0:T(8,128)S(1)} %get-tuple-element.58.v_ref.refs_2_.refs_3_.refs_0_, f32[36,36,128]{2,1,0:T(8,128)S(1)} %get-tuple-element.63.early_ref), custom_call_target="tpu_custom_call" | custom-call | tf_op jit(solution)/shard_map/gram/pallas_call | solution.py:182
  19.5 1.3 %image_0.1 = (f32[256,256]{1,0:T(8,128)S(1)}, f32[1,128]{1,0:T(1,128)S(1)}) custom-call(f32[36,256,256]{2,1,0:T(8,128)S(1)} %get-tuple-element.58.v_ref.refs_2_.refs_3_.refs_0_, f32[128,256]{1,0:T(8,128)S(1)} %collective-permute-done.first_ref, f32[128,256]{1,0:T(8,128)S(1)} %collective-permute-done.1.second_ref, ...), custom_call_target="tpu_custom_call" | custom-call | tf_op jit(solution)/shard_map/image_0/pallas_call | solution.py:301
  20.9 22.8 %all_to_all.25 = f32[128,1,384]{2,1,0:T(1,128)S(1)} all-to-all(f32[128,1,384]{2,1,0:T(1,128)S(1)} %bitcast.27), channel_id=1, replica_groups=mesh['gy'=2,'gx'=64] {'gy','gx'}, dimensions={0} | all-to-all | bytes 393216 | tf_op jit(solution)/shard_map/all_to_all | solution.py:704
  43.7 0.8 shard_map.41
  46.1 1.0 collective-permute-start.6
  47.1 1.1 shard_map.43
  48.2 1.4 %shard_map.44 = (f32[256,256]{1,0:T(8,128)S(1)}, f32[1,128]{1,0:T(1,128)S(1)}) custom-call(f32[36,256,256]{2,1,0:T(8,128)S(1)} %get-tuple-element.58.v_ref.refs_2_.refs_3_.refs_0_, f32[256,256]{1,0:T(8,128)S(1)} %get-tuple-element.70.refs_1_.refs_3_.refs_4_.refs_2_, f32[8,256]{1,0:T(8,128)S(1)} %collective-permute-done.6.refs_2_, f32[256,256]{1,0:T(8,128)S(1)} %bitcast.24, ...), custom_call_target="tpu_custom_call" | custom-call | tf_op jit(solution)/shard_map/pallas_call | solution.py:373
  49.6 0.9 shard_map.45
  50.6 20.1 %all_to_all.26 = f32[128,1,128]{2,1,0:T(1,128)S(1)} all-to-all(f32[128,1,128]{2,1,0:T(1,128)S(1)} %bitcast.32), channel_id=1, replica_groups=mesh['gy'=2,'gx'=64] {'gy','gx'}, dimensions={0} | all-to-all | bytes 131072 | tf_op jit(solution)/shard_map/all_to_all | solution.py:704
  73.0 1.1 collective-permute-start.9
  74.1 1.1 shard_map.48
  75.2 1.4 %shard_map.49 = (f32[256,256]{1,0:T(8,128)S(1)}, f32[1,128]{1,0:T(1,128)S(1)}) custom-call(f32[36,256,256]{2,1,0:T(8,128)S(1)} %get-tuple-element.58.v_ref.refs_2_.refs_3_.refs_0_, f32[256,256]{1,0:T(8,128)S(1)} %get-tuple-element.70.refs_1_.refs_3_.refs_4_.refs_2_, f32[256,256]{1,0:T(8,128)S(1)} %get-tuple-element.81.refs_2_.refs_4_.refs_5_.refs_3_, ...), custom_call_target="tpu_custom_call" | custom-call | tf_op jit(solution)/shard_map/pallas_call | solution.py:373
  76.7 0.9 shard_map.50
  77.6 20.1 %all_to_all.27 = f32[128,1,128]{2,1,0:T(1,128)S(1)} all-to-all(f32[128,1,128]{2,1,0:T(1,128)S(1)} %bitcast.33), channel_id=1, replica_groups=mesh['gy'=2,'gx'=64] {'gy','gx'}, dimensions={0} | all-to-all | bytes 131072 | tf_op jit(solution)/shard_map/all_to_all | solution.py:704
  100.1 1.1 collective-permute-start.12
  101.2 1.1 shard_map.53
  102.4 1.4 %shard_map.54 = (f32[256,256]{1,0:T(8,128)S(1)}, f32[1,128]{1,0:T(1,128)S(1)}) custom-call(f32[36,256,256]{2,1,0:T(8,128)S(1)} %get-tuple-element.58.v_ref.refs_2_.refs_3_.refs_0_, f32[256,256]{1,0:T(8,128)S(1)} %get-tuple-element.70.refs_1_.refs_3_.refs_4_.refs_2_, f32[256,256]{1,0:T(8,128)S(1)} %get-tuple-element.81.refs_2_.refs_4_.refs_5_.refs_3_, ...), custom_call_target="tpu_custom_call" | custom-call | tf_op jit(solution)/shard_map/pallas_call | solution.py:373
  103.8 1.0 shard_map.55
  104.8 20.1 %all_to_all.28 = f32[128,1,128]{2,1,0:T(1,128)S(1)} all-to-all(f32[128,1,128]{2,1,0:T(1,128)S(1)} %bitcast.34), channel_id=1, replica_groups=mesh['gy'=2,'gx'=64] {'gy','gx'}, dimensions={0} | all-to-all | bytes 131072 | tf_op jit(solution)/shard_map/all_to_all | solution.py:704
  124.9 1.8 %last.1 = (f32[256,256]{1,0:T(8,128)S(1)}, f32[88,128]{1,0:T(8,128)S(1)}, f32[1,128]{1,0:T(1,128)S(1)}, f32[1,128]{1,0:T(1,128)S(1)}, s32[1]{0:T(128)}) custom-call(f32[128,128]{1,0:T(8,128)S(1)} %bitcast.29, f32[256,256]{1,0:T(8,128)S(1)} %get-tuple-element.98.refs_1_, f32[36,256,256]{2,1,0:T(8,128)S(1)} %get-tuple-element.58.v_ref.refs_2_.refs_3_.refs_0_, ...), custom_call_target="tpu_custom_call" | custom-call | tf_op jit(solution)/shard_map/last/pallas_call | solution.py:641
  127.3 1.1 finish.1
  (30 shorter events, 7.1 us)
Async XLA Ops:
  0.6 18.8 %copy-start = (f32[4,64,256]{2,1,0:T(8,128)S(1)}, f32[4,64,256]{2,1,0:T(8,128)}, u32[]{:S(2)}) copy-start(f32[4,64,256]{2,1,0:T(8,128)} %param.5) | copy-start | bytes 786436
  4.8 14.6 %collective-permute-start = (f32[128,256]{1,0:T(8,128)S(1)}, f32[128,256]{1,0:T(8,128)S(1)}, u32[]{:S(2)}, u32[]{:S(2)}) collective-permute-start(f32[128,256]{1,0:T(8,128)S(1)} %get-tuple-element.59), channel_id=1, source_target_pairs={{0,1},{2,3},{4,5},{6,7},{8,9},{10,11},{12,13},{14,15},{16,17},{18,... | collective-permute-start | bytes 393224 | tf_op jit(solution)/shard_map/ppermute | solution.py:693
  6.9 12.5 %collective-permute-start.1 = (f32[128,256]{1,0:T(8,128)S(1)}, f32[128,256]{1,0:T(8,128)S(1)}, u32[]{:S(2)}, u32[]{:S(2)}) collective-permute-start(f32[128,256]{1,0:T(8,128)S(1)} %get-tuple-element.60), channel_id=1, source_target_pairs={{1,2},{3,4},{5,6},{7,8},{9,10},{11,12},{13,14},{15,16},{17,18},{19... | collective-permute-start | bytes 393224 | tf_op jit(solution)/shard_map/ppermute | solution.py:693
  7.6 11.8 %collective-permute-start.2 = (f32[8,256]{1,0:T(8,128)S(1)}, f32[8,256]{1,0:T(8,128)S(1)}, u32[]{:S(2)}, u32[]{:S(2)}) collective-permute-start(f32[8,256]{1,0:T(8,128)S(1)} %get-tuple-element.61), channel_id=1, source_target_pairs={{0,64},{64,0},{1,65},{65,1},{2,66},{66,2},{3,67},{67,3},{4,68},{68... | collective-permute-start | bytes 24584 | tf_op jit(solution)/shard_map/ppermute | solution.py:697
  19.4 1.4 %collective-permute-start.3 = (f32[3,128]{1,0:T(4,128)S(1)}, f32[3,128]{1,0:T(4,128)S(1)}, u32[]{:S(2)}, u32[]{:S(2)}) collective-permute-start(f32[3,128]{1,0:T(4,128)S(1)} %get-tuple-element.65), channel_id=1, source_target_pairs={{0,64},{64,0},{1,65},{65,1},{2,66},{66,2},{3,67},{67,3},{4,68},{68... | collective-permute-start | bytes 4616 | tf_op jit(solution)/shard_map/ppermute | solution.py:697
  45.1 4.5 %collective-permute-start.4 = (f32[128,256]{1,0:T(8,128)S(1)}, f32[128,256]{1,0:T(8,128)S(1)}, u32[]{:S(2)}, u32[]{:S(2)}) collective-permute-start(f32[128,256]{1,0:T(8,128)S(1)} %get-tuple-element.69.refs_1_), channel_id=1, source_target_pairs={{0,1},{2,3},{4,5},{6,7},{8,9},{10,11},{12,13},{14,15},{16,17},{18,... | collective-permute-start | bytes 393224 | tf_op jit(solution)/shard_map/ppermute | solution.py:693
  45.5 4.2 %collective-permute-start.5 = (f32[128,256]{1,0:T(8,128)S(1)}, f32[128,256]{1,0:T(8,128)S(1)}, u32[]{:S(2)}, u32[]{:S(2)}) collective-permute-start(f32[128,256]{1,0:T(8,128)S(1)} %get-tuple-element.68.refs_1_.refs_2_), channel_id=1, source_target_pairs={{1,2},{3,4},{5,6},{7,8},{9,10},{11,12},{13,14},{15,16},{17,18},{19... | collective-permute-start | bytes 393224 | tf_op jit(solution)/shard_map/ppermute | solution.py:693
  46.1 2.1 %collective-permute-start.6 = (f32[8,256]{1,0:T(8,128)S(1)}, f32[8,256]{1,0:T(8,128)S(1)}, u32[]{:S(2)}, u32[]{:S(2)}) collective-permute-start(f32[8,256]{1,0:T(8,128)S(1)} %get-tuple-element.71), channel_id=1, source_target_pairs={{0,64},{64,0},{1,65},{65,1},{2,66},{66,2},{3,67},{67,3},{4,68},{68... | collective-permute-start | bytes 24584 | tf_op jit(solution)/shard_map/ppermute | solution.py:697
  72.0 4.7 %collective-permute-start.7 = (f32[128,256]{1,0:T(8,128)S(1)}, f32[128,256]{1,0:T(8,128)S(1)}, u32[]{:S(2)}, u32[]{:S(2)}) collective-permute-start(f32[128,256]{1,0:T(8,128)S(1)} %get-tuple-element.80.refs_1_), channel_id=1, source_target_pairs={{0,1},{2,3},{4,5},{6,7},{8,9},{10,11},{12,13},{14,15},{16,17},{18,... | collective-permute-start | bytes 393224 | tf_op jit(solution)/shard_map/ppermute | solution.py:693
  72.4 4.3 %collective-permute-start.8 = (f32[128,256]{1,0:T(8,128)S(1)}, f32[128,256]{1,0:T(8,128)S(1)}, u32[]{:S(2)}, u32[]{:S(2)}) collective-permute-start(f32[128,256]{1,0:T(8,128)S(1)} %get-tuple-element.79.refs_1_.refs_2_), channel_id=1, source_target_pairs={{1,2},{3,4},{5,6},{7,8},{9,10},{11,12},{13,14},{15,16},{17,18},{19... | collective-permute-start | bytes 393224 | tf_op jit(solution)/shard_map/ppermute | solution.py:693
  73.0 2.2 %collective-permute-start.9 = (f32[8,256]{1,0:T(8,128)S(1)}, f32[8,256]{1,0:T(8,128)S(1)}, u32[]{:S(2)}, u32[]{:S(2)}) collective-permute-start(f32[8,256]{1,0:T(8,128)S(1)} %get-tuple-element.82), channel_id=1, source_target_pairs={{0,64},{64,0},{1,65},{65,1},{2,66},{66,2},{3,67},{67,3},{4,68},{68... | collective-permute-start | bytes 24584 | tf_op jit(solution)/shard_map/ppermute | solution.py:697
  99.1 4.7 %collective-permute-start.10 = (f32[128,256]{1,0:T(8,128)S(1)}, f32[128,256]{1,0:T(8,128)S(1)}, u32[]{:S(2)}, u32[]{:S(2)}) collective-permute-start(f32[128,256]{1,0:T(8,128)S(1)} %get-tuple-element.91.refs_1_), channel_id=1, source_target_pairs={{0,1},{2,3},{4,5},{6,7},{8,9},{10,11},{12,13},{14,15},{16,17},{18,... | collective-permute-start | bytes 393224 | tf_op jit(solution)/shard_map/ppermute | solution.py:693
  99.5 4.3 %collective-permute-start.11 = (f32[128,256]{1,0:T(8,128)S(1)}, f32[128,256]{1,0:T(8,128)S(1)}, u32[]{:S(2)}, u32[]{:S(2)}) collective-permute-start(f32[128,256]{1,0:T(8,128)S(1)} %get-tuple-element.90.refs_1_.refs_2_), channel_id=1, source_target_pairs={{1,2},{3,4},{5,6},{7,8},{9,10},{11,12},{13,14},{15,16},{17,18},{19... | collective-permute-start | bytes 393224 | tf_op jit(solution)/shard_map/ppermute | solution.py:693
  100.1 2.2 %collective-permute-start.12 = (f32[8,256]{1,0:T(8,128)S(1)}, f32[8,256]{1,0:T(8,128)S(1)}, u32[]{:S(2)}, u32[]{:S(2)}) collective-permute-start(f32[8,256]{1,0:T(8,128)S(1)} %get-tuple-element.93), channel_id=1, source_target_pairs={{0,64},{64,0},{1,65},{65,1},{2,66},{66,2},{3,67},{67,3},{4,68},{68... | collective-permute-start | bytes 24584 | tf_op jit(solution)/shard_map/ppermute | solution.py:697

commit v10 on v9

--- a/solution.py
+++ b/solution.py
@@ -32,6 +32,7 @@
 
 PARAMS = pltpu.CompilerParams(vmem_limit_bytes=16 * 2**20)
 SMEM_SPEC = pl.BlockSpec(memory_space=pltpu.SMEM)
+HBM_SPEC = pl.BlockSpec(memory_space=pltpu.HBM)
 VMEM_SPEC = pl.BlockSpec(memory_space=pltpu.VMEM)
 
 
@@ -617,7 +618,8 @@
 def last_kernel(cells, *refs):
     count = STEPS - 1
     recv_ref, w_ref, v_ref, *others = refs[: 3 + count]
-    state_in, u_ref, state_ref, square_ref, guess_ref, sound_ref, weight_ref = refs[3 + count :]
+    state_in, u_ref, state_ref, square_ref, guess_ref, sound_ref, new_ref = refs[3 + count : 10 + count]
+    weight_ref, scaled_ref, sems = refs[10 + count :]
     weights, first, gram, image_square = solve_weights(
         count, cells, recv_ref, state_in, state_ref, weight_ref, None
     )
@@ -626,6 +628,16 @@
     guess_ref[...] = jnp.where(iota((1, 128), 1) == 0, guess, 0.0)
     sound = jnp.where(guess > SOUND_SHARE * image_square, 1, 0)
     sound_ref[0] = sound[0, 0]
+    lane = iota((1, 128), 1)
+    inverse_row = state_ref[pl.ds(STATE_D, 1), :]
+    copies = []
+    for j, other in enumerate(others):
+        inverse = jnp.sum(jnp.where(lane == KEEP + j, inverse_row, 0.0), axis=1, keepdims=True)
+        for c in range(ROWS // CHUNK):
+            rows = pl.ds(c * CHUNK, CHUNK)
+            scaled_ref[j, rows, :] = other[rows, :] * inverse
+        copies.append(pltpu.make_async_copy(scaled_ref.at[j], new_ref.at[j], sems.at[j]))
+        copies[-1].start()
 
     def step(c, acc):
         rows = pl.ds(pl.multiple_of(c * BLOCK, BLOCK), BLOCK)
@@ -635,57 +647,62 @@
 
     acc = lax.fori_loop(0, ROWS // BLOCK, step, jnp.zeros((8, ZS), F32))
     square_ref[...] = fold_row(acc)
+    for copy in copies:
+        copy.wait()
 
 
 def last_call(recv, w, v, created, state, cells):
     return pl.pallas_call(
         functools.partial(last_kernel, cells),
         in_specs=[VMEM_SPEC] * (4 + len(created)),
-        out_specs=(VMEM_SPEC,) * 4 + (SMEM_SPEC,),
+        out_specs=(VMEM_SPEC,) * 4 + (SMEM_SPEC, HBM_SPEC),
         out_shape=(
             pltpu.VMEM((ROWS, ZS), F32),
             jax.ShapeDtypeStruct((STATE_ROWS, 128), F32),
             *LAST_SHAPES,
+            pltpu.HBM((STEPS, ROWS, ZS), F32),
         ),
-        scratch_shapes=[pltpu.VMEM(WEIGHT_SHAPE, F32)],
+        scratch_shapes=[
+            pltpu.VMEM(WEIGHT_SHAPE, F32),
+            pltpu.VMEM((STEPS - 1, ROWS, ZS), F32),
+            pltpu.SemaphoreType.DMA((STEPS - 1,)),
+        ],
         compiler_params=PARAMS,
         name="last",
     )(recv, w, v, *created, state)
 
 
-def finish_kernel(*refs):
-    square_ref, state_ref, *created = refs[: 2 + STEPS]
-    new_ref, hess_ref = refs[2 + STEPS :]
-    lane = iota((1, 128), 1)
+def finish_kernel(square_ref, state_ref, u_ref, new_in, new_ref, hess_ref, scaled_ref, sem):
     norm = jnp.sqrt(jnp.sum(square_ref[...], axis=1, keepdims=True) + EPSILON)
+    inverse = 1.0 / norm
+    for c in range(ROWS // CHUNK):
+        rows = pl.ds(c * CHUNK, CHUNK)
+        scaled_ref[rows, :] = u_ref[rows, :] * inverse
+    copy = pltpu.make_async_copy(scaled_ref, new_ref.at[STEPS - 1], sem)
+    copy.start()
     lanes = iota((BASIS, 128), 1)
     subs = iota((BASIS, 128), 0)
     hess = state_ref[pl.ds(STATE_H, BASIS), :]
     hess = jnp.where((subs == BASIS - 1) & (lanes == STEPS - 1), norm, hess)
-    hess_ref[...] = jnp.transpose(jnp.concatenate([hess, jnp.zeros((128 - BASIS, 128), F32)], axis=0))[:STEPS, :BASIS]
-    inverse_row = state_ref[pl.ds(STATE_D, 1), :]
-    for j, u_ref in enumerate(created):
-        if j == STEPS - 1:
-            inverse = 1.0 / norm
-        else:
-            inverse = jnp.sum(jnp.where(lane == KEEP + j, inverse_row, 0.0), axis=1, keepdims=True)
-        for c in range(ROWS // CHUNK):
-            rows = pl.ds(c * CHUNK, CHUNK)
-            new_ref[j, rows, :] = u_ref[rows, :] * inverse
-
-
-def finish_call(square, state, created):
+    hess = jnp.concatenate([hess, jnp.zeros((128 - BASIS, 128), F32)], axis=0)
+    hess_ref[...] = jnp.transpose(hess)[:STEPS, :BASIS]
+    copy.wait()
+
+
+def finish_call(square, state, u, new):
     return pl.pallas_call(
         finish_kernel,
-        in_specs=[VMEM_SPEC] * (2 + STEPS),
-        out_specs=(VMEM_SPEC, VMEM_SPEC),
+        in_specs=[VMEM_SPEC] * 3 + [HBM_SPEC],
+        out_specs=(HBM_SPEC, VMEM_SPEC),
         out_shape=(
-            jax.ShapeDtypeStruct((STEPS, ROWS, ZS), F32),
+            pltpu.HBM((STEPS, ROWS, ZS), F32),
             jax.ShapeDtypeStruct((STEPS, BASIS), F32),
         ),
+        scratch_shapes=[pltpu.VMEM((ROWS, ZS), F32), pltpu.SemaphoreType.DMA],
+        input_output_aliases={3: 0},
         compiler_params=PARAMS,
         name="finish",
-    )(square, state, *created)
+    )(square, state, u, new)
 
 
 def paired(half, start):
@@ -731,8 +748,8 @@
         created.append(u)
         inner, extra = inner_call(v, created, swap, reaction, own)
         w, payload = outer_call(v, created, first, second, inner, extra, devices)
-    u, state, square, guess, sound = last_call(from_all(payload), w, v, created, state, cells)
-    created.append(u)
+    recv = from_all(payload)
+    u, state, square, guess, sound, new = last_call(recv, w, v, created, state, cells)
     square = lax.cond(
         sound[0] == 1,
         lambda guess, square: guess,
@@ -740,7 +757,7 @@
         guess,
         jnp.broadcast_to(square, (devices, 128)),
     )
-    new, hessenberg = finish_call(square, state, created)
+    new, hessenberg = finish_call(square, state, u, new)
     return new.reshape(STEPS, XS, YS, ZS), hessenberg.T
 
 

time: 129 us -> 130 us (level)
  no operation moved by 1% of the time
where the time goes in v10:
time: 130 us; the launch traced here: 129 us
  blocking collectives  83.2 us (64%)
  Pallas kernels  34.4 us (26%)
  starting transfers between devices  10.1 us (8%)
  between operations  1.58 us (1%)
    all_to_all x4, blocking collectives, from_all(): got = lax.all_to_all(copies, axes, split_axis=0, concat_axis=0, tiled=True)  83.2 us
    pallas_call x1, Pallas kernels, gram_call(): pl.pallas_call(gram_kernel, in_specs=[VMEM_SPEC, VMEM_SPEC], out_specs=(V...  10.8 us
    ppermute x8, starting transfers between devices, paired(): lax.ppermute(half, 'gx', [(i, i + 1) for i in lower] + [(i + 1, i) for i...  5.87 us
    pallas_call x3, Pallas kernels, inner_call(): pl.pallas_call(functools.partial(inner_kernel, count), in_specs=[VMEM_SPE...  4.25 us
    ppermute x5, starting transfers between devices, across(): return lax.ppermute(edge, 'gy', [(0, 1), (1, 0)])  4.21 us
    pallas_call x1, Pallas kernels, start_call(): pl.pallas_call(start_kernel, in_specs=[pl.BlockSpec(memory_space=pltpu.HB...  4.17 us
    pallas_call x3, Pallas kernels, own_call(): pl.pallas_call(functools.partial(own_kernel, count), in_specs=[VMEM_SPEC]...  3.38 us
    pallas_call x3, Pallas kernels, outer_call(): pl.pallas_call(functools.partial(outer_kernel, count), in_specs=[VMEM_SPE...  2.79 us
  transfers between devices with their start and end apart: 13, of which 0 were waited for; matrix products, arithmetic and copies ran while one was open for 0% of the time, Pallas kernels for 15%

profile of v10, /device:TPU:1, one launch (start us, length us, event | category | flops | bytes accessed | tf_op | source)
XLA Modules:
  0.0 129.3 jit_solution(17828818659118709779)
XLA Ops:
  0.6 4.2 %start.1 = (f32[36,256,256]{2,1,0:T(8,128)S(1)}, f32[128,256]{1,0:T(8,128)S(1)}, f32[128,256]{1,0:T(8,128)S(1)}, f32[8,256]{1,0:T(8,128)S(1)}, f32[36,36,128]{2,1,0:T(8,128)S(1)}) custom-call(f32[36,256,256]{2,1,0:T(8,128)} %bitcast.35), custom_call_target="tpu_custom_call" | custom-call | tf_op jit(solution)/shard_map/start/pallas_call | solution.py:133
  4.8 2.1 %collective-permute-start = (f32[128,256]{1,0:T(8,128)S(1)}, f32[128,256]{1,0:T(8,128)S(1)}, u32[]{:S(2)}, u32[]{:S(2)}) collective-permute-start(f32[128,256]{1,0:T(8,128)S(1)} %get-tuple-element.60), channel_id=1, source_target_pairs={{0,1},{2,3},{4,5},{6,7},{8,9},{10,11},{12,13},{14,15},{16,17},{18,... | collective-permute-start | bytes 393224 | tf_op jit(solution)/shard_map/ppermute | solution.py:710
  7.6 1.0 collective-permute-start.2
  8.6 10.8 %gram.1 = (f32[3,128]{1,0:T(4,128)S(1)}, f32[3,128]{1,0:T(4,128)S(1)}) custom-call(f32[36,256,256]{2,1,0:T(8,128)S(1)} %get-tuple-element.59.v_ref.refs_2_.refs_3_.refs_0_, f32[36,36,128]{2,1,0:T(8,128)S(1)} %get-tuple-element.64.early_ref), custom_call_target="tpu_custom_call" | custom-call | tf_op jit(solution)/shard_map/gram/pallas_call | solution.py:183
  19.5 1.3 %image_0.1 = (f32[256,256]{1,0:T(8,128)S(1)}, f32[1,128]{1,0:T(1,128)S(1)}) custom-call(f32[36,256,256]{2,1,0:T(8,128)S(1)} %get-tuple-element.59.v_ref.refs_2_.refs_3_.refs_0_, f32[128,256]{1,0:T(8,128)S(1)} %collective-permute-done.first_ref, f32[128,256]{1,0:T(8,128)S(1)} %collective-permute-done.1.second_ref, ...), custom_call_target="tpu_custom_call" | custom-call | tf_op jit(solution)/shard_map/image_0/pallas_call | solution.py:302
  20.9 22.8 %all_to_all.25 = f32[128,1,384]{2,1,0:T(1,128)S(1)} all-to-all(f32[128,1,384]{2,1,0:T(1,128)S(1)} %bitcast.27), channel_id=1, replica_groups=mesh['gy'=2,'gx'=64] {'gy','gx'}, dimensions={0} | all-to-all | bytes 393216 | tf_op jit(solution)/shard_map/all_to_all | solution.py:721
  43.7 0.8 shard_map.41
  46.1 1.0 collective-permute-start.6
  47.1 1.1 shard_map.43
  48.2 1.4 %shard_map.44 = (f32[256,256]{1,0:T(8,128)S(1)}, f32[1,128]{1,0:T(1,128)S(1)}) custom-call(f32[36,256,256]{2,1,0:T(8,128)S(1)} %get-tuple-element.59.v_ref.refs_2_.refs_3_.refs_0_, f32[256,256]{1,0:T(8,128)S(1)} %get-tuple-element.71.refs_1_.refs_3_.refs_4_, f32[8,256]{1,0:T(8,128)S(1)} %collective-permute-done.6.refs_2_, f32[256,256]{1,0:T(8,128)S(1)} %bitcast.24, ...), custom_call_target="tpu_custom_call" | custom-call | tf_op jit(solution)/shard_map/pallas_call | solution.py:374
  49.6 0.9 shard_map.45
  50.6 20.1 %all_to_all.26 = f32[128,1,128]{2,1,0:T(1,128)S(1)} all-to-all(f32[128,1,128]{2,1,0:T(1,128)S(1)} %bitcast.32), channel_id=1, replica_groups=mesh['gy'=2,'gx'=64] {'gy','gx'}, dimensions={0} | all-to-all | bytes 131072 | tf_op jit(solution)/shard_map/all_to_all | solution.py:721
  73.0 1.1 collective-permute-start.9
  74.1 1.1 shard_map.48
  75.2 1.4 %shard_map.49 = (f32[256,256]{1,0:T(8,128)S(1)}, f32[1,128]{1,0:T(1,128)S(1)}) custom-call(f32[36,256,256]{2,1,0:T(8,128)S(1)} %get-tuple-element.59.v_ref.refs_2_.refs_3_.refs_0_, f32[256,256]{1,0:T(8,128)S(1)} %get-tuple-element.71.refs_1_.refs_3_.refs_4_, f32[256,256]{1,0:T(8,128)S(1)} %get-tuple-element.82.refs_2_.refs_4_.refs_5_, ...), custom_call_target="tpu_custom_call" | custom-call | tf_op jit(solution)/shard_map/pallas_call | solution.py:374
  76.7 0.9 shard_map.50
  77.6 20.1 %all_to_all.27 = f32[128,1,128]{2,1,0:T(1,128)S(1)} all-to-all(f32[128,1,128]{2,1,0:T(1,128)S(1)} %bitcast.33), channel_id=1, replica_groups=mesh['gy'=2,'gx'=64] {'gy','gx'}, dimensions={0} | all-to-all | bytes 131072 | tf_op jit(solution)/shard_map/all_to_all | solution.py:721
  100.1 1.1 collective-permute-start.12
  101.2 1.1 shard_map.53
  102.4 1.4 %shard_map.54 = (f32[256,256]{1,0:T(8,128)S(1)}, f32[1,128]{1,0:T(1,128)S(1)}) custom-call(f32[36,256,256]{2,1,0:T(8,128)S(1)} %get-tuple-element.59.v_ref.refs_2_.refs_3_.refs_0_, f32[256,256]{1,0:T(8,128)S(1)} %get-tuple-element.71.refs_1_.refs_3_.refs_4_, f32[256,256]{1,0:T(8,128)S(1)} %get-tuple-element.82.refs_2_.refs_4_.refs_5_, ...), custom_call_target="tpu_custom_call" | custom-call | tf_op jit(solution)/shard_map/pallas_call | solution.py:374
  103.8 0.9 shard_map.55
  104.8 20.1 %all_to_all.28 = f32[128,1,128]{2,1,0:T(1,128)S(1)} all-to-all(f32[128,1,128]{2,1,0:T(1,128)S(1)} %bitcast.34), channel_id=1, replica_groups=mesh['gy'=2,'gx'=64] {'gy','gx'}, dimensions={0} | all-to-all | bytes 131072 | tf_op jit(solution)/shard_map/all_to_all | solution.py:721
  124.9 2.2 %last.1 = (f32[256,256]{1,0:T(8,128)S(1)}, f32[88,128]{1,0:T(8,128)S(1)}, f32[1,128]{1,0:T(1,128)S(1)}, f32[1,128]{1,0:T(1,128)S(1)}, s32[1]{0:T(128)}, /*index=5*/f32[4,256,256]{2,1,0:T(8,128)}) custom-call(f32[128,128]{1,0:T(8,128)S(1)} %bitcast.29, f32[256,256]{1,0:T(8,128)S(1)} %get-tuple-element.99.refs_1_, ...), custom_call_target="tpu_custom_call" | custom-call | tf_op jit(solution)/shard_map/last/pallas_call | solution.py:655
  127.7 1.4 %finish.1 = (f32[4,256,256]{2,1,0:T(8,128)}, f32[4,40]{1,0:T(4,128)}) custom-call(f32[1,128]{1,0:T(1,128)S(1)} %get-tuple-element.109.square_ref, f32[88,128]{1,0:T(8,128)S(1)} %get-tuple-element.104.state_ref, f32[256,256]{1,0:T(8,128)S(1)} %get-tuple-element.105.u_ref, f32[4,256,256]{2,1,0:T(8,128)} %get-tuple-element.106.new_in), custom_call_target="tpu_custom_call", output_to_operand_aliasing={{0}: (3, {})} | custom-call | tf_op jit(solution)/shard_map/finish/pallas_call | solution.py:693
  (30 shorter events, 7.1 us)
Async XLA Ops:
  0.6 18.8 %copy-start = (f32[4,64,256]{2,1,0:T(8,128)S(1)}, f32[4,64,256]{2,1,0:T(8,128)}, u32[]{:S(2)}) copy-start(f32[4,64,256]{2,1,0:T(8,128)} %param.5) | copy-start | bytes 786436
  4.8 14.6 %collective-permute-start = (f32[128,256]{1,0:T(8,128)S(1)}, f32[128,256]{1,0:T(8,128)S(1)}, u32[]{:S(2)}, u32[]{:S(2)}) collective-permute-start(f32[128,256]{1,0:T(8,128)S(1)} %get-tuple-element.60), channel_id=1, source_target_pairs={{0,1},{2,3},{4,5},{6,7},{8,9},{10,11},{12,13},{14,15},{16,17},{18,... | collective-permute-start | bytes 393224 | tf_op jit(solution)/shard_map/ppermute | solution.py:710
  6.9 12.5 %collective-permute-start.1 = (f32[128,256]{1,0:T(8,128)S(1)}, f32[128,256]{1,0:T(8,128)S(1)}, u32[]{:S(2)}, u32[]{:S(2)}) collective-permute-start(f32[128,256]{1,0:T(8,128)S(1)} %get-tuple-element.61), channel_id=1, source_target_pairs={{1,2},{3,4},{5,6},{7,8},{9,10},{11,12},{13,14},{15,16},{17,18},{19... | collective-permute-start | bytes 393224 | tf_op jit(solution)/shard_map/ppermute | solution.py:710
  7.6 11.8 %collective-permute-start.2 = (f32[8,256]{1,0:T(8,128)S(1)}, f32[8,256]{1,0:T(8,128)S(1)}, u32[]{:S(2)}, u32[]{:S(2)}) collective-permute-start(f32[8,256]{1,0:T(8,128)S(1)} %get-tuple-element.62), channel_id=1, source_target_pairs={{0,64},{64,0},{1,65},{65,1},{2,66},{66,2},{3,67},{67,3},{4,68},{68... | collective-permute-start | bytes 24584 | tf_op jit(solution)/shard_map/ppermute | solution.py:714
  19.4 1.4 %collective-permute-start.3 = (f32[3,128]{1,0:T(4,128)S(1)}, f32[3,128]{1,0:T(4,128)S(1)}, u32[]{:S(2)}, u32[]{:S(2)}) collective-permute-start(f32[3,128]{1,0:T(4,128)S(1)} %get-tuple-element.66), channel_id=1, source_target_pairs={{0,64},{64,0},{1,65},{65,1},{2,66},{66,2},{3,67},{67,3},{4,68},{68... | collective-permute-start | bytes 4616 | tf_op jit(solution)/shard_map/ppermute | solution.py:714
  45.1 4.5 %collective-permute-start.4 = (f32[128,256]{1,0:T(8,128)S(1)}, f32[128,256]{1,0:T(8,128)S(1)}, u32[]{:S(2)}, u32[]{:S(2)}) collective-permute-start(f32[128,256]{1,0:T(8,128)S(1)} %get-tuple-element.70.refs_1_), channel_id=1, source_target_pairs={{0,1},{2,3},{4,5},{6,7},{8,9},{10,11},{12,13},{14,15},{16,17},{18,... | collective-permute-start | bytes 393224 | tf_op jit(solution)/shard_map/ppermute | solution.py:710
  45.5 4.2 %collective-permute-start.5 = (f32[128,256]{1,0:T(8,128)S(1)}, f32[128,256]{1,0:T(8,128)S(1)}, u32[]{:S(2)}, u32[]{:S(2)}) collective-permute-start(f32[128,256]{1,0:T(8,128)S(1)} %get-tuple-element.69.refs_1_.refs_2_), channel_id=1, source_target_pairs={{1,2},{3,4},{5,6},{7,8},{9,10},{11,12},{13,14},{15,16},{17,18},{19... | collective-permute-start | bytes 393224 | tf_op jit(solution)/shard_map/ppermute | solution.py:710
  46.1 2.1 %collective-permute-start.6 = (f32[8,256]{1,0:T(8,128)S(1)}, f32[8,256]{1,0:T(8,128)S(1)}, u32[]{:S(2)}, u32[]{:S(2)}) collective-permute-start(f32[8,256]{1,0:T(8,128)S(1)} %get-tuple-element.72), channel_id=1, source_target_pairs={{0,64},{64,0},{1,65},{65,1},{2,66},{66,2},{3,67},{67,3},{4,68},{68... | collective-permute-start | bytes 24584 | tf_op jit(solution)/shard_map/ppermute | solution.py:714
  72.0 4.7 %collective-permute-start.7 = (f32[128,256]{1,0:T(8,128)S(1)}, f32[128,256]{1,0:T(8,128)S(1)}, u32[]{:S(2)}, u32[]{:S(2)}) collective-permute-start(f32[128,256]{1,0:T(8,128)S(1)} %get-tuple-element.81.refs_1_), channel_id=1, source_target_pairs={{0,1},{2,3},{4,5},{6,7},{8,9},{10,11},{12,13},{14,15},{16,17},{18,... | collective-permute-start | bytes 393224 | tf_op jit(solution)/shard_map/ppermute | solution.py:710
  72.4 4.3 %collective-permute-start.8 = (f32[128,256]{1,0:T(8,128)S(1)}, f32[128,256]{1,0:T(8,128)S(1)}, u32[]{:S(2)}, u32[]{:S(2)}) collective-permute-start(f32[128,256]{1,0:T(8,128)S(1)} %get-tuple-element.80.refs_1_.refs_2_), channel_id=1, source_target_pairs={{1,2},{3,4},{5,6},{7,8},{9,10},{11,12},{13,14},{15,16},{17,18},{19... | collective-permute-start | bytes 393224 | tf_op jit(solution)/shard_map/ppermute | solution.py:710
  73.0 2.2 %collective-permute-start.9 = (f32[8,256]{1,0:T(8,128)S(1)}, f32[8,256]{1,0:T(8,128)S(1)}, u32[]{:S(2)}, u32[]{:S(2)}) collective-permute-start(f32[8,256]{1,0:T(8,128)S(1)} %get-tuple-element.83), channel_id=1, source_target_pairs={{0,64},{64,0},{1,65},{65,1},{2,66},{66,2},{3,67},{67,3},{4,68},{68... | collective-permute-start | bytes 24584 | tf_op jit(solution)/shard_map/ppermute | solution.py:714
  99.1 4.7 %collective-permute-start.10 = (f32[128,256]{1,0:T(8,128)S(1)}, f32[128,256]{1,0:T(8,128)S(1)}, u32[]{:S(2)}, u32[]{:S(2)}) collective-permute-start(f32[128,256]{1,0:T(8,128)S(1)} %get-tuple-element.92.refs_1_), channel_id=1, source_target_pairs={{0,1},{2,3},{4,5},{6,7},{8,9},{10,11},{12,13},{14,15},{16,17},{18,... | collective-permute-start | bytes 393224 | tf_op jit(solution)/shard_map/ppermute | solution.py:710
  99.5 4.3 %collective-permute-start.11 = (f32[128,256]{1,0:T(8,128)S(1)}, f32[128,256]{1,0:T(8,128)S(1)}, u32[]{:S(2)}, u32[]{:S(2)}) collective-permute-start(f32[128,256]{1,0:T(8,128)S(1)} %get-tuple-element.91.refs_1_.refs_2_), channel_id=1, source_target_pairs={{1,2},{3,4},{5,6},{7,8},{9,10},{11,12},{13,14},{15,16},{17,18},{19... | collective-permute-start | bytes 393224 | tf_op jit(solution)/shard_map/ppermute | solution.py:710
  100.1 2.2 %collective-permute-start.12 = (f32[8,256]{1,0:T(8,128)S(1)}, f32[8,256]{1,0:T(8,128)S(1)}, u32[]{:S(2)}, u32[]{:S(2)}) collective-permute-start(f32[8,256]{1,0:T(8,128)S(1)} %get-tuple-element.94), channel_id=1, source_target_pairs={{0,64},{64,0},{1,65},{65,1},{2,66},{66,2},{3,67},{67,3},{4,68},{68... | collective-permute-start | bytes 24584 | tf_op jit(solution)/shard_map/ppermute | solution.py:714
